TPU v7x, 128 devices: a whole 4x4x4 slice. The times are simulated.
128 devices in a mesh: seq: 32 (over y, z, core), dp: 4 (over x).
Axes of the slice: x: 4, y: 4, z: 4, core: 2. Of those that a mesh axis runs over, the one named last changes fastest.
Arguments:
- query_input: bfloat16 [4, 16384, 2048], P('dp', 'seq'), may hold values from -6 to 6
- key_input: bfloat16 [4, 16384, 2048], P('dp', 'seq'), may hold values from -6 to 6
- value_input: bfloat16 [4, 16384, 2048], P('dp', 'seq'), may hold values from -6 to 6
- grad_output: bfloat16 [4, 16384, 2048], P('dp', 'seq'), may hold values from -6 to 6
- out_weight: bfloat16 [2048, 2048], P(('seq', 'dp')), may hold values from -0.125 to 0.125
- norm_gain: float32 [2048], replicated, may hold values from 0.1 to 1.9
Outputs:
- result: bfloat16 [4, 16384, 2048], P('dp', 'seq')
- grad_query: bfloat16 [4, 16384, 2048], P('dp', 'seq')
- grad_key: bfloat16 [4, 16384, 2048], P('dp', 'seq')
- grad_value: bfloat16 [4, 16384, 2048], P('dp', 'seq')
- grad_weight: float32 [2048, 2048], P(('seq', 'dp'))
All inputs are finite; a program needn't handle non-finite values.
Results may differ from a plain program's by a relative error of at most 0.015.
Values may be sent and summed in bfloat16 or wider, within the bound.
No kernel may reach another device: no remote copies, remote signals or barrier semaphores. Data moves between devices by JAX's collectives and lax.ppermute only.
A program may use at most 192 MiB of HBM per device.

v0:
```python
import jax
import jax.numpy as jnp
from jax import lax
from jax.experimental import pallas as pl
from jax.experimental.pallas import tpu as pltpu
from jax.sharding import Mesh
from jax.sharding import PartitionSpec as P

HEADS = 16
HEAD_DIM = 128
BLOCK = 512
HALF = BLOCK // 2
PAIR = 2 * HEAD_DIM
FEATURES = HEADS * HEAD_DIM
ROWS = 128
SEQ = ("seq_0", "seq_1", "seq_2")
SEQ_DP = ("seq_0", "seq_1", "seq_2", "dp")
F32 = jnp.float32
BF16 = jnp.bfloat16


epsilon = 1e-06


def head(i):
    return slice(i * HEAD_DIM, (i + 1) * HEAD_DIM)


def dot_nn(left, right):
    return lax.dot_general(left, right, (((1,), (0,)), ((), ())), preferred_element_type=F32)


def dot_nt(left, right):
    return lax.dot_general(left, right, (((1,), (1,)), ((), ())), preferred_element_type=F32)


def dot_tn(left, right):
    return lax.dot_general(left, right, (((0,), (0,)), ((), ())), preferred_element_type=F32)


def silu_low(raw):
    wide = raw.astype(F32)
    return (wide * jax.nn.sigmoid(wide)).astype(BF16)


def silu_slope(raw):
    wide = raw.astype(F32)
    s = jax.nn.sigmoid(wide)
    return s * (1.0 + wide * (1.0 - s))


def causal(scores):
    row = lax.broadcasted_iota(jnp.int32, scores.shape, 0)
    col = lax.broadcasted_iota(jnp.int32, scores.shape, 1)
    return jnp.where(row >= col, scores, 0.0).astype(BF16)


def spec(shape, index):
    return pl.BlockSpec(shape, index)


def call(body, grid, in_specs, out_specs, out_shape, flops, moved, scratch=(), name=None):
    return pl.pallas_call(
        body,
        grid=grid,
        in_specs=in_specs,
        out_specs=out_specs,
        out_shape=out_shape,
        scratch_shapes=scratch,
        compiler_params=pltpu.CompilerParams(vmem_limit_bytes=48 * 1024 * 1024),
        cost_estimate=pl.CostEstimate(flops=flops, bytes_accessed=moved, transcendentals=0),
        name=name,
    )


PAIR_SPEC = spec((BLOCK, PAIR), lambda i: (0, i))
STATE_SPEC = spec((2, HEAD_DIM, HEAD_DIM), lambda i: (i, 0, 0))
WIDE_LOW = jax.ShapeDtypeStruct((BLOCK, FEATURES), BF16)
WIDE = jax.ShapeDtypeStruct((BLOCK, FEATURES), F32)
STATE_LOW = jax.ShapeDtypeStruct((HEADS, HEAD_DIM, HEAD_DIM), BF16)
MIB = 1 << 20


def states_body(key, value, feat_key, state):
    for i in range(2):
        low = silu_low(key[:, head(i)])
        feat_key[:, head(i)] = low
        state[i] = dot_tn(low, value[:, head(i)]).astype(BF16)


def block_states(key, value):
    return call(
        states_body,
        (HEADS // 2,),
        [PAIR_SPEC, PAIR_SPEC],
        [PAIR_SPEC, STATE_SPEC],
        [WIDE_LOW, STATE_LOW],
        1 << 29,
        7 * MIB,
        name="block_states",
    )(key, value)


def inside_body(query, feat_key, value, feat_query, inside):
    for i in range(2):
        low = silu_low(query[:, head(i)])
        feat_query[:, head(i)] = low
        keys = feat_key[:, head(i)]
        values = value[:, head(i)]
        first = causal(dot_nt(low[:HALF], keys[:HALF]))
        below = dot_nt(low[HALF:], keys[:HALF]).astype(BF16)
        second = causal(dot_nt(low[HALF:], keys[HALF:]))
        inside[:HALF, head(i)] = dot_nn(first, values[:HALF])
        inside[HALF:, head(i)] = dot_nn(below, values[:HALF]) + dot_nn(second, values[HALF:])


def inside_blocks(query, feat_key, value):
    return call(
        inside_body,
        (HEADS // 2,),
        [PAIR_SPEC] * 3,
        [PAIR_SPEC] * 2,
        [WIDE_LOW, WIDE],
        1 << 32,
        12 * MIB,
        name="inside_blocks",
    )(query, feat_key, value)


def scan_body(reverse, pieces, sums):
    peers = pieces.shape[0]
    total = jnp.zeros(pieces.shape[1:], F32)
    for k in reversed(range(peers)) if reverse else range(peers):
        sums[k] = total.astype(BF16)
        total = total + pieces[k].astype(F32)


def exclusive_sums(pieces, reverse):
    peers, rows, lanes = pieces.shape
    part = spec((peers, rows // 2, lanes), lambda i: (0, i, 0))
    return call(
        lambda a, b: scan_body(reverse, a, b),
        (2,),
        [part],
        part,
        jax.ShapeDtypeStruct(pieces.shape, BF16),
        1 << 23,
        MIB,
        name="exclusive_sums",
    )(pieces)


def scanned(block_state, reverse):
    peers = 1
    for axis in SEQ:
        peers *= lax.axis_size(axis)
    pieces = block_state.reshape(peers, -1, HEAD_DIM)
    pieces = lax.all_to_all(pieces, SEQ, 0, 0, tiled=True)
    sums = exclusive_sums(pieces, reverse)
    sums = lax.all_to_all(sums, SEQ, 0, 0, tiled=True)
    return sums.reshape(block_state.shape)


ROW_SPEC = spec((ROWS, FEATURES), lambda i: (i, 0))
EDGE_SPEC = spec((ROWS, HEAD_DIM), lambda i: (i, 0))
GAIN_SPEC = spec((1, FEATURES), lambda i: (0, 0))
ALL_STATES = spec((HEADS, HEAD_DIM, HEAD_DIM), lambda i: (0, 0, 0))
SPLIT_SPEC = spec((2, ROWS, FEATURES // 2), lambda i: (0, i, 0))


def attend_body(inside, feat_query, state, gain, mixed, split, normed, inverse):
    squares = jnp.zeros((ROWS, HEAD_DIM), F32)
    for i in range(HEADS):
        attention = inside[:, head(i)] + dot_nn(feat_query[:, head(i)], state[i])
        normed[:, head(i)] = attention
        squares = squares + attention * attention
    radius = jnp.sqrt(jnp.sum(squares, axis=1, keepdims=True) / FEATURES + epsilon)
    scale = 1.0 / radius
    inverse[...] = jnp.broadcast_to(scale, inverse.shape)
    part = HEAD_DIM // 2
    for i in range(0, HEADS, 2):
        lows = []
        for j in (i, i + 1):
            value = normed[:, head(j)] * scale
            normed[:, head(j)] = value
            low = (value * gain[:, head(j)]).astype(BF16)
            mixed[:, head(j)] = low
            lows.append(low)
        at = head(i // 2)
        split[0, :, at] = jnp.concatenate([lows[0][:, :part], lows[1][:, :part]], axis=1)
        split[1, :, at] = jnp.concatenate([lows[0][:, part:], lows[1][:, part:]], axis=1)


def attend(inside, feat_query, state, gain):
    return call(
        attend_body,
        (BLOCK // ROWS,),
        [ROW_SPEC, ROW_SPEC, ALL_STATES, GAIN_SPEC],
        [ROW_SPEC, SPLIT_SPEC, ROW_SPEC, EDGE_SPEC],
        [
            WIDE_LOW,
            jax.ShapeDtypeStruct((2, BLOCK, FEATURES // 2), BF16),
            WIDE,
            jax.ShapeDtypeStruct((BLOCK, HEAD_DIM), F32),
        ],
        1 << 29,
        15 * MIB,
        name="attend",
    )(inside, feat_query, state, gain)


def norm_back_body(grad_mixed, normed, inverse, gain, feat_query, grad_att, state, sums):
    step = pl.program_id(0)
    products = jnp.zeros((ROWS, HEAD_DIM), F32)
    for i in range(HEADS):
        hat = grad_mixed[:, head(i)] * gain[:, head(i)]
        products = products + hat * normed[:, head(i)]
    mean = jnp.sum(products, axis=1, keepdims=True) / FEATURES
    scale = inverse[:, :1]
    for i in range(HEADS):
        hat = grad_mixed[:, head(i)] * gain[:, head(i)]
        low = ((hat - normed[:, head(i)] * mean) * scale).astype(BF16)
        grad_att[:, head(i)] = low
        update = dot_tn(feat_query[:, head(i)], low)

        @pl.when(step == 0)
        def _():
            sums[i] = update

        @pl.when(step > 0)
        def _():
            sums[i] = sums[i] + update

    @pl.when(step == pl.num_programs(0) - 1)
    def _():
        state[...] = sums[...].astype(BF16)


def norm_back(grad_mixed, normed, inverse, gain, feat_query):
    return call(
        norm_back_body,
        (BLOCK // ROWS,),
        [ROW_SPEC, ROW_SPEC, EDGE_SPEC, GAIN_SPEC, ROW_SPEC],
        [ROW_SPEC, ALL_STATES],
        [WIDE_LOW, STATE_LOW],
        1 << 29,
        13 * MIB,
        scratch=[pltpu.VMEM((HEADS, HEAD_DIM, HEAD_DIM), F32)],
        name="norm_back",
    )(grad_mixed, normed, inverse, gain, feat_query)


def back_body(query, feat_query, feat_key, value, grad, state, grad_query, part_key, part_value):
    for i in range(2):
        at = head(i)
        q0, q1 = feat_query[:HALF, at], feat_query[HALF:, at]
        k0, k1 = feat_key[:HALF, at], feat_key[HALF:, at]
        v0, v1 = value[:HALF, at], value[HALF:, at]
        g0, g1 = grad[:HALF, at], grad[HALF:, at]
        s00 = causal(dot_nt(q0, k0))
        s10 = dot_nt(q1, k0).astype(BF16)
        s11 = causal(dot_nt(q1, k1))
        part_value[:HALF, at] = dot_tn(s00, g0) + dot_tn(s10, g1)
        part_value[HALF:, at] = dot_tn(s11, g1)
        d00 = causal(dot_nt(g0, v0))
        d10 = dot_nt(g1, v0).astype(BF16)
        d11 = causal(dot_nt(g1, v1))
        part_key[:HALF, at] = dot_tn(d00, q0) + dot_tn(d10, q1)
        part_key[HALF:, at] = dot_tn(d11, q1)
        fq0 = dot_nn(d00, k0) + dot_nt(g0, state[i])
        fq1 = dot_nn(d10, k0) + dot_nn(d11, k1) + dot_nt(g1, state[i])
        grad_query[:HALF, at] = (fq0 * silu_slope(query[:HALF, at])).astype(BF16)
        grad_query[HALF:, at] = (fq1 * silu_slope(query[HALF:, at])).astype(BF16)


def back_inside(query, feat_query, feat_key, value, grad, state):
    return call(
        back_body,
        (HEADS // 2,),
        [PAIR_SPEC] * 5 + [STATE_SPEC],
        [PAIR_SPEC] * 3,
        [WIDE_LOW, WIDE, WIDE],
        3 << 32,
        20 * MIB,
        name="back_inside",
    )(query, feat_query, feat_key, value, grad, state)


def finish_body(key, feat_key, value, part_key, part_value, later, grad_key, grad_value):
    for i in range(2):
        at = head(i)
        fk = part_key[:, at] + dot_nt(value[:, at], later[i])
        grad_key[:, at] = (fk * silu_slope(key[:, at])).astype(BF16)
        grad_value[:, at] = (part_value[:, at] + dot_nn(feat_key[:, at], later[i])).astype(BF16)


def finish(key, feat_key, value, part_key, part_value, later):
    return call(
        finish_body,
        (HEADS // 2,),
        [PAIR_SPEC] * 5 + [STATE_SPEC],
        [PAIR_SPEC] * 2,
        [WIDE_LOW, WIDE_LOW],
        1 << 30,
        18 * MIB,
        name="finish",
    )(key, feat_key, value, part_key, part_value, later)


def gradient_rows(split, grad_result):
    chips = lax.axis_size("seq_0") * lax.axis_size("seq_1")
    core = lax.axis_index("seq_2")
    mine = lax.dynamic_index_in_dim(split, core, 0, keepdims=False)
    other = lax.dynamic_index_in_dim(split, 1 - core, 0, keepdims=False)
    sent = dot_tn(other, grad_result).astype(BF16)
    got = lax.ppermute(sent, "seq_2", [(0, 1), (1, 0)])
    kept = dot_tn(mine, grad_result)
    total = (kept + got.astype(F32)).astype(BF16)
    places = chips * lax.axis_size("dp")
    total = total.reshape(places, -1, total.shape[-1])
    total = lax.all_to_all(total, ("seq_0", "seq_1", "dp"), 0, 0, tiled=True)
    return jnp.sum(total.astype(F32), axis=0)


def shards(query_input, key_input, value_input, grad_output, out_weight, norm_gain):
    query, key, value, grad_result = query_input[0], key_input[0], value_input[0], grad_output[0]
    gain = norm_gain.reshape(1, FEATURES)
    full_weight = lax.all_gather(out_weight, SEQ_DP, axis=0, tiled=True)
    feat_key, block_kv = block_states(key, value)
    prefix = scanned(block_kv, False)
    feat_query, inside = inside_blocks(query, feat_key, value)
    mixed, split, normed, inverse = attend(inside, feat_query, prefix, gain)
    grad_weight = gradient_rows(split, grad_result)
    grad_mixed = dot_nt(grad_result, full_weight)
    grad_att, block_grad = norm_back(grad_mixed, normed, inverse, gain, feat_query)
    later = scanned(block_grad, True)
    result = dot_nn(mixed, full_weight).astype(BF16)
    grad_query, part_key, part_value = back_inside(
        query, feat_query, feat_key, value, grad_att, prefix
    )
    grad_key, grad_value = finish(key, feat_key, value, part_key, part_value, later)
    return (result[None], grad_query[None], grad_key[None], grad_value[None], grad_weight)


def solution(mesh):
    torus = Mesh(mesh.devices.reshape(4, 4, 2, mesh.shape["dp"]), ("seq_0", "seq_1", "seq_2", "dp"))
    placed = (
        P("dp", SEQ, None),
        P("dp", SEQ, None),
        P("dp", SEQ, None),
        P("dp", SEQ, None),
        P(SEQ_DP, None),
        P(),
    )
    return jax.shard_map(
        shards,
        mesh=torus,
        in_specs=placed,
        out_specs=(
            P("dp", SEQ, None),
            P("dp", SEQ, None),
            P("dp", SEQ, None),
            P("dp", SEQ, None),
            P(SEQ_DP, None),
        ),
        check_vma=False,
    )
```

profile of v0, /device:TPU:2, one launch (start us, length us, event | category | flops | bytes accessed | tf_op | source)
XLA Modules:
  0.0 233.0 jit_solution(6805625974080327973)
XLA Ops:
  7.2 0.0 copy-start
  7.2 0.0 all-gather.2.cloned.1.call-start
  7.2 0.7 all-gather.2.cloned.1.call-update
  7.9 0.0 copy-start.5
  7.9 1.6 copy-done.5
  9.5 5.7 %block_states.1 = (bf16[512,2048]{1,0:T(8,128)(2,1)S(1)}, bf16[16,128,128]{2,1,0:T(8,128)(2,1)S(1)}) custom-call(bf16[512,2048]{1,0:T(8,128)(2,1)S(1)} %bitcast.32, bf16[512,2048]{1,0:T(8,128)(2,1)} %bitcast.43), custom_call_target="tpu_custom_call" | custom-call | flops 536870912 | bytes 7340032 | tf_op jit(solution)/shard_map/block_states/pallas_call | solution.py:92
  15.2 0.0 copy-start.7
  15.2 1.3 copy-done.7
  16.5 19.5 %all_to_all.25.a = bf16[32,64,128]{2,1,0:T(8,128)(2,1)S(1)} all-to-all(bf16[32,64,128]{2,1,0:T(8,128)(2,1)S(1)} %bitcast.38), channel_id=1, replica_groups=mesh['seq_0'=4,'seq_1'=4,'seq_2'=2,'dp'=4] {'seq_0','seq_1','seq_2'}, dimensions={0} | all-to-all | bytes 1048576 | tf_op jit(solution)/shard_map/all_to_all | solution.py:158
  36.1 0.9 exclusive_sums.2
  37.0 4.2 %all-to-all-start.1 = ((bf16[32,64,128]{2,1,0:T(8,128)(2,1)}), bf16[32,64,128]{2,1,0:T(8,128)(2,1)S(1)}, u32[]{:S(2)}, u32[]{:S(2)}) async-start(bf16[32,64,128]{2,1,0:T(8,128)(2,1)} %exclusive_sums.2), calls=%async_computation.1 | async-start | bytes 1048576 | tf_op jit(solution)/shard_map/all_to_all | solution.py:160
  41.2 0.0 copy-start.11
  41.2 1.6 copy-done.11
  42.8 0.0 copy-start.10
  42.8 9.3 %inside_blocks.1 = (bf16[512,2048]{1,0:T(8,128)(2,1)S(1)}, f32[512,2048]{1,0:T(8,128)}) custom-call(bf16[512,2048]{1,0:T(8,128)(2,1)S(1)} %bitcast.41, bf16[512,2048]{1,0:T(8,128)(2,1)} %copy-done.7, bf16[512,2048]{1,0:T(8,128)(2,1)} %bitcast.44), custom_call_target="tpu_custom_call" | custom-call | flops 4294967296 | bytes 12582912 | tf_op jit(solution)/shard_map/inside_blocks/pallas_call | solution.py:118
  52.1 1.3 copy-done.2
  53.4 0.0 all-to-all-done.1
  53.4 0.0 copy-done.10
  53.4 6.6 %attend.1 = (bf16[512,2048]{1,0:T(8,128)(2,1)S(1)}, bf16[2,512,1024]{2,1,0:T(8,128)(2,1)S(1)}, f32[512,2048]{1,0:T(8,128)}, f32[512,128]{1,0:T(8,128)S(1)}) custom-call(f32[512,2048]{1,0:T(8,128)} %get-tuple-element.21.inside, bf16[512,2048]{1,0:T(8,128)(2,1)} %copy-done.2, bf16[16,128,128]{2,1,0:T(8,128)(2,1)S(1)} %bitcast.34, f32[1,2048]{1,0:T(1,128)S(1)} %bitcast.39), custom_call_target="tpu_custom_call" | custom-call | flops 536870912 | bytes 15728640 | tf_op jit(solution)/shard_map/attend/pallas_call | solution.py:195
  60.0 0.0 copy-done
  60.0 4.3 %convolution_convert_fusion = bf16[1024,2048]{1,0:T(8,128)(2,1)} fusion(bf16[1,512,2048]{2,1,0:T(8,128)(2,1)S(1)} %copy-done, bf16[2,512,1024]{2,1,0:T(8,128)(2,1)S(1)} %get-tuple-element.34, s32[]{:T(128)S(6)} %select_n.8), kind=kOutput, calls=%fused_computation.2 | convolution fusion | flops 2149580800 | bytes 7340036 | tf_op jit(solution)/shard_map/dot_general | solution.py:38
  64.3 0.0 copy-done.13
  64.3 0.0 copy-done.14
  64.3 0.9 collective-permute-start
  65.2 10.0 %collective-permute-done = bf16[1024,2048]{1,0:T(8,128)(2,1)} collective-permute-done((bf16[1024,2048]{1,0:T(8,128)(2,1)}, bf16[1024,2048]{1,0:T(8,128)(2,1)}, u32[]{:S(2)}, u32[]{:S(2)}) %collective-permute-start) | collective-permute-done | bytes 4194336 | tf_op jit(solution)/shard_map/ppermute | solution.py:316
  75.2 5.0 %add_convert_fusion = bf16[1024,2048]{1,0:T(8,128)(2,1)S(1)} fusion(bf16[1024,2048]{1,0:T(8,128)(2,1)} %collective-permute-done, bf16[1,512,2048]{2,1,0:T(8,128)(2,1)S(1)} %copy-done, bf16[2,512,1024]{2,1,0:T(8,128)(2,1)} %copy-done.14, s32[]{:T(128)S(6)} %select_n.7), kind=kOutput, calls=%fused_computation.1 | convolution fusion | flops 2153775104 | bytes 11534340 | tf_op jit(solution)/shard_map/dot_general | solution.py:38
  80.2 62.8 %all_to_all.26 = bf16[64,16,2048]{2,1,0:T(8,128)(2,1)S(1)} all-to-all(bf16[64,16,2048]{2,1,0:T(8,128)(2,1)S(1)} %bitcast.47), channel_id=1, replica_groups=mesh['seq_0'=4,'seq_1'=4,'seq_2'=2,'dp'=4] {'seq_0','seq_1','dp'}, dimensions={0} | all-to-all | bytes 8388608 | tf_op jit(solution)/shard_map/all_to_all | solution.py:321
  142.9 1.3 convert_reduce_fusion
  144.3 9.6 %fusion.4.grad_mixed = f32[512,2048]{1,0:T(8,128)} fusion(bf16[2048,2048]{1,0:T(8,128)(2,1)} %all-gather.2.cloned.1.call-done, bf16[1,512,2048]{2,1,0:T(8,128)(2,1)S(1)} %copy-done), kind=kOutput, calls=%fused_computation.8 | convolution fusion | flops 4294967296 | bytes 14680064 | tf_op jit(solution)/shard_map/dot_general | solution.py:34
  153.9 0.0 copy-done.3
  153.9 15.0 %norm_back.1 = (bf16[512,2048]{1,0:T(8,128)(2,1)S(1)}, bf16[16,128,128]{2,1,0:T(8,128)(2,1)S(1)}) custom-call(f32[512,2048]{1,0:T(8,128)} %fusion.4.grad_mixed, f32[512,2048]{1,0:T(8,128)} %get-tuple-element.25.normed, f32[512,128]{1,0:T(8,128)S(1)} %get-tuple-element.26.inverse, f32[1,2048]{1,0:T(1,128)S(1)} %bitcast.40, bf16[512,2048]{1,0:T(8,128)(2,1)S(1)} %copy-done.3), custom_call_target="tpu_custom_call" | custom-call | flops 536870912 | bytes 13631488 | tf_op jit(solution)/shard_map/norm_back/pallas_call | solution.py:240
  168.8 0.0 copy-start.9
  168.8 0.8 copy-done.9
  169.6 1.3 copy-done.15
  171.0 3.9 %all-to-all-start.2 = ((bf16[32,64,128]{2,1,0:T(8,128)(2,1)}), bf16[32,64,128]{2,1,0:T(8,128)(2,1)S(1)}, u32[]{:S(2)}, u32[]{:S(2)}) async-start(bf16[32,64,128]{2,1,0:T(8,128)(2,1)} %bitcast.37), calls=%async_computation.2 | async-start | bytes 1048576 | tf_op jit(solution)/shard_map/all_to_all | solution.py:158
  174.9 0.0 copy-done.4
  174.9 0.0 copy-start.12
  174.9 1.6 copy-done.12
  176.5 18.1 %back_inside.1 = (bf16[512,2048]{1,0:T(8,128)(2,1)}, f32[512,2048]{1,0:T(8,128)}, f32[512,2048]{1,0:T(8,128)}) custom-call(bf16[512,2048]{1,0:T(8,128)(2,1)S(1)} %bitcast.42, bf16[512,2048]{1,0:T(8,128)(2,1)S(1)} %copy-done.4, bf16[512,2048]{1,0:T(8,128)(2,1)} %copy-done.7, bf16[512,2048]{1,0:T(8,128)(2,1)} %bitcast.45, bf16[512,2048]{1,0:T(8,128)(2,1)} %copy-done.15, ...), custom_call_target="tpu_custom_call" | custom-call | flops 12884901888 | bytes 20971520 | tf_op jit(solution)/shard_map/back_inside/pallas_call | solution.py:277
  194.6 0.0 all-to-all-done.2.a
  194.6 0.9 exclusive_sums.3
  195.5 7.4 %all-to-all-start.3 = ((bf16[32,64,128]{2,1,0:T(8,128)(2,1)}), bf16[32,64,128]{2,1,0:T(8,128)(2,1)S(1)}, u32[]{:S(2)}, u32[]{:S(2)}) async-start(bf16[32,64,128]{2,1,0:T(8,128)(2,1)} %exclusive_sums.3), calls=%async_computation.3 | async-start | bytes 1048576 | tf_op jit(solution)/shard_map/all_to_all | solution.py:160
  202.9 9.8 %fusion = bf16[1,512,2048]{2,1,0:T(8,128)(2,1)} fusion(bf16[512,2048]{1,0:T(8,128)(2,1)} %copy-done.13, bf16[2048,2048]{1,0:T(8,128)(2,1)} %all-gather.2.cloned.1.call-done), kind=kOutput, calls=%fused_computation.4 | convolution fusion | flops 4296015872 | bytes 12582912 | tf_op jit(solution)/shard_map/dot_general | solution.py:30
  212.7 1.2 all-to-all-done.3
  213.9 1.6 copy-done.6
  215.5 1.6 copy-done.8
  217.1 9.0 %finish.1 = (bf16[512,2048]{1,0:T(8,128)(2,1)}, bf16[512,2048]{1,0:T(8,128)(2,1)}) custom-call(bf16[512,2048]{1,0:T(8,128)(2,1)S(1)} %bitcast.33, bf16[512,2048]{1,0:T(8,128)(2,1)S(1)} %copy-done.8, bf16[512,2048]{1,0:T(8,128)(2,1)} %bitcast.46, f32[512,2048]{1,0:T(8,128)} %get-tuple-element.29.part_key, f32[512,2048]{1,0:T(8,128)} %get-tuple-element.30.part_value, ...), custom_call_target="tpu_custom_call" | custom-call | flops 1073741824 | bytes 18874368 | tf_op jit(solution)/shard_map/finish/pallas_call | solution.py:298
  226.2 0.0 copy-done.1
  (10 shorter events, 0.0 us)
Async XLA Ops:
  7.2 52.8 %copy-start = (bf16[1,512,2048]{2,1,0:T(8,128)(2,1)S(1)}, bf16[1,512,2048]{2,1,0:T(8,128)(2,1)}, u32[]{:S(2)}) copy-start(bf16[1,512,2048]{2,1,0:T(8,128)(2,1)} %param.9) | copy-start | bytes 6291460
  7.2 137.1 %all-gather.2.cloned.1.call-start = ((), (), s32[]{:S(2)}) async-start(), calls=%async_computation.5 | async-start | bytes 8454144 | tf_op jit(solution)/shard_map/all_gather | solution.py:328
  7.9 1.6 copy-start.5
  15.2 1.3 copy-start.7
  37.0 16.4 %all-to-all-start.1 = ((bf16[32,64,128]{2,1,0:T(8,128)(2,1)}), bf16[32,64,128]{2,1,0:T(8,128)(2,1)S(1)}, u32[]{:S(2)}, u32[]{:S(2)}) async-start(bf16[32,64,128]{2,1,0:T(8,128)(2,1)} %exclusive_sums.2), calls=%async_computation.1 | async-start | bytes 1048576 | tf_op jit(solution)/shard_map/all_to_all | solution.py:160
  41.2 1.6 copy-start.11
  42.8 10.6 %copy-start.10 = (f32[2048]{0:T(1024)S(1)}, f32[2048]{0:T(1024)}, u32[]{:S(2)}) copy-start(f32[2048]{0:T(1024)} %param.11) | copy-start | bytes 24580
  52.1 1.3 copy-start.2
  60.0 4.4 %copy-start.13 = (bf16[512,2048]{1,0:T(8,128)(2,1)}, bf16[512,2048]{1,0:T(8,128)(2,1)S(1)}, u32[]{:S(2)}) copy-start(bf16[512,2048]{1,0:T(8,128)(2,1)S(1)} %get-tuple-element.24) | copy-start | bytes 6291460
  60.0 4.4 %copy-start.14 = (bf16[2,512,1024]{2,1,0:T(8,128)(2,1)}, bf16[2,512,1024]{2,1,0:T(8,128)(2,1)S(1)}, u32[]{:S(2)}) copy-start(bf16[2,512,1024]{2,1,0:T(8,128)(2,1)S(1)} %get-tuple-element.34) | copy-start | bytes 6291460
  64.3 10.9 %collective-permute-start = (bf16[1024,2048]{1,0:T(8,128)(2,1)}, bf16[1024,2048]{1,0:T(8,128)(2,1)}, u32[]{:S(2)}, u32[]{:S(2)}) collective-permute-start(bf16[1024,2048]{1,0:T(8,128)(2,1)} %convolution_convert_fusion), channel_id=1, source_target_pairs={{0,4},{4,0},{1,5},{5,1},{2,6},{6,2},{3,7},{7,3},{8,12},{12,8},{9,1... | collective-permute-start | bytes 12582920 | tf_op jit(solution)/shard_map/ppermute | solution.py:316
  144.3 9.6 %copy-start.3 = (bf16[512,2048]{1,0:T(8,128)(2,1)S(1)}, bf16[512,2048]{1,0:T(8,128)(2,1)}, u32[]{:S(2)}) copy-start(bf16[512,2048]{1,0:T(8,128)(2,1)} %copy-done.2) | copy-start | bytes 6291460
  153.9 21.0 %copy-start.4 = (bf16[512,2048]{1,0:T(8,128)(2,1)S(1)}, bf16[512,2048]{1,0:T(8,128)(2,1)}, u32[]{:S(2)}) copy-start(bf16[512,2048]{1,0:T(8,128)(2,1)} %copy-done.2) | copy-start | bytes 6291460
  168.8 0.8 copy-start.9
  169.6 1.3 copy-start.15
  171.0 23.6 %all-to-all-start.2 = ((bf16[32,64,128]{2,1,0:T(8,128)(2,1)}), bf16[32,64,128]{2,1,0:T(8,128)(2,1)S(1)}, u32[]{:S(2)}, u32[]{:S(2)}) async-start(bf16[32,64,128]{2,1,0:T(8,128)(2,1)} %bitcast.37), calls=%async_computation.2 | async-start | bytes 1048576 | tf_op jit(solution)/shard_map/all_to_all | solution.py:158
  174.9 1.6 copy-start.12
  195.5 18.5 %all-to-all-start.3 = ((bf16[32,64,128]{2,1,0:T(8,128)(2,1)}), bf16[32,64,128]{2,1,0:T(8,128)(2,1)S(1)}, u32[]{:S(2)}, u32[]{:S(2)}) async-start(bf16[32,64,128]{2,1,0:T(8,128)(2,1)} %exclusive_sums.3), calls=%async_computation.3 | async-start | bytes 1048576 | tf_op jit(solution)/shard_map/all_to_all | solution.py:160
  213.9 1.6 copy-start.6
  215.5 1.6 copy-start.8
  217.1 9.1 %copy-start.1 = (bf16[1,512,2048]{2,1,0:T(8,128)(2,1)S(1)}, bf16[1,512,2048]{2,1,0:T(8,128)(2,1)}, u32[]{:S(2)}) copy-start(bf16[1,512,2048]{2,1,0:T(8,128)(2,1)} %param.9) | copy-start | bytes 6291460
Sparse Core Ops, SparseCore 0:
  11.1 73.5 all-gather.1
where the time goes:
time: 237 us; the launch traced here: 233 us
  blocking collectives  82.3 us (35%)
  Pallas kernels  65.4 us (28%)
  matrix products  28.7 us (12%)
  starting transfers between devices  16.4 us (7%)
  between operations  14.2 us (6%)
  local copies, waits for them, and re-layouts  12.7 us (5%)
  waiting for transfers between devices  11.9 us (5%)
    all_to_all x1, blocking collectives, gradient_rows(): total = lax.all_to_all(total, ('seq_0', 'seq_1', 'dp'), 0, 0, tiled=True)  62.8 us
    all_to_all x1, blocking collectives, scanned(): pieces = lax.all_to_all(pieces, SEQ, 0, 0, tiled=True)  19.5 us
    pallas_call x1, Pallas kernels, back_inside(): call(back_body, (HEADS // 2,), [PAIR_SPEC] * 5 + [STATE_SPEC], [PAIR_SPEC...  18.1 us
    pallas_call x1, Pallas kernels, norm_back(): call(norm_back_body, (BLOCK // ROWS,), [ROW_SPEC, ROW_SPEC, EDGE_SPEC, GA...  15 us
    unnamed x32, local copies, waits for them, and re-layouts  12.7 us
    all_to_all x2, starting transfers between devices, scanned(): sums = lax.all_to_all(sums, SEQ, 0, 0, tiled=True)  11.6 us
    ppermute x1, waiting for transfers between devices, gradient_rows(): got = lax.ppermute(sent, 'seq_2', [(0, 1), (1, 0)])  9.99 us
    dot_general x1, matrix products, dot_nn(): lax.dot_general(left, right, (((1,), (0,)), ((), ())), preferred_element_...  9.84 us
  transfers between devices with their start and end apart: 5, of which 2 were waited for; matrix products, arithmetic and copies ran while one was open for 9% of the time, Pallas kernels for 17%

commit v1 on v0

--- a/solution.py
+++ b/solution.py
@@ -6,11 +6,13 @@
 from jax.sharding import Mesh
 from jax.sharding import PartitionSpec as P
 
+
 HEADS = 16
 HEAD_DIM = 128
 BLOCK = 512
 HALF = BLOCK // 2
-PAIR = 2 * HEAD_DIM
+GROUP = 4
+PAIR = GROUP * HEAD_DIM
 FEATURES = HEADS * HEAD_DIM
 ROWS = 128
 SEQ = ("seq_0", "seq_1", "seq_2")
@@ -59,7 +61,7 @@
     return pl.BlockSpec(shape, index)
 
 
-def call(body, grid, in_specs, out_specs, out_shape, flops, moved, scratch=(), name=None):
+def call(body, grid, in_specs, out_specs, out_shape, flops, moved, scratch=()):
     return pl.pallas_call(
         body,
         grid=grid,
@@ -67,14 +69,13 @@
         out_specs=out_specs,
         out_shape=out_shape,
         scratch_shapes=scratch,
-        compiler_params=pltpu.CompilerParams(vmem_limit_bytes=48 * 1024 * 1024),
+        compiler_params=pltpu.CompilerParams(vmem_limit_bytes=60 * 1024 * 1024),
         cost_estimate=pl.CostEstimate(flops=flops, bytes_accessed=moved, transcendentals=0),
-        name=name,
     )
 
 
 PAIR_SPEC = spec((BLOCK, PAIR), lambda i: (0, i))
-STATE_SPEC = spec((2, HEAD_DIM, HEAD_DIM), lambda i: (i, 0, 0))
+STATE_SPEC = spec((GROUP, HEAD_DIM, HEAD_DIM), lambda i: (i, 0, 0))
 WIDE_LOW = jax.ShapeDtypeStruct((BLOCK, FEATURES), BF16)
 WIDE = jax.ShapeDtypeStruct((BLOCK, FEATURES), F32)
 STATE_LOW = jax.ShapeDtypeStruct((HEADS, HEAD_DIM, HEAD_DIM), BF16)
@@ -82,7 +83,7 @@
 
 
 def states_body(key, value, feat_key, state):
-    for i in range(2):
+    for i in range(GROUP):
         low = silu_low(key[:, head(i)])
         feat_key[:, head(i)] = low
         state[i] = dot_tn(low, value[:, head(i)]).astype(BF16)
@@ -91,18 +92,17 @@
 def block_states(key, value):
     return call(
         states_body,
-        (HEADS // 2,),
+        (HEADS // GROUP,),
         [PAIR_SPEC, PAIR_SPEC],
         [PAIR_SPEC, STATE_SPEC],
         [WIDE_LOW, STATE_LOW],
         1 << 29,
         7 * MIB,
-        name="block_states",
     )(key, value)
 
 
 def inside_body(query, feat_key, value, feat_query, inside):
-    for i in range(2):
+    for i in range(GROUP):
         low = silu_low(query[:, head(i)])
         feat_query[:, head(i)] = low
         keys = feat_key[:, head(i)]
@@ -117,13 +117,12 @@
 def inside_blocks(query, feat_key, value):
     return call(
         inside_body,
-        (HEADS // 2,),
+        (HEADS // GROUP,),
         [PAIR_SPEC] * 3,
         [PAIR_SPEC] * 2,
         [WIDE_LOW, WIDE],
         1 << 32,
         12 * MIB,
-        name="inside_blocks",
     )(query, feat_key, value)
 
 
@@ -146,7 +145,6 @@
         jax.ShapeDtypeStruct(pieces.shape, BF16),
         1 << 23,
         MIB,
-        name="exclusive_sums",
     )(pieces)
 
 
@@ -205,53 +203,69 @@
         ],
         1 << 29,
         15 * MIB,
-        name="attend",
     )(inside, feat_query, state, gain)
 
 
-def norm_back_body(grad_mixed, normed, inverse, gain, feat_query, grad_att, state, sums):
+CHUNK = 2 * HEAD_DIM
+CHUNKS = FEATURES // CHUNK
+
+
+def norm_back_body(
+    grad, weight, normed, inverse, gain, feat_query, grad_att, state, hats, norms, feats, products
+):
     step = pl.program_id(0)
-    products = jnp.zeros((ROWS, HEAD_DIM), F32)
-    for i in range(HEADS):
-        hat = grad_mixed[:, head(i)] * gain[:, head(i)]
-        products = products + hat * normed[:, head(i)]
-    mean = jnp.sum(products, axis=1, keepdims=True) / FEATURES
-    scale = inverse[:, :1]
-    for i in range(HEADS):
-        hat = grad_mixed[:, head(i)] * gain[:, head(i)]
-        low = ((hat - normed[:, head(i)] * mean) * scale).astype(BF16)
-        grad_att[:, head(i)] = low
-        update = dot_tn(feat_query[:, head(i)], low)
-
-        @pl.when(step == 0)
-        def _():
-            sums[i] = update
-
-        @pl.when(step > 0)
-        def _():
-            sums[i] = sums[i] + update
-
-    @pl.when(step == pl.num_programs(0) - 1)
+
+    @pl.when(step == 0)
     def _():
-        state[...] = sums[...].astype(BF16)
-
-
-def norm_back(grad_mixed, normed, inverse, gain, feat_query):
+        products[...] = jnp.zeros_like(products)
+
+    hat = dot_nt(grad[...], weight[...]) * gain[...]
+    product = hat * normed[...]
+    products[...] += product[:, :HEAD_DIM] + product[:, HEAD_DIM:]
+    hats[step] = hat
+    norms[step] = normed[...]
+    feats[step] = feat_query[...]
+
+    @pl.when(step == CHUNKS - 1)
+    def _():
+        mean = jnp.sum(products[...], axis=1, keepdims=True) / FEATURES
+        scale = inverse[:, :1]
+        for i in range(HEADS):
+            c, at = i // 2, head(i % 2)
+            low = ((hats[c, :, at] - norms[c, :, at] * mean) * scale).astype(BF16)
+            grad_att[:, head(i)] = low
+            state[i] = dot_tn(feats[c, :, at], low).astype(BF16)
+
+
+def norm_back(grad_result, weight, normed, inverse, gain, feat_query):
+    part = spec((BLOCK, CHUNK), lambda i: (0, i))
+    whole = spec((BLOCK, FEATURES), lambda i: (0, 0))
     return call(
         norm_back_body,
-        (BLOCK // ROWS,),
-        [ROW_SPEC, ROW_SPEC, EDGE_SPEC, GAIN_SPEC, ROW_SPEC],
-        [ROW_SPEC, ALL_STATES],
+        (CHUNKS,),
+        [
+            whole,
+            spec((CHUNK, FEATURES), lambda i: (i, 0)),
+            part,
+            spec((BLOCK, HEAD_DIM), lambda i: (0, 0)),
+            spec((1, CHUNK), lambda i: (0, i)),
+            part,
+        ],
+        [whole, ALL_STATES],
         [WIDE_LOW, STATE_LOW],
-        1 << 29,
-        13 * MIB,
-        scratch=[pltpu.VMEM((HEADS, HEAD_DIM, HEAD_DIM), F32)],
-        name="norm_back",
-    )(grad_mixed, normed, inverse, gain, feat_query)
+        5 << 30,
+        18 * MIB,
+        scratch=[
+            pltpu.VMEM((CHUNKS, BLOCK, CHUNK), F32),
+            pltpu.VMEM((CHUNKS, BLOCK, CHUNK), F32),
+            pltpu.VMEM((CHUNKS, BLOCK, CHUNK), BF16),
+            pltpu.VMEM((BLOCK, HEAD_DIM), F32),
+        ],
+    )(grad_result, weight, normed, inverse, gain, feat_query)
 
 
 def back_body(query, feat_query, feat_key, value, grad, state, grad_query, part_key, part_value):
-    for i in range(2):
+    for i in range(GROUP):
         at = head(i)
         q0, q1 = feat_query[:HALF, at], feat_query[HALF:, at]
         k0, k1 = feat_key[:HALF, at], feat_key[HALF:, at]
@@ -276,18 +290,17 @@
 def back_inside(query, feat_query, feat_key, value, grad, state):
     return call(
         back_body,
-        (HEADS // 2,),
+        (HEADS // GROUP,),
         [PAIR_SPEC] * 5 + [STATE_SPEC],
         [PAIR_SPEC] * 3,
         [WIDE_LOW, WIDE, WIDE],
         3 << 32,
         20 * MIB,
-        name="back_inside",
     )(query, feat_query, feat_key, value, grad, state)
 
 
 def finish_body(key, feat_key, value, part_key, part_value, later, grad_key, grad_value):
-    for i in range(2):
+    for i in range(GROUP):
         at = head(i)
         fk = part_key[:, at] + dot_nt(value[:, at], later[i])
         grad_key[:, at] = (fk * silu_slope(key[:, at])).astype(BF16)
@@ -297,32 +310,135 @@
 def finish(key, feat_key, value, part_key, part_value, later):
     return call(
         finish_body,
-        (HEADS // 2,),
+        (HEADS // GROUP,),
         [PAIR_SPEC] * 5 + [STATE_SPEC],
         [PAIR_SPEC] * 2,
         [WIDE_LOW, WIDE_LOW],
         1 << 30,
         18 * MIB,
-        name="finish",
     )(key, feat_key, value, part_key, part_value, later)
 
 
+COLORS = 4
+WIDTH = FEATURES // COLORS
+SLAB = 16
+PLACES = 64
+CYCLES = (((0, 1), (1, 0), (2, 3), (3, 2)), ((0, 3), (3, 0), (1, 2), (2, 1)))
+
+
+def on_ring(low, high):
+    return low + high * (3 - 2 * low)
+
+
+def my_bits(axis):
+    at = lax.axis_index(axis)
+    high = (at >= 2).astype(jnp.int32)
+    low = ((at == 1) | (at == 2)).astype(jnp.int32)
+    return (low, high)
+
+
+def hop(sent, axis, which):
+    return lax.ppermute(sent, axis, CYCLES[which])
+
+
+def product_body(place, left, right, out):
+    out[...] = dot_tn(left[0], right[...]).astype(BF16)
+
+
+def first_body(color, place, left, right, got, kept, sent, acc):
+    acc[...] = (dot_tn(left[0], right[...]) + got[...].astype(F32)).astype(BF16)
+    bit = place[2 + color]
+    for side, out in ((bit, kept), (1 - bit, sent)):
+        for s in range(PLACES // 2):
+            other, rest, z = s // 16, (s // 4) % 4, s % 4
+            z = on_ring(z // 2, z % 2)
+            far = on_ring(rest // 2, rest % 2)
+            near = on_ring(side, other) if color % 2 == 0 else on_ring(other, side)
+            y, x = (far, near) if color < 2 else (near, far)
+            at = pl.multiple_of((y * 16 + z * 4 + x) * SLAB, SLAB)
+            out[s * SLAB : (s + 1) * SLAB] = acc[pl.ds(at, SLAB)]
+
+
 def gradient_rows(split, grad_result):
-    chips = lax.axis_size("seq_0") * lax.axis_size("seq_1")
     core = lax.axis_index("seq_2")
-    mine = lax.dynamic_index_in_dim(split, core, 0, keepdims=False)
-    other = lax.dynamic_index_in_dim(split, 1 - core, 0, keepdims=False)
-    sent = dot_tn(other, grad_result).astype(BF16)
-    got = lax.ppermute(sent, "seq_2", [(0, 1), (1, 0)])
-    kept = dot_tn(mine, grad_result)
-    total = (kept + got.astype(F32)).astype(BF16)
-    places = chips * lax.axis_size("dp")
-    total = total.reshape(places, -1, total.shape[-1])
-    total = lax.all_to_all(total, ("seq_0", "seq_1", "dp"), 0, 0, tiled=True)
-    return jnp.sum(total.astype(F32), axis=0)
-
-
-def shards(query_input, key_input, value_input, grad_output, out_weight, norm_gain):
+    xs, ys, zs = my_bits("dp"), my_bits("seq_0"), my_bits("seq_1")
+    place = jnp.stack([core, 1 - core, xs[0], xs[1], ys[0], ys[1]]).astype(jnp.int32)
+    half = FEATURES // 2
+
+    def grid_spec(which, color, more, outs):
+        return pltpu.PrefetchScalarGridSpec(
+            num_scalar_prefetch=1,
+            grid=(1,),
+            in_specs=[
+                pl.BlockSpec((1, BLOCK, half), lambda i, p: (p[which], 0, 0)),
+                pl.BlockSpec((BLOCK, WIDTH), lambda i, p: (0, color)),
+            ]
+            + more,
+            out_specs=outs,
+            scratch_shapes=[pltpu.VMEM((half, WIDTH), BF16)] if more else [],
+        )
+
+    whole = pl.BlockSpec((half, WIDTH), lambda i, p: (0, 0))
+    part = pl.BlockSpec((half // 2, WIDTH), lambda i, p: (0, 0))
+    params = pltpu.CompilerParams(vmem_limit_bytes=32 * MIB)
+    cost = pl.CostEstimate(flops=1 << 30, bytes_accessed=4 * MIB, transcendentals=0)
+
+    gots = []
+    for color in range(COLORS):
+        sent = pl.pallas_call(
+            product_body,
+            grid_spec=grid_spec(1, color, [], whole),
+            out_shape=jax.ShapeDtypeStruct((half, WIDTH), BF16),
+            compiler_params=params,
+            cost_estimate=cost,
+            name="pair_product",
+        )(place, split, grad_result)
+        gots.append(lax.ppermute(sent, "seq_2", [(0, 1), (1, 0)]))
+    order = ((xs, "dp"), (ys, "seq_0"))
+    keeps = []
+    for color in range(COLORS):
+        kept, sent = pl.pallas_call(
+            lambda *refs, color=color: first_body(color, *refs),
+            grid_spec=grid_spec(0, color, [whole], [part, part]),
+            out_shape=[jax.ShapeDtypeStruct((half // 2, WIDTH), BF16)] * 2,
+            compiler_params=params,
+            cost_estimate=cost,
+            name="first_halves",
+        )(place, split, grad_result, gots[color])
+        keeps.append((kept, hop(sent, order[color // 2][1], color % 2)))
+
+    def halves(total, bit, axis):
+        count = total.shape[axis] // 2
+        kept = lax.dynamic_slice_in_dim(total, bit * count, count, axis)
+        sent = lax.dynamic_slice_in_dim(total, (1 - bit) * count, count, axis)
+        return (kept, sent)
+
+    def add(kept, got):
+        return (kept.astype(F32) + got.astype(F32)).astype(BF16)
+
+    seconds = []
+    for color, (kept, got) in enumerate(keeps):
+        bits, axis = order[color // 2]
+        which = 1 - color % 2
+        kept, sent = halves(add(kept, got), bits[which], 0)
+        seconds.append((kept, hop(sent, axis, which)))
+    joined = []
+    for near in range(2):
+        bits, axis = order[1 - near]
+        total = jnp.stack([add(*seconds[2 * near]), add(*seconds[2 * near + 1])])
+        for which in range(2):
+            kept, sent = halves(total, bits[which], 1)
+            total = add(kept, hop(sent, axis, which))
+        joined.append(total)
+    total = jnp.concatenate(joined, axis=0)
+    kept, sent = halves(total, zs[0], 1)
+    total = add(kept, hop(sent, "seq_1", 0))
+    kept, sent = halves(total, zs[1], 1)
+    total = kept.astype(F32) + hop(sent, "seq_1", 1).astype(F32)
+    return jnp.concatenate([total[c] for c in range(COLORS)], axis=1)
+
+
+def layer(query_input, key_input, value_input, grad_output, out_weight, norm_gain):
     query, key, value, grad_result = query_input[0], key_input[0], value_input[0], grad_output[0]
     gain = norm_gain.reshape(1, FEATURES)
     full_weight = lax.all_gather(out_weight, SEQ_DP, axis=0, tiled=True)
@@ -331,8 +447,9 @@
     feat_query, inside = inside_blocks(query, feat_key, value)
     mixed, split, normed, inverse = attend(inside, feat_query, prefix, gain)
     grad_weight = gradient_rows(split, grad_result)
-    grad_mixed = dot_nt(grad_result, full_weight)
-    grad_att, block_grad = norm_back(grad_mixed, normed, inverse, gain, feat_query)
+    grad_att, block_grad = norm_back(
+        grad_result, full_weight, normed, inverse, gain, feat_query
+    )
     later = scanned(block_grad, True)
     result = dot_nn(mixed, full_weight).astype(BF16)
     grad_query, part_key, part_value = back_inside(
@@ -353,7 +470,7 @@
         P(),
     )
     return jax.shard_map(
-        shards,
+        layer,
         mesh=torus,
         in_specs=placed,
         out_specs=(

time: 237 us -> 209 us (0.88)
  the two profiles are of different devices: /device:TPU:2 before, /device:TPU:1 now
where the time goes in v1:
time: 209 us; the launch traced here: 208 us
  Pallas kernels  81.1 us (39%)
  starting transfers between devices  36.8 us (18%)
  waiting for transfers between devices  35.3 us (17%)
  blocking collectives  21.5 us (10%)
  between operations  14.4 us (7%)
  matrix products  9.05 us (4%)
  local copies, waits for them, and re-layouts  6.7 us (3%)
  other arithmetic  2.9 us (1%)
    ppermute x14, waiting for transfers between devices, hop(): return lax.ppermute(sent, axis, CYCLES[which])  28.5 us
    all_to_all x1, blocking collectives, scanned(): pieces = lax.all_to_all(pieces, SEQ, 0, 0, tiled=True)  21.5 us
    pallas_call x1, Pallas kernels, back_inside(): call(back_body, (HEADS // GROUP,), [PAIR_SPEC] * 5 + [STATE_SPEC], [PAIR_...  17.7 us
    ppermute x14, starting transfers between devices, hop(): return lax.ppermute(sent, axis, CYCLES[which])  14.3 us
    pallas_call x1, Pallas kernels, norm_back(): call(norm_back_body, (CHUNKS,), [whole, spec((CHUNK, FEATURES), lambda i:...  14 us
    all_to_all x2, starting transfers between devices, scanned(): sums = lax.all_to_all(sums, SEQ, 0, 0, tiled=True)  11.2 us
    all_to_all x1, starting transfers between devices, scanned(): pieces = lax.all_to_all(pieces, SEQ, 0, 0, tiled=True)  10.2 us
    dot_general x1, matrix products, dot_nn(): lax.dot_general(left, right, (((1,), (0,)), ((), ())), preferred_element_...  9.05 us
  transfers between devices with their start and end apart: 22, of which 14 were waited for; matrix products, arithmetic and copies ran while one was open for 6% of the time, Pallas kernels for 27%

profile of v1, /device:TPU:1, one launch (start us, length us, event | category | flops | bytes accessed | tf_op | source)
XLA Modules:
  0.0 207.7 jit_solution(18437230667479452875)
XLA Ops:
  7.9 4.7 %shard_map.101 = (bf16[512,2048]{1,0:T(8,128)(2,1)}, bf16[16,128,128]{2,1,0:T(8,128)(2,1)}) custom-call(bf16[512,2048]{1,0:T(8,128)(2,1)} %bitcast.47, bf16[512,2048]{1,0:T(8,128)(2,1)} %bitcast.49), custom_call_target="tpu_custom_call" | custom-call | flops 536870912 | bytes 7340032 | tf_op jit(solution)/shard_map/pallas_call | solution.py:93
  12.6 21.5 %all_to_all.20.a = bf16[32,64,128]{2,1,0:T(8,128)(2,1)} all-to-all(bf16[32,64,128]{2,1,0:T(8,128)(2,1)} %bitcast.57), channel_id=1, replica_groups=mesh['seq_0'=4,'seq_1'=4,'seq_2'=2,'dp'=4] {'seq_0','seq_1','seq_2'}, dimensions={0} | all-to-all | bytes 1048576 | tf_op jit(solution)/shard_map/all_to_all | solution.py:156
  34.2 1.8 shard_map.103
  35.9 3.7 %all-to-all-start.1 = ((bf16[32,64,128]{2,1,0:T(8,128)(2,1)}), bf16[32,64,128]{2,1,0:T(8,128)(2,1)S(1)}, u32[]{:S(2)}, u32[]{:S(2)}) async-start(bf16[32,64,128]{2,1,0:T(8,128)(2,1)} %shard_map.103), calls=%async_computation.1 | async-start | bytes 1048576 | tf_op jit(solution)/shard_map/all_to_all | solution.py:158
  39.7 7.9 %shard_map.102 = (bf16[512,2048]{1,0:T(8,128)(2,1)}, f32[512,2048]{1,0:T(8,128)}) custom-call(bf16[512,2048]{1,0:T(8,128)(2,1)} %bitcast.60, bf16[512,2048]{1,0:T(8,128)(2,1)} %get-tuple-element.28.feat_key, bf16[512,2048]{1,0:T(8,128)(2,1)} %bitcast.50), custom_call_target="tpu_custom_call" | custom-call | flops 4294967296 | bytes 12582912 | tf_op jit(solution)/shard_map/pallas_call | solution.py:118
  47.6 3.5 %all-to-all-done.1 = bf16[32,64,128]{2,1,0:T(8,128)(2,1)S(1)} async-done(((bf16[32,64,128]{2,1,0:T(8,128)(2,1)}), bf16[32,64,128]{2,1,0:T(8,128)(2,1)S(1)}, u32[]{:S(2)}, u32[]{:S(2)}) %all-to-all-start.1) | async-done | bytes 524320 | tf_op jit(solution)/shard_map/all_to_all | solution.py:158
  51.2 0.8 copy-done.6
  52.0 7.7 %shard_map.104 = (bf16[512,2048]{1,0:T(8,128)(2,1)}, bf16[2,512,1024]{2,1,0:T(8,128)(2,1)}, f32[512,2048]{1,0:T(8,128)}, f32[512,128]{1,0:T(8,128)}) custom-call(f32[512,2048]{1,0:T(8,128)} %get-tuple-element.29.inside, bf16[512,2048]{1,0:T(8,128)(2,1)} %get-tuple-element.30.feat_query, bf16[16,128,128]{2,1,0:T(8,128)(2,1)} %bitcast.53, f32[1,2048]{1,0:T(1,128)} %bitcast.58), custom_call_target="tpu_custom_call" | custom-call | flops 536870912 | bytes 15728640 | tf_op jit(solution)/shard_map/pallas_call | solution.py:193
  59.7 1.6 copy-done.1
  61.3 1.3 pair_product.4
  62.7 2.3 %pair_product.5 = bf16[1024,512]{1,0:T(8,128)(2,1)} custom-call(s32[6]{0:T(128)S(1)} %stack.45.place.refs_0_, bf16[2,512,1024]{2,1,0:T(8,128)(2,1)S(1)} %copy-done.1, bf16[512,2048]{1,0:T(8,128)(2,1)S(1)} %bitcast.40), custom_call_target="tpu_custom_call" | custom-call | flops 1073741824 | bytes 4194304 | tf_op jit(solution)/shard_map/pair_product/pallas_call | solution.py:388
  65.5 2.3 %pair_product.6 = bf16[1024,512]{1,0:T(8,128)(2,1)} custom-call(s32[6]{0:T(128)S(1)} %stack.45.place.refs_0_, bf16[2,512,1024]{2,1,0:T(8,128)(2,1)S(1)} %copy-done.1, bf16[512,2048]{1,0:T(8,128)(2,1)S(1)} %bitcast.41), custom_call_target="tpu_custom_call" | custom-call | flops 1073741824 | bytes 4194304 | tf_op jit(solution)/shard_map/pair_product/pallas_call | solution.py:388
  67.7 2.3 %pair_product.7 = bf16[1024,512]{1,0:T(8,128)(2,1)} custom-call(s32[6]{0:T(128)S(1)} %stack.45.place.refs_0_, bf16[2,512,1024]{2,1,0:T(8,128)(2,1)S(1)} %copy-done.1, bf16[512,2048]{1,0:T(8,128)(2,1)S(1)} %bitcast.42), custom_call_target="tpu_custom_call" | custom-call | flops 1073741824 | bytes 4194304 | tf_op jit(solution)/shard_map/pair_product/pallas_call | solution.py:388
  70.5 2.2 %first_halves.4 = (bf16[512,512]{1,0:T(8,128)(2,1)S(1)}, bf16[512,512]{1,0:T(8,128)(2,1)}) custom-call(s32[6]{0:T(128)S(1)} %stack.45.place.refs_0_, bf16[2,512,1024]{2,1,0:T(8,128)(2,1)S(1)} %copy-done.1, bf16[512,2048]{1,0:T(8,128)(2,1)S(1)} %bitcast.43, bf16[1024,512]{1,0:T(8,128)(2,1)S(1)} %collective-permute-done.refs_3_), custom_call_target="tpu_custom_call" | custom-call | flops 1073741824 | bytes 4194304 | tf_op jit(solution)/shard_map/first_halves/pallas_call | solution.py:400
  72.7 0.8 copy-done.3
  73.5 1.2 collective-permute-start.1
  74.7 1.7 copy-done.2
  76.4 2.7 %first_halves.5 = (bf16[512,512]{1,0:T(8,128)(2,1)S(1)}, bf16[512,512]{1,0:T(8,128)(2,1)S(1)}) custom-call(s32[6]{0:T(128)S(1)} %stack.45.place.refs_0_, bf16[2,512,1024]{2,1,0:T(8,128)(2,1)S(1)} %copy-done.2, bf16[512,2048]{1,0:T(8,128)(2,1)S(1)} %bitcast.44, bf16[1024,512]{1,0:T(8,128)(2,1)} %collective-permute-done.3.refs_3_), custom_call_target="tpu_custom_call" | custom-call | flops 1073741824 | bytes 4194304 | tf_op jit(solution)/shard_map/first_halves/pallas_call | solution.py:400
  79.1 1.9 collective-permute-start.4
  81.0 2.6 %first_halves.6 = (bf16[512,512]{1,0:T(8,128)(2,1)S(1)}, bf16[512,512]{1,0:T(8,128)(2,1)S(1)}) custom-call(s32[6]{0:T(128)S(1)} %stack.45.place.refs_0_, bf16[2,512,1024]{2,1,0:T(8,128)(2,1)S(1)} %copy-done.2, bf16[512,2048]{1,0:T(8,128)(2,1)S(1)} %bitcast.45, bf16[1024,512]{1,0:T(8,128)(2,1)} %collective-permute-done.8.refs_3_), custom_call_target="tpu_custom_call" | custom-call | flops 1073741824 | bytes 4194304 | tf_op jit(solution)/shard_map/first_halves/pallas_call | solution.py:400
  83.8 1.4 first_halves.7
  85.2 1.6 collective-permute-start.12
  86.8 5.0 %collective-permute-done.1 = bf16[512,512]{1,0:T(8,128)(2,1)} collective-permute-done((bf16[512,512]{1,0:T(8,128)(2,1)}, bf16[512,512]{1,0:T(8,128)(2,1)}, u32[]{:S(2)}, u32[]{:S(2)}) %collective-permute-start.1) | collective-permute-done | bytes 524320 | tf_op jit(solution)/shard_map/ppermute | solution.py:341
  91.8 1.2 add_convert_fusion.3
  93.0 1.7 collective-permute-start.2
  95.4 1.1 collective-permute-done.9
  96.6 1.6 collective-permute-start.10
  98.2 0.9 collective-permute-done.12
  99.4 2.3 %collective-permute-done.2 = bf16[256,512]{1,0:T(8,128)(2,1)S(1)} collective-permute-done((bf16[256,512]{1,0:T(8,128)(2,1)S(1)}, bf16[256,512]{1,0:T(8,128)(2,1)S(1)}, u32[]{:S(2)}, u32[]{:S(2)}) %collective-permute-start.2) | collective-permute-done | bytes 262176 | tf_op jit(solution)/shard_map/ppermute | solution.py:341
  102.1 1.3 collective-permute-start.6
  103.4 0.9 collective-permute-done.10
  104.4 1.1 collective-permute-done.13
  106.2 5.0 %collective-permute-done.6 = bf16[2,128,512]{2,1,0:T(8,128)(2,1)S(1)} collective-permute-done((bf16[2,128,512]{2,1,0:T(8,128)(2,1)S(1)}, bf16[2,128,512]{2,1,0:T(8,128)(2,1)S(1)}, u32[]{:S(2)}, u32[]{:S(2)}) %collective-permute-start.6) | collective-permute-done | bytes 262176 | tf_op jit(solution)/shard_map/ppermute | solution.py:341
  111.3 2.0 collective-permute-start.7
  113.4 1.0 collective-permute-start.15
  114.4 2.0 collective-permute-done.7
  116.4 2.4 %collective-permute-done.15 = bf16[2,64,512]{2,1,0:T(8,128)(2,1)S(1)} collective-permute-done((bf16[2,64,512]{2,1,0:T(8,128)(2,1)S(1)}, bf16[2,64,512]{2,1,0:T(8,128)(2,1)S(1)}, u32[]{:S(2)}, u32[]{:S(2)}) %collective-permute-start.15) | collective-permute-done | bytes 131104 | tf_op jit(solution)/shard_map/ppermute | solution.py:341
  119.0 3.9 %collective-permute-done.16 = bf16[4,32,512]{2,1,0:T(8,128)(2,1)S(1)} collective-permute-done((bf16[4,32,512]{2,1,0:T(8,128)(2,1)S(1)}, bf16[4,32,512]{2,1,0:T(8,128)(2,1)S(1)}, u32[]{:S(2)}, u32[]{:S(2)}) %collective-permute-start.16) | collective-permute-done | bytes 131104 | tf_op jit(solution)/shard_map/ppermute | solution.py:341
  123.6 3.7 %collective-permute-done.17 = bf16[4,16,512]{2,1,0:T(8,128)(2,1)S(1)} collective-permute-done((bf16[4,16,512]{2,1,0:T(8,128)(2,1)S(1)}, bf16[4,16,512]{2,1,0:T(8,128)(2,1)S(1)}, u32[]{:S(2)}, u32[]{:S(2)}) %collective-permute-start.17) | collective-permute-done | bytes 65568 | tf_op jit(solution)/shard_map/ppermute | solution.py:341
  128.0 14.0 %shard_map.105 = (bf16[512,2048]{1,0:T(8,128)(2,1)}, bf16[16,128,128]{2,1,0:T(8,128)(2,1)}) custom-call(bf16[512,2048]{1,0:T(8,128)(2,1)} %bitcast.38, bf16[2048,2048]{1,0:T(8,128)(2,1)} %all-gather.2.cloned.1.call-done.weight, f32[512,2048]{1,0:T(8,128)} %get-tuple-element.33.normed, f32[512,128]{1,0:T(8,128)} %get-tuple-element.34.inverse, ...), custom_call_target="tpu_custom_call" | custom-call | flops 5368709120 | bytes 18874368 | tf_op jit(solution)/shard_map/pallas_call | solution.py:243
  142.0 10.2 %all-to-all-start.2 = ((bf16[32,64,128]{2,1,0:T(8,128)(2,1)}), bf16[32,64,128]{2,1,0:T(8,128)(2,1)S(1)}, u32[]{:S(2)}, u32[]{:S(2)}) async-start(bf16[32,64,128]{2,1,0:T(8,128)(2,1)} %bitcast.56), calls=%async_computation.2 | async-start | bytes 1048576 | tf_op jit(solution)/shard_map/all_to_all | solution.py:156
  152.2 17.7 %shard_map.106 = (bf16[512,2048]{1,0:T(8,128)(2,1)}, f32[512,2048]{1,0:T(8,128)}, f32[512,2048]{1,0:T(8,128)}) custom-call(bf16[512,2048]{1,0:T(8,128)(2,1)} %bitcast.61, bf16[512,2048]{1,0:T(8,128)(2,1)} %get-tuple-element.30.feat_query, bf16[512,2048]{1,0:T(8,128)(2,1)} %get-tuple-element.28.feat_key, bf16[512,2048]{1,0:T(8,128)(2,1)} %bitcast.51, ...), custom_call_target="tpu_custom_call" | custom-call | flops 12884901888 | bytes 20971520 | tf_op jit(solution)/shard_map/pallas_call | solution.py:291
  170.8 1.8 shard_map.107
  172.6 7.5 %all-to-all-start.3 = ((bf16[32,64,128]{2,1,0:T(8,128)(2,1)}), bf16[32,64,128]{2,1,0:T(8,128)(2,1)S(1)}, u32[]{:S(2)}, u32[]{:S(2)}) async-start(bf16[32,64,128]{2,1,0:T(8,128)(2,1)} %shard_map.107), calls=%async_computation.3 | async-start | bytes 1048576 | tf_op jit(solution)/shard_map/all_to_all | solution.py:158
  180.1 9.0 %fusion = bf16[1,512,2048]{2,1,0:T(8,128)(2,1)} fusion(bf16[512,2048]{1,0:T(8,128)(2,1)S(1)} %copy-done.8, bf16[2048,2048]{1,0:T(8,128)(2,1)} %all-gather.2.cloned.1.call-done.weight), kind=kOutput, calls=%fused_computation.1 | convolution fusion | flops 4296015872 | bytes 12582912 | tf_op jit(solution)/shard_map/dot_general | solution.py:32
  189.2 2.5 %all-to-all-done.3 = bf16[32,64,128]{2,1,0:T(8,128)(2,1)S(1)} async-done(((bf16[32,64,128]{2,1,0:T(8,128)(2,1)}), bf16[32,64,128]{2,1,0:T(8,128)(2,1)S(1)}, u32[]{:S(2)}, u32[]{:S(2)}) %all-to-all-start.3) | async-done | bytes 524320 | tf_op jit(solution)/shard_map/all_to_all | solution.py:158
  191.7 0.8 copy-done.7
  192.5 8.3 %shard_map.108 = (bf16[512,2048]{1,0:T(8,128)(2,1)}, bf16[512,2048]{1,0:T(8,128)(2,1)}) custom-call(bf16[512,2048]{1,0:T(8,128)(2,1)} %bitcast.48, bf16[512,2048]{1,0:T(8,128)(2,1)} %get-tuple-element.28.feat_key, bf16[512,2048]{1,0:T(8,128)(2,1)} %bitcast.52, f32[512,2048]{1,0:T(8,128)} %get-tuple-element.37.part_key, ...), custom_call_target="tpu_custom_call" | custom-call | flops 1073741824 | bytes 18874368 | tf_op jit(solution)/shard_map/pallas_call | solution.py:311
  (60 shorter events, 6.8 us)
Async XLA Ops:
  7.2 120.8 %all-gather.2.cloned.1.call-start = ((), (), s32[]{:S(2)}) async-start(), calls=%async_computation.4 | async-start | bytes 8454144 | tf_op jit(solution)/shard_map/all_gather | solution.py:444
  35.9 15.2 %all-to-all-start.1 = ((bf16[32,64,128]{2,1,0:T(8,128)(2,1)}), bf16[32,64,128]{2,1,0:T(8,128)(2,1)S(1)}, u32[]{:S(2)}, u32[]{:S(2)}) async-start(bf16[32,64,128]{2,1,0:T(8,128)(2,1)} %shard_map.103), calls=%async_computation.1 | async-start | bytes 1048576 | tf_op jit(solution)/shard_map/all_to_all | solution.py:158
  51.2 0.8 copy-start.6
  52.0 7.7 %copy-start = (bf16[1,512,2048]{2,1,0:T(8,128)(2,1)S(1)}, bf16[1,512,2048]{2,1,0:T(8,128)(2,1)}, u32[]{:S(2)}) copy-start(bf16[1,512,2048]{2,1,0:T(8,128)(2,1)} %param.9) | copy-start | bytes 6291460
  59.7 1.6 copy-start.1
  62.6 7.9 %collective-permute-start = (bf16[1024,512]{1,0:T(8,128)(2,1)S(1)}, bf16[1024,512]{1,0:T(8,128)(2,1)S(1)}, u32[]{:S(2)}, u32[]{:S(2)}) collective-permute-start(bf16[1024,512]{1,0:T(8,128)(2,1)S(1)} %pair_product.4), channel_id=1, source_target_pairs={{0,4},{4,0},{1,5},{5,1},{2,6},{6,2},{3,7},{7,3},{8,12},{12,8},{9,1... | collective-permute-start | bytes 3145736 | tf_op jit(solution)/shard_map/ppermute | solution.py:396
  65.0 9.7 %collective-permute-start.3 = (bf16[1024,512]{1,0:T(8,128)(2,1)}, bf16[1024,512]{1,0:T(8,128)(2,1)}, u32[]{:S(2)}, u32[]{:S(2)}) collective-permute-start(bf16[1024,512]{1,0:T(8,128)(2,1)} %pair_product.5), channel_id=1, source_target_pairs={{0,4},{4,0},{1,5},{5,1},{2,6},{6,2},{3,7},{7,3},{8,12},{12,8},{9,1... | collective-permute-start | bytes 3145736 | tf_op jit(solution)/shard_map/ppermute | solution.py:396
  67.7 13.3 %collective-permute-start.8 = (bf16[1024,512]{1,0:T(8,128)(2,1)}, bf16[1024,512]{1,0:T(8,128)(2,1)}, u32[]{:S(2)}, u32[]{:S(2)}) collective-permute-start(bf16[1024,512]{1,0:T(8,128)(2,1)} %pair_product.6), channel_id=1, source_target_pairs={{0,4},{4,0},{1,5},{5,1},{2,6},{6,2},{3,7},{7,3},{8,12},{12,8},{9,1... | collective-permute-start | bytes 3145736 | tf_op jit(solution)/shard_map/ppermute | solution.py:396
  70.0 13.8 %collective-permute-start.11 = (bf16[1024,512]{1,0:T(8,128)(2,1)}, bf16[1024,512]{1,0:T(8,128)(2,1)S(1)}, u32[]{:S(2)}, u32[]{:S(2)}) collective-permute-start(bf16[1024,512]{1,0:T(8,128)(2,1)} %pair_product.7), channel_id=1, source_target_pairs={{0,4},{4,0},{1,5},{5,1},{2,6},{6,2},{3,7},{7,3},{8,12},{12,8},{9,1... | collective-permute-start | bytes 3145736 | tf_op jit(solution)/shard_map/ppermute | solution.py:396
  72.7 0.8 copy-start.3
  73.5 18.3 %collective-permute-start.1 = (bf16[512,512]{1,0:T(8,128)(2,1)}, bf16[512,512]{1,0:T(8,128)(2,1)}, u32[]{:S(2)}, u32[]{:S(2)}) collective-permute-start(bf16[512,512]{1,0:T(8,128)(2,1)} %get-tuple-element.44), channel_id=1, source_target_pairs={{0,1},{1,0},{2,3},{3,2},{4,5},{5,4},{6,7},{7,6},{8,9},{9,8},{10,11... | collective-permute-start | bytes 1572872 | tf_op jit(solution)/shard_map/ppermute | solution.py:341
  74.7 1.7 copy-start.2
  79.1 15.7 %collective-permute-start.4 = (bf16[512,512]{1,0:T(8,128)(2,1)S(1)}, bf16[512,512]{1,0:T(8,128)(2,1)S(1)}, u32[]{:S(2)}, u32[]{:S(2)}) collective-permute-start(bf16[512,512]{1,0:T(8,128)(2,1)S(1)} %get-tuple-element.46), channel_id=1, source_target_pairs={{0,3},{3,0},{1,2},{2,1},{4,7},{7,4},{5,6},{6,5},{8,11},{11,8},{9,1... | collective-permute-start | bytes 1572872 | tf_op jit(solution)/shard_map/ppermute | solution.py:341
  83.6 8.2 %copy-start.4 = (bf16[512,512]{1,0:T(8,128)(2,1)S(1)}, bf16[512,512]{1,0:T(8,128)(2,1)}, u32[]{:S(2)}) copy-start(bf16[512,512]{1,0:T(8,128)(2,1)} %copy-done.3) | copy-start | bytes 1572868
  83.6 12.8 %collective-permute-start.9 = (bf16[512,512]{1,0:T(8,128)(2,1)S(1)}, bf16[512,512]{1,0:T(8,128)(2,1)S(1)}, u32[]{:S(2)}, u32[]{:S(2)}) collective-permute-start(bf16[512,512]{1,0:T(8,128)(2,1)S(1)} %get-tuple-element.48), channel_id=1, source_target_pairs={{0,32},{32,0},{64,96},{96,64},{1,33},{33,1},{65,97},{97,65},{2,34}... | collective-permute-start | bytes 1572872 | tf_op jit(solution)/shard_map/ppermute | solution.py:341
  85.2 13.9 %collective-permute-start.12 = (bf16[512,512]{1,0:T(8,128)(2,1)S(1)}, bf16[512,512]{1,0:T(8,128)(2,1)S(1)}, u32[]{:S(2)}, u32[]{:S(2)}) collective-permute-start(bf16[512,512]{1,0:T(8,128)(2,1)S(1)} %get-tuple-element.50), channel_id=1, source_target_pairs={{0,96},{96,0},{32,64},{64,32},{1,97},{97,1},{33,65},{65,33},{2,98}... | collective-permute-start | bytes 1572872 | tf_op jit(solution)/shard_map/ppermute | solution.py:341
  93.0 8.7 %collective-permute-start.2 = (bf16[256,512]{1,0:T(8,128)(2,1)S(1)}, bf16[256,512]{1,0:T(8,128)(2,1)S(1)}, u32[]{:S(2)}, u32[]{:S(2)}) collective-permute-start(bf16[256,512]{1,0:T(8,128)(2,1)S(1)} %constant_dynamic-slice_fusion.6), channel_id=1, source_target_pairs={{0,3},{3,0},{1,2},{2,1},{4,7},{7,4},{5,6},{6,5},{8,11},{11,8},{9,1... | collective-permute-start | bytes 786440 | tf_op jit(solution)/shard_map/ppermute | solution.py:341
  95.0 7.1 %collective-permute-start.5 = (bf16[256,512]{1,0:T(8,128)(2,1)S(1)}, bf16[256,512]{1,0:T(8,128)(2,1)S(1)}, u32[]{:S(2)}, u32[]{:S(2)}) collective-permute-start(bf16[256,512]{1,0:T(8,128)(2,1)S(1)} %constant_dynamic-slice_fusion.5), channel_id=1, source_target_pairs={{0,1},{1,0},{2,3},{3,2},{4,5},{5,4},{6,7},{7,6},{8,9},{9,8},{10,11... | collective-permute-start | bytes 786440 | tf_op jit(solution)/shard_map/ppermute | solution.py:341
  96.6 7.7 %collective-permute-start.10 = (bf16[256,512]{1,0:T(8,128)(2,1)S(1)}, bf16[256,512]{1,0:T(8,128)(2,1)S(1)}, u32[]{:S(2)}, u32[]{:S(2)}) collective-permute-start(bf16[256,512]{1,0:T(8,128)(2,1)S(1)} %constant_dynamic-slice_fusion.3), channel_id=1, source_target_pairs={{0,96},{96,0},{32,64},{64,32},{1,97},{97,1},{33,65},{65,33},{2,98}... | collective-permute-start | bytes 786440 | tf_op jit(solution)/shard_map/ppermute | solution.py:341
  99.3 6.2 %collective-permute-start.13 = (bf16[256,512]{1,0:T(8,128)(2,1)S(1)}, bf16[256,512]{1,0:T(8,128)(2,1)S(1)}, u32[]{:S(2)}, u32[]{:S(2)}) collective-permute-start(bf16[256,512]{1,0:T(8,128)(2,1)S(1)} %constant_dynamic-slice_fusion.2), channel_id=1, source_target_pairs={{0,32},{32,0},{64,96},{96,64},{1,33},{33,1},{65,97},{97,65},{2,34}... | collective-permute-start | bytes 786440 | tf_op jit(solution)/shard_map/ppermute | solution.py:341
  102.1 9.0 %collective-permute-start.6 = (bf16[2,128,512]{2,1,0:T(8,128)(2,1)S(1)}, bf16[2,128,512]{2,1,0:T(8,128)(2,1)S(1)}, u32[]{:S(2)}, u32[]{:S(2)}) collective-permute-start(bf16[2,128,512]{2,1,0:T(8,128)(2,1)S(1)} %fusion.7), channel_id=1, source_target_pairs={{0,32},{32,0},{64,96},{96,64},{1,33},{33,1},{65,97},{97,65},{2,34}... | collective-permute-start | bytes 786440 | tf_op jit(solution)/shard_map/ppermute | solution.py:341
  105.6 7.6 %collective-permute-start.14 = (bf16[2,128,512]{2,1,0:T(8,128)(2,1)S(1)}, bf16[2,128,512]{2,1,0:T(8,128)(2,1)S(1)}, u32[]{:S(2)}, u32[]{:S(2)}) collective-permute-start(bf16[2,128,512]{2,1,0:T(8,128)(2,1)S(1)} %fusion.5), channel_id=1, source_target_pairs={{0,1},{1,0},{2,3},{3,2},{4,5},{5,4},{6,7},{7,6},{8,9},{9,8},{10,11... | collective-permute-start | bytes 786440 | tf_op jit(solution)/shard_map/ppermute | solution.py:341
  111.3 5.1 %collective-permute-start.7 = (bf16[2,64,512]{2,1,0:T(8,128)(2,1)S(1)}, bf16[2,64,512]{2,1,0:T(8,128)(2,1)S(1)}, u32[]{:S(2)}, u32[]{:S(2)}) collective-permute-start(bf16[2,64,512]{2,1,0:T(8,128)(2,1)S(1)} %constant_dynamic-slice_fusion.4), channel_id=1, source_target_pairs={{0,96},{96,0},{32,64},{64,32},{1,97},{97,1},{33,65},{65,33},{2,98}... | collective-permute-start | bytes 393224 | tf_op jit(solution)/shard_map/ppermute | solution.py:341
  113.4 5.4 %collective-permute-start.15 = (bf16[2,64,512]{2,1,0:T(8,128)(2,1)S(1)}, bf16[2,64,512]{2,1,0:T(8,128)(2,1)S(1)}, u32[]{:S(2)}, u32[]{:S(2)}) collective-permute-start(bf16[2,64,512]{2,1,0:T(8,128)(2,1)S(1)} %constant_dynamic-slice_fusion.1), channel_id=1, source_target_pairs={{0,3},{3,0},{1,2},{2,1},{4,7},{7,4},{5,6},{6,5},{8,11},{11,8},{9,1... | collective-permute-start | bytes 393224 | tf_op jit(solution)/shard_map/ppermute | solution.py:341
  118.9 4.0 %collective-permute-start.16 = (bf16[4,32,512]{2,1,0:T(8,128)(2,1)S(1)}, bf16[4,32,512]{2,1,0:T(8,128)(2,1)S(1)}, u32[]{:S(2)}, u32[]{:S(2)}) collective-permute-start(bf16[4,32,512]{2,1,0:T(8,128)(2,1)S(1)} %fusion.9), channel_id=1, source_target_pairs={{0,8},{8,0},{16,24},{24,16},{1,9},{9,1},{17,25},{25,17},{2,10},{10... | collective-permute-start | bytes 393224 | tf_op jit(solution)/shard_map/ppermute | solution.py:341
  122.9 4.4 %collective-permute-start.17 = (bf16[4,16,512]{2,1,0:T(8,128)(2,1)S(1)}, bf16[4,16,512]{2,1,0:T(8,128)(2,1)S(1)}, u32[]{:S(2)}, u32[]{:S(2)}) collective-permute-start(bf16[4,16,512]{2,1,0:T(8,128)(2,1)S(1)} %constant_dynamic-slice_fusion), channel_id=1, source_target_pairs={{0,24},{24,0},{8,16},{16,8},{1,25},{25,1},{9,17},{17,9},{2,26},{26... | collective-permute-start | bytes 196616 | tf_op jit(solution)/shard_map/ppermute | solution.py:341
  142.0 28.0 %all-to-all-start.2 = ((bf16[32,64,128]{2,1,0:T(8,128)(2,1)}), bf16[32,64,128]{2,1,0:T(8,128)(2,1)S(1)}, u32[]{:S(2)}, u32[]{:S(2)}) async-start(bf16[32,64,128]{2,1,0:T(8,128)(2,1)} %bitcast.56), calls=%async_computation.2 | async-start | bytes 1048576 | tf_op jit(solution)/shard_map/all_to_all | solution.py:156
  170.0 10.1 %copy-start.8 = (bf16[512,2048]{1,0:T(8,128)(2,1)S(1)}, bf16[512,2048]{1,0:T(8,128)(2,1)}, u32[]{:S(2)}) copy-start(bf16[512,2048]{1,0:T(8,128)(2,1)} %get-tuple-element.32) | copy-start | bytes 6291460
  170.0 0.8 copy-start.5
  172.6 19.1 %all-to-all-start.3 = ((bf16[32,64,128]{2,1,0:T(8,128)(2,1)}), bf16[32,64,128]{2,1,0:T(8,128)(2,1)S(1)}, u32[]{:S(2)}, u32[]{:S(2)}) async-start(bf16[32,64,128]{2,1,0:T(8,128)(2,1)} %shard_map.107), calls=%async_computation.3 | async-start | bytes 1048576 | tf_op jit(solution)/shard_map/all_to_all | solution.py:158
  191.7 0.8 copy-start.7
Sparse Core Ops, SparseCore 0:
  11.1 75.7 all-gather.1

commit v2 on v1

--- a/solution.py
+++ b/solution.py
@@ -74,6 +74,11 @@
     )
 
 
+COLORS = 4
+WIDTH = FEATURES // COLORS
+SLAB = 16
+PLACES = 64
+CYCLES = (((0, 1), (1, 0), (2, 3), (3, 2)), ((0, 3), (3, 0), (1, 2), (2, 1)))
 PAIR_SPEC = spec((BLOCK, PAIR), lambda i: (0, i))
 STATE_SPEC = spec((GROUP, HEAD_DIM, HEAD_DIM), lambda i: (i, 0, 0))
 WIDE_LOW = jax.ShapeDtypeStruct((BLOCK, FEATURES), BF16)
@@ -210,8 +215,13 @@
 CHUNKS = FEATURES // CHUNK
 
 
+CHUNK = 2 * HEAD_DIM
+CHUNKS = FEATURES // CHUNK
+
+
 def norm_back_body(
-    grad, weight, normed, inverse, gain, feat_query, grad_att, state, hats, norms, feats, products
+    place, grad, w0, w1, w2, w3, o0, o1, o2, o3, normed, inverse, gain, feat_query,
+    grad_att, state, weight, hats, norms, feats, products
 ):
     step = pl.program_id(0)
 
@@ -219,6 +229,13 @@
     def _():
         products[...] = jnp.zeros_like(products)
 
+    part = HEAD_DIM // 2
+    for i in range(2):
+        rows = slice(i * part, (i + 1) * part)
+        for side, pieces in ((place[0], (w0, w1, w2, w3)), (place[1], (o0, o1, o2, o3))):
+            at = pl.multiple_of(i * HEAD_DIM + side * part, part)
+            for c, piece in enumerate(pieces):
+                weight[pl.ds(at, part), c * WIDTH : (c + 1) * WIDTH] = piece[rows]
     hat = dot_nt(grad[...], weight[...]) * gain[...]
     product = hat * normed[...]
     products[...] += product[:, :HEAD_DIM] + product[:, HEAD_DIM:]
@@ -237,31 +254,42 @@
             state[i] = dot_tn(feats[c, :, at], low).astype(BF16)
 
 
-def norm_back(grad_result, weight, normed, inverse, gain, feat_query):
-    part = spec((BLOCK, CHUNK), lambda i: (0, i))
-    whole = spec((BLOCK, FEATURES), lambda i: (0, 0))
-    return call(
+def norm_back(place, grad_result, pieces, normed, inverse, gain, feat_query):
+    part = spec((BLOCK, CHUNK), lambda i, p: (0, i))
+    whole = spec((BLOCK, FEATURES), lambda i, p: (0, 0))
+    piece = spec((CHUNK // 2, WIDTH), lambda i, p: (i, 0))
+    return pl.pallas_call(
         norm_back_body,
-        (CHUNKS,),
-        [
-            whole,
-            spec((CHUNK, FEATURES), lambda i: (i, 0)),
-            part,
-            spec((BLOCK, HEAD_DIM), lambda i: (0, 0)),
-            spec((1, CHUNK), lambda i: (0, i)),
-            part,
-        ],
-        [whole, ALL_STATES],
-        [WIDE_LOW, STATE_LOW],
-        5 << 30,
-        18 * MIB,
-        scratch=[
-            pltpu.VMEM((CHUNKS, BLOCK, CHUNK), F32),
-            pltpu.VMEM((CHUNKS, BLOCK, CHUNK), F32),
-            pltpu.VMEM((CHUNKS, BLOCK, CHUNK), BF16),
-            pltpu.VMEM((BLOCK, HEAD_DIM), F32),
-        ],
-    )(grad_result, weight, normed, inverse, gain, feat_query)
+        grid_spec=pltpu.PrefetchScalarGridSpec(
+            num_scalar_prefetch=1,
+            grid=(CHUNKS,),
+            in_specs=[whole]
+            + [piece] * 8
+            + [
+                part,
+                spec((BLOCK, HEAD_DIM), lambda i, p: (0, 0)),
+                spec((1, CHUNK), lambda i, p: (0, i)),
+                part,
+            ],
+            out_specs=[
+                whole,
+                spec((HEADS, HEAD_DIM, HEAD_DIM), lambda i, p: (0, 0, 0)),
+                spec((CHUNK, FEATURES), lambda i, p: (i, 0)),
+            ],
+            scratch_shapes=[
+                pltpu.VMEM((CHUNKS, BLOCK, CHUNK), F32),
+                pltpu.VMEM((CHUNKS, BLOCK, CHUNK), F32),
+                pltpu.VMEM((CHUNKS, BLOCK, CHUNK), BF16),
+                pltpu.VMEM((BLOCK, HEAD_DIM), F32),
+            ],
+        ),
+        out_shape=[WIDE_LOW, STATE_LOW, jax.ShapeDtypeStruct((FEATURES, FEATURES), BF16)],
+        compiler_params=pltpu.CompilerParams(vmem_limit_bytes=60 * MIB),
+        cost_estimate=pl.CostEstimate(
+            flops=5 << 30, bytes_accessed=26 * MIB, transcendentals=0
+        ),
+        name="norm_back",
+    )(place, grad_result, *(p[0] for p in pieces), *(p[1] for p in pieces), normed, inverse, gain, feat_query)
 
 
 def back_body(query, feat_query, feat_key, value, grad, state, grad_query, part_key, part_value):
@@ -319,13 +347,6 @@
     )(key, feat_key, value, part_key, part_value, later)
 
 
-COLORS = 4
-WIDTH = FEATURES // COLORS
-SLAB = 16
-PLACES = 64
-CYCLES = (((0, 1), (1, 0), (2, 3), (3, 2)), ((0, 3), (3, 0), (1, 2), (2, 1)))
-
-
 def on_ring(low, high):
     return low + high * (3 - 2 * low)
 
@@ -345,24 +366,72 @@
     out[...] = dot_tn(left[0], right[...]).astype(BF16)
 
 
+def slab_at(color, side, s):
+    other, rest, z = s // 16, (s // 4) % 4, s % 4
+    z = on_ring(z // 2, z % 2)
+    far = on_ring(rest // 2, rest % 2)
+    near = on_ring(side, other) if color % 2 == 0 else on_ring(other, side)
+    y, x = (far, near) if color < 2 else (near, far)
+    return pl.multiple_of((y * 16 + z * 4 + x) * SLAB, SLAB)
+
+
 def first_body(color, place, left, right, got, kept, sent, acc):
     acc[...] = (dot_tn(left[0], right[...]) + got[...].astype(F32)).astype(BF16)
     bit = place[2 + color]
     for side, out in ((bit, kept), (1 - bit, sent)):
         for s in range(PLACES // 2):
-            other, rest, z = s // 16, (s // 4) % 4, s % 4
-            z = on_ring(z // 2, z % 2)
-            far = on_ring(rest // 2, rest % 2)
-            near = on_ring(side, other) if color % 2 == 0 else on_ring(other, side)
-            y, x = (far, near) if color < 2 else (near, far)
-            at = pl.multiple_of((y * 16 + z * 4 + x) * SLAB, SLAB)
+            at = slab_at(color, side, s)
             out[s * SLAB : (s + 1) * SLAB] = acc[pl.ds(at, SLAB)]
 
 
-def gradient_rows(split, grad_result):
-    core = lax.axis_index("seq_2")
-    xs, ys, zs = my_bits("dp"), my_bits("seq_0"), my_bits("seq_1")
-    place = jnp.stack([core, 1 - core, xs[0], xs[1], ys[0], ys[1]]).astype(jnp.int32)
+def last_body(color, place, mine, got, out):
+    bit = place[2 + color]
+    for side, part in ((bit, mine), (1 - bit, got)):
+        for s in range(PLACES // 2):
+            at = slab_at(color, side, s)
+            out[pl.ds(at, SLAB)] = part[s * SLAB : (s + 1) * SLAB]
+
+
+def widened(mine, got, bit):
+    low = jnp.where(bit == 0, mine, got)
+    high = jnp.where(bit == 0, got, mine)
+    return jnp.concatenate([low, high], axis=0)
+
+
+def own_rows(rows, place, xs, ys, zs):
+    for which in (1, 0):
+        rows = widened(rows, hop(rows, "seq_1", which), zs[which])
+    sides = []
+    for near, (bits, axis) in enumerate(((ys, "seq_0"), (xs, "dp"))):
+        part = rows[:, near * FEATURES // 2 : (near + 1) * FEATURES // 2]
+        for which in (1, 0):
+            part = widened(part, hop(part, axis, which), bits[which])
+        sides += [part[:, :WIDTH], part[:, WIDTH:]]
+    order = ((xs, "dp"), (ys, "seq_0"))
+    for color in range(COLORS):
+        bits, axis = order[color // 2]
+        which = 1 - color % 2
+        sides[color] = widened(sides[color], hop(sides[color], axis, which), bits[which])
+    half = FEATURES // 2
+    part = pl.BlockSpec((half // 2, WIDTH), lambda i, p: (0, 0))
+    whole = pl.BlockSpec((half, WIDTH), lambda i, p: (0, 0))
+    pieces = []
+    for color in range(COLORS):
+        axis = order[color // 2][1]
+        own = pl.pallas_call(
+            lambda *refs, color=color: last_body(color, *refs),
+            grid_spec=pltpu.PrefetchScalarGridSpec(
+                num_scalar_prefetch=1, grid=(1,), in_specs=[part, part], out_specs=whole
+            ),
+            out_shape=jax.ShapeDtypeStruct((half, WIDTH), BF16),
+            cost_estimate=pl.CostEstimate(flops=1 << 26, bytes_accessed=2 * MIB, transcendentals=0),
+            name="last_rows",
+        )(place, sides[color], hop(sides[color], axis, color % 2))
+        pieces.append((own, lax.ppermute(own, "seq_2", [(0, 1), (1, 0)])))
+    return pieces
+
+
+def gradient_rows(split, grad_result, place, xs, ys, zs):
     half = FEATURES // 2
 
     def grid_spec(which, color, more, outs):
@@ -441,14 +510,17 @@
 def layer(query_input, key_input, value_input, grad_output, out_weight, norm_gain):
     query, key, value, grad_result = query_input[0], key_input[0], value_input[0], grad_output[0]
     gain = norm_gain.reshape(1, FEATURES)
-    full_weight = lax.all_gather(out_weight, SEQ_DP, axis=0, tiled=True)
+    core = lax.axis_index("seq_2")
+    xs, ys, zs = my_bits("dp"), my_bits("seq_0"), my_bits("seq_1")
+    place = jnp.stack([core, 1 - core, xs[0], xs[1], ys[0], ys[1]]).astype(jnp.int32)
+    pieces = own_rows(out_weight, place, xs, ys, zs)
     feat_key, block_kv = block_states(key, value)
     prefix = scanned(block_kv, False)
     feat_query, inside = inside_blocks(query, feat_key, value)
     mixed, split, normed, inverse = attend(inside, feat_query, prefix, gain)
-    grad_weight = gradient_rows(split, grad_result)
-    grad_att, block_grad = norm_back(
-        grad_result, full_weight, normed, inverse, gain, feat_query
+    grad_weight = gradient_rows(split, grad_result, place, xs, ys, zs)
+    grad_att, block_grad, full_weight = norm_back(
+        place, grad_result, pieces, normed, inverse, gain, feat_query
     )
     later = scanned(block_grad, True)
     result = dot_nn(mixed, full_weight).astype(BF16)

time: 209 us -> 243 us (1.16)
  the two profiles are of different devices: /device:TPU:1 before, /device:TPU:2 now
where the time goes in v2:
time: 243 us; the launch traced here: 241 us
  Pallas kernels  101 us (42%)
  starting transfers between devices  72.6 us (30%)
  waiting for transfers between devices  38.8 us (16%)
  other arithmetic  10.9 us (4%)
  matrix products  9.02 us (4%)
  local copies, waits for them, and re-layouts  6.67 us (3%)
    ppermute x28, starting transfers between devices, hop(): return lax.ppermute(sent, axis, CYCLES[which])  42.2 us
    ppermute x28, waiting for transfers between devices, hop(): return lax.ppermute(sent, axis, CYCLES[which])  38.8 us
    pallas_call x1, Pallas kernels, norm_back(): pl.pallas_call(norm_back_body, grid_spec=pltpu.PrefetchScalarGridSpec(num...  17.9 us
    pallas_call x1, Pallas kernels, back_inside(): call(back_body, (HEADS // GROUP,), [PAIR_SPEC] * 5 + [STATE_SPEC], [PAIR_...  17.7 us
    all_to_all x2, starting transfers between devices, scanned(): pieces = lax.all_to_all(pieces, SEQ, 0, 0, tiled=True)  16.1 us
    all_to_all x2, starting transfers between devices, scanned(): sums = lax.all_to_all(sums, SEQ, 0, 0, tiled=True)  12.6 us
    pallas_call x4, Pallas kernels, gradient_rows(): pl.pallas_call(lambda *refs, color=color: first_body(color, *refs), grid_...  12.5 us
    pallas_call x4, Pallas kernels, own_rows(): pl.pallas_call(lambda *refs, color=color: last_body(color, *refs), grid_s...  11.9 us
  transfers between devices with their start and end apart: 40, of which 9 were waited for; matrix products, arithmetic and copies ran while one was open for 8% of the time, Pallas kernels for 39%

profile of v2, /device:TPU:2, one launch (start us, length us, event | category | flops | bytes accessed | tf_op | source)
XLA Modules:
  0.0 240.7 jit_solution(8652393071293293385)
XLA Ops:
  0.6 4.1 %collective-permute-start = (bf16[16,2048]{1,0:T(8,128)(2,1)}, bf16[16,2048]{1,0:T(8,128)(2,1)S(1)}, u32[]{:S(2)}, u32[]{:S(2)}) collective-permute-start(bf16[16,2048]{1,0:T(8,128)(2,1)} %param.10), channel_id=1, source_target_pairs={{0,24},{24,0},{8,16},{16,8},{1,25},{25,1},{9,17},{17,9},{2,26},{26... | collective-permute-start | bytes 196616 | tf_op jit(solution)/shard_map/ppermute | solution.py:362
  4.7 2.5 %collective-permute-done = bf16[16,2048]{1,0:T(8,128)(2,1)S(1)} collective-permute-done((bf16[16,2048]{1,0:T(8,128)(2,1)}, bf16[16,2048]{1,0:T(8,128)(2,1)S(1)}, u32[]{:S(2)}, u32[]{:S(2)}) %collective-permute-start) | collective-permute-done | bytes 65568 | tf_op jit(solution)/shard_map/ppermute | solution.py:362
  8.2 4.7 %shard_map.101 = (bf16[512,2048]{1,0:T(8,128)(2,1)}, bf16[16,128,128]{2,1,0:T(8,128)(2,1)}) custom-call(bf16[512,2048]{1,0:T(8,128)(2,1)} %bitcast.47, bf16[512,2048]{1,0:T(8,128)(2,1)} %bitcast.49), custom_call_target="tpu_custom_call" | custom-call | flops 536870912 | bytes 7340032 | tf_op jit(solution)/shard_map/pallas_call | solution.py:98
  12.9 9.0 %all-to-all-start = ((bf16[32,64,128]{2,1,0:T(8,128)(2,1)}), bf16[32,64,128]{2,1,0:T(8,128)(2,1)S(1)}, u32[]{:S(2)}, u32[]{:S(2)}) async-start(bf16[32,64,128]{2,1,0:T(8,128)(2,1)} %bitcast.57), calls=%async_computation | async-start | bytes 1048576 | tf_op jit(solution)/shard_map/all_to_all | solution.py:161
  23.6 7.9 %shard_map.102 = (bf16[512,2048]{1,0:T(8,128)(2,1)}, f32[512,2048]{1,0:T(8,128)}) custom-call(bf16[512,2048]{1,0:T(8,128)(2,1)} %bitcast.60, bf16[512,2048]{1,0:T(8,128)(2,1)} %get-tuple-element.29.feat_key, bf16[512,2048]{1,0:T(8,128)(2,1)} %bitcast.50), custom_call_target="tpu_custom_call" | custom-call | flops 4294967296 | bytes 12582912 | tf_op jit(solution)/shard_map/pallas_call | solution.py:123
  31.5 3.1 %collective-permute-start.2 = (bf16[64,1024]{1,0:T(8,128)(2,1)S(1)}, bf16[64,1024]{1,0:T(8,128)(2,1)S(1)}, u32[]{:S(2)}, u32[]{:S(2)}) collective-permute-start(bf16[64,1024]{1,0:T(8,128)(2,1)S(1)} %get-tuple-element.72), channel_id=1, source_target_pairs={{0,96},{96,0},{32,64},{64,32},{1,97},{97,1},{33,65},{65,33},{2,98}... | collective-permute-start | bytes 393224 | tf_op jit(solution)/shard_map/ppermute | solution.py:362
  34.7 1.9 collective-permute-start.9
  36.6 1.6 collective-permute-done.2
  39.5 1.8 shard_map.103
  41.3 8.0 %all-to-all-start.1 = ((bf16[32,64,128]{2,1,0:T(8,128)(2,1)}), bf16[32,64,128]{2,1,0:T(8,128)(2,1)S(1)}, u32[]{:S(2)}, u32[]{:S(2)}) async-start(bf16[32,64,128]{2,1,0:T(8,128)(2,1)} %shard_map.103), calls=%async_computation.1 | async-start | bytes 1048576 | tf_op jit(solution)/shard_map/all_to_all | solution.py:163
  49.5 1.9 collective-permute-start.12
  51.4 2.1 collective-permute-start.10
  54.4 1.8 collective-permute-start.6
  56.2 7.3 %collective-permute-done.12 = bf16[256,512]{1,0:T(8,128)(2,1)S(1)} collective-permute-done((bf16[256,512]{1,0:T(8,128)(2,1)S(1)}, bf16[256,512]{1,0:T(8,128)(2,1)S(1)}, u32[]{:S(2)}, u32[]{:S(2)}) %collective-permute-start.12) | collective-permute-done | bytes 262176 | tf_op jit(solution)/shard_map/ppermute | solution.py:362
  64.3 2.1 collective-permute-start.13
  68.8 7.7 %shard_map.104 = (bf16[512,2048]{1,0:T(8,128)(2,1)}, bf16[2,512,1024]{2,1,0:T(8,128)(2,1)}, f32[512,2048]{1,0:T(8,128)}, f32[512,128]{1,0:T(8,128)}) custom-call(f32[512,2048]{1,0:T(8,128)} %get-tuple-element.30.inside, bf16[512,2048]{1,0:T(8,128)(2,1)} %get-tuple-element.31.feat_query, bf16[16,128,128]{2,1,0:T(8,128)(2,1)} %bitcast.53, f32[1,2048]{1,0:T(1,128)} %bitcast.58), custom_call_target="tpu_custom_call" | custom-call | flops 536870912 | bytes 15728640 | tf_op jit(solution)/shard_map/pallas_call | solution.py:198
  78.1 2.3 pair_product.7
  80.3 2.3 pair_product.6
  82.6 2.3 pair_product.5
  89.3 1.7 collective-permute-start.5
  91.1 2.3 pair_product.4
  93.3 8.8 %collective-permute-done.7.refs_2_ = bf16[512,512]{1,0:T(8,128)(2,1)S(1)} collective-permute-done((bf16[512,512]{1,0:T(8,128)(2,1)S(1)}, bf16[512,512]{1,0:T(8,128)(2,1)S(1)}, u32[]{:S(2)}, u32[]{:S(2)}) %collective-permute-start.7) | collective-permute-done | bytes 524320 | tf_op jit(solution)/shard_map/ppermute | solution.py:362
  102.9 2.9 %last_rows.7.w3 = bf16[1024,512]{1,0:T(8,128)(2,1)} custom-call(s32[6]{0:T(128)} %copy-done.7, bf16[512,512]{1,0:T(8,128)(2,1)} %pad_maximum_fusion.3.refs_1_, bf16[512,512]{1,0:T(8,128)(2,1)} %collective-permute-done.13.refs_2_), custom_call_target="tpu_custom_call" | custom-call | flops 67108864 | bytes 2097152 | tf_op jit(solution)/shard_map/last_rows/pallas_call | solution.py:421
  105.9 2.9 %last_rows.6.w2 = bf16[1024,512]{1,0:T(8,128)(2,1)} custom-call(s32[6]{0:T(128)} %copy-done.7, bf16[512,512]{1,0:T(8,128)(2,1)} %pad_maximum_fusion.2.refs_1_, bf16[512,512]{1,0:T(8,128)(2,1)} %collective-permute-done.11.refs_2_), custom_call_target="tpu_custom_call" | custom-call | flops 67108864 | bytes 2097152 | tf_op jit(solution)/shard_map/last_rows/pallas_call | solution.py:421
  108.8 3.1 %last_rows.5.w1 = bf16[1024,512]{1,0:T(8,128)(2,1)} custom-call(s32[6]{0:T(128)} %copy-done.7, bf16[512,512]{1,0:T(8,128)(2,1)} %copy-done.9, bf16[512,512]{1,0:T(8,128)(2,1)} %copy-done.13), custom_call_target="tpu_custom_call" | custom-call | flops 67108864 | bytes 2097152 | tf_op jit(solution)/shard_map/last_rows/pallas_call | solution.py:421
  112.9 2.9 %last_rows.4.w0 = bf16[1024,512]{1,0:T(8,128)(2,1)} custom-call(s32[6]{0:T(128)} %copy-done.7, bf16[512,512]{1,0:T(8,128)(2,1)} %pad_maximum_fusion.refs_1_, bf16[512,512]{1,0:T(8,128)(2,1)} %collective-permute-done.5.refs_2_), custom_call_target="tpu_custom_call" | custom-call | flops 67108864 | bytes 2097152 | tf_op jit(solution)/shard_map/last_rows/pallas_call | solution.py:421
  117.6 2.2 first_halves.7
  119.7 3.4 %first_halves.6 = (bf16[512,512]{1,0:T(8,128)(2,1)S(1)}, bf16[512,512]{1,0:T(8,128)(2,1)}) custom-call(s32[6]{0:T(128)S(1)} %copy-done.8, bf16[2,512,1024]{2,1,0:T(8,128)(2,1)S(1)} %copy-done.2, bf16[512,2048]{1,0:T(8,128)(2,1)S(1)} %bitcast.44, bf16[1024,512]{1,0:T(8,128)(2,1)} %collective-permute-done.26.refs_3_), custom_call_target="tpu_custom_call" | custom-call | flops 1073741824 | bytes 4194304 | tf_op jit(solution)/shard_map/first_halves/pallas_call | solution.py:469
  123.2 3.4 %first_halves.5 = (bf16[512,512]{1,0:T(8,128)(2,1)S(1)}, bf16[512,512]{1,0:T(8,128)(2,1)}) custom-call(s32[6]{0:T(128)S(1)} %copy-done.8, bf16[2,512,1024]{2,1,0:T(8,128)(2,1)S(1)} %copy-done.2, bf16[512,2048]{1,0:T(8,128)(2,1)S(1)} %bitcast.45, bf16[1024,512]{1,0:T(8,128)(2,1)} %collective-permute-done.21.refs_3_), custom_call_target="tpu_custom_call" | custom-call | flops 1073741824 | bytes 4194304 | tf_op jit(solution)/shard_map/first_halves/pallas_call | solution.py:469
  127.2 3.4 %first_halves.4 = (bf16[512,512]{1,0:T(8,128)(2,1)S(1)}, bf16[512,512]{1,0:T(8,128)(2,1)}) custom-call(s32[6]{0:T(128)S(1)} %copy-done.8, bf16[2,512,1024]{2,1,0:T(8,128)(2,1)S(1)} %copy-done.2, bf16[512,2048]{1,0:T(8,128)(2,1)S(1)} %bitcast.46, bf16[1024,512]{1,0:T(8,128)(2,1)} %collective-permute-done.18.refs_3_), custom_call_target="tpu_custom_call" | custom-call | flops 1073741824 | bytes 4194304 | tf_op jit(solution)/shard_map/first_halves/pallas_call | solution.py:469
  132.5 3.0 %collective-permute-start.19 = (bf16[512,512]{1,0:T(8,128)(2,1)}, bf16[512,512]{1,0:T(8,128)(2,1)S(1)}, u32[]{:S(2)}, u32[]{:S(2)}) collective-permute-start(bf16[512,512]{1,0:T(8,128)(2,1)} %get-tuple-element.46), channel_id=1, source_target_pairs={{0,1},{1,0},{2,3},{3,2},{4,5},{5,4},{6,7},{7,6},{8,9},{9,8},{10,11... | collective-permute-start | bytes 1572872 | tf_op jit(solution)/shard_map/ppermute | solution.py:362
  135.5 17.9 %norm_back.1 = (bf16[512,2048]{1,0:T(8,128)(2,1)}, bf16[16,128,128]{2,1,0:T(8,128)(2,1)}, bf16[2048,2048]{1,0:T(8,128)(2,1)}) custom-call(s32[6]{0:T(128)} %copy-done.7, bf16[512,2048]{1,0:T(8,128)(2,1)} %bitcast.38, bf16[1024,512]{1,0:T(8,128)(2,1)} %last_rows.4.w0, bf16[1024,512]{1,0:T(8,128)(2,1)} %last_rows.5.w1, bf16[1024,512]{1,0:T(8,128)(2,1)} %last_rows.6.w2, ...), custom_call_target="tpu_custom_call" | custom-call | flops 5368709120 | bytes 27262976 | tf_op jit(solution)/shard_map/norm_back/pallas_call | solution.py:261
  153.5 7.1 %all-to-all-start.2 = ((bf16[32,64,128]{2,1,0:T(8,128)(2,1)}), bf16[32,64,128]{2,1,0:T(8,128)(2,1)}, u32[]{:S(2)}, u32[]{:S(2)}) async-start(bf16[32,64,128]{2,1,0:T(8,128)(2,1)} %bitcast.56), calls=%async_computation.2 | async-start | bytes 1048576 | tf_op jit(solution)/shard_map/all_to_all | solution.py:161
  161.8 1.8 collective-permute-start.31
  164.8 2.2 collective-permute-start.28
  167.4 2.2 collective-permute-start.20
  169.7 4.9 %collective-permute-done.31 = bf16[256,512]{1,0:T(8,128)(2,1)S(1)} collective-permute-done((bf16[256,512]{1,0:T(8,128)(2,1)S(1)}, bf16[256,512]{1,0:T(8,128)(2,1)S(1)}, u32[]{:S(2)}, u32[]{:S(2)}) %collective-permute-start.31) | collective-permute-done | bytes 262176 | tf_op jit(solution)/shard_map/ppermute | solution.py:362
  176.5 7.3 %collective-permute-done.32 = bf16[2,128,512]{2,1,0:T(8,128)(2,1)S(1)} collective-permute-done((bf16[2,128,512]{2,1,0:T(8,128)(2,1)S(1)}, bf16[2,128,512]{2,1,0:T(8,128)(2,1)S(1)}, u32[]{:S(2)}, u32[]{:S(2)}) %collective-permute-start.32) | collective-permute-done | bytes 262176 | tf_op jit(solution)/shard_map/ppermute | solution.py:362
  183.9 2.2 collective-permute-start.33
  187.2 1.9 collective-permute-done.33
  189.1 3.4 %collective-permute-done.25 = bf16[2,64,512]{2,1,0:T(8,128)(2,1)S(1)} collective-permute-done((bf16[2,64,512]{2,1,0:T(8,128)(2,1)S(1)}, bf16[2,64,512]{2,1,0:T(8,128)(2,1)S(1)}, u32[]{:S(2)}, u32[]{:S(2)}) %collective-permute-start.25) | collective-permute-done | bytes 131104 | tf_op jit(solution)/shard_map/ppermute | solution.py:362
  192.5 1.8 collective-permute-start.34
  194.4 17.7 %shard_map.105 = (bf16[512,2048]{1,0:T(8,128)(2,1)}, f32[512,2048]{1,0:T(8,128)}, f32[512,2048]{1,0:T(8,128)}) custom-call(bf16[512,2048]{1,0:T(8,128)(2,1)} %bitcast.61, bf16[512,2048]{1,0:T(8,128)(2,1)} %get-tuple-element.31.feat_query, bf16[512,2048]{1,0:T(8,128)(2,1)} %get-tuple-element.29.feat_key, bf16[512,2048]{1,0:T(8,128)(2,1)} %bitcast.51, ...), custom_call_target="tpu_custom_call" | custom-call | flops 12884901888 | bytes 20971520 | tf_op jit(solution)/shard_map/pallas_call | solution.py:319
  212.1 1.9 shard_map.106
  214.1 4.6 %all-to-all-start.3 = ((bf16[32,64,128]{2,1,0:T(8,128)(2,1)}), bf16[32,64,128]{2,1,0:T(8,128)(2,1)S(1)}, u32[]{:S(2)}, u32[]{:S(2)}) async-start(bf16[32,64,128]{2,1,0:T(8,128)(2,1)} %shard_map.106), calls=%async_computation.3 | async-start | bytes 1048576 | tf_op jit(solution)/shard_map/all_to_all | solution.py:163
  218.7 3.1 %collective-permute-start.35 = (bf16[4,16,512]{2,1,0:T(8,128)(2,1)S(1)}, bf16[4,16,512]{2,1,0:T(8,128)(2,1)S(1)}, u32[]{:S(2)}, u32[]{:S(2)}) collective-permute-start(bf16[4,16,512]{2,1,0:T(8,128)(2,1)S(1)} %constant_dynamic-slice_fusion), channel_id=1, source_target_pairs={{0,24},{24,0},{8,16},{16,8},{1,25},{25,1},{9,17},{17,9},{2,26},{26... | collective-permute-start | bytes 196616 | tf_op jit(solution)/shard_map/ppermute | solution.py:362
  221.8 9.0 %fusion = bf16[1,512,2048]{2,1,0:T(8,128)(2,1)} fusion(bf16[512,2048]{1,0:T(8,128)(2,1)S(1)} %copy-done.14, bf16[2048,2048]{1,0:T(8,128)(2,1)} %get-tuple-element.36), kind=kOutput, calls=%fused_computation.1 | convolution fusion | flops 4296015872 | bytes 12582912 | tf_op jit(solution)/shard_map/dot_general | solution.py:32
  231.7 8.3 %shard_map.107 = (bf16[512,2048]{1,0:T(8,128)(2,1)}, bf16[512,2048]{1,0:T(8,128)(2,1)}) custom-call(bf16[512,2048]{1,0:T(8,128)(2,1)} %bitcast.48, bf16[512,2048]{1,0:T(8,128)(2,1)} %get-tuple-element.29.feat_key, bf16[512,2048]{1,0:T(8,128)(2,1)} %bitcast.52, f32[512,2048]{1,0:T(8,128)} %get-tuple-element.39.part_key, ...), custom_call_target="tpu_custom_call" | custom-call | flops 1073741824 | bytes 18874368 | tf_op jit(solution)/shard_map/pallas_call | solution.py:339
  (130 shorter events, 27.9 us)
Async XLA Ops:
  0.6 6.6 %collective-permute-start = (bf16[16,2048]{1,0:T(8,128)(2,1)}, bf16[16,2048]{1,0:T(8,128)(2,1)S(1)}, u32[]{:S(2)}, u32[]{:S(2)}) collective-permute-start(bf16[16,2048]{1,0:T(8,128)(2,1)} %param.10), channel_id=1, source_target_pairs={{0,24},{24,0},{8,16},{16,8},{1,25},{25,1},{9,17},{17,9},{2,26},{26... | collective-permute-start | bytes 196616 | tf_op jit(solution)/shard_map/ppermute | solution.py:362
  8.1 13.8 %collective-permute-start.1 = (bf16[32,2048]{1,0:T(8,128)(2,1)S(1)}, bf16[32,2048]{1,0:T(8,128)(2,1)S(1)}, u32[]{:S(2)}, u32[]{:S(2)}) collective-permute-start(bf16[32,2048]{1,0:T(8,128)(2,1)S(1)} %pad_maximum_fusion.9), channel_id=1, source_target_pairs={{0,8},{8,0},{16,24},{24,16},{1,9},{9,1},{17,25},{25,17},{2,10},{10... | collective-permute-start | bytes 393224 | tf_op jit(solution)/shard_map/ppermute | solution.py:362
  12.9 25.8 %all-to-all-start = ((bf16[32,64,128]{2,1,0:T(8,128)(2,1)}), bf16[32,64,128]{2,1,0:T(8,128)(2,1)S(1)}, u32[]{:S(2)}, u32[]{:S(2)}) async-start(bf16[32,64,128]{2,1,0:T(8,128)(2,1)} %bitcast.57), calls=%async_computation | async-start | bytes 1048576 | tf_op jit(solution)/shard_map/all_to_all | solution.py:161
  22.0 12.6 %collective-permute-start.8 = (bf16[64,1024]{1,0:T(8,128)(2,1)S(1)}, bf16[64,1024]{1,0:T(8,128)(2,1)S(1)}, u32[]{:S(2)}, u32[]{:S(2)}) collective-permute-start(bf16[64,1024]{1,0:T(8,128)(2,1)S(1)} %get-tuple-element.71), channel_id=1, source_target_pairs={{0,3},{3,0},{1,2},{2,1},{4,7},{7,4},{5,6},{6,5},{8,11},{11,8},{9,1... | collective-permute-start | bytes 393224 | tf_op jit(solution)/shard_map/ppermute | solution.py:362
  31.5 59.5 %copy-start.7 = (s32[6]{0:T(128)}, s32[6]{0:T(128)S(1)}, u32[]{:S(2)}) copy-start(s32[6]{0:T(128)S(1)} %stack.45.refs_0_.place) | copy-start | bytes 76
  31.5 6.6 %collective-permute-start.2 = (bf16[64,1024]{1,0:T(8,128)(2,1)S(1)}, bf16[64,1024]{1,0:T(8,128)(2,1)S(1)}, u32[]{:S(2)}, u32[]{:S(2)}) collective-permute-start(bf16[64,1024]{1,0:T(8,128)(2,1)S(1)} %get-tuple-element.72), channel_id=1, source_target_pairs={{0,96},{96,0},{32,64},{64,32},{1,97},{97,1},{33,65},{65,33},{2,98}... | collective-permute-start | bytes 393224 | tf_op jit(solution)/shard_map/ppermute | solution.py:362
  34.7 14.7 %collective-permute-start.9 = (bf16[128,1024]{1,0:T(8,128)(2,1)S(1)}, bf16[128,1024]{1,0:T(8,128)(2,1)S(1)}, u32[]{:S(2)}, u32[]{:S(2)}) collective-permute-start(bf16[128,1024]{1,0:T(8,128)(2,1)S(1)} %pad_maximum_fusion.7), channel_id=1, source_target_pairs={{0,1},{1,0},{2,3},{3,2},{4,5},{5,4},{6,7},{7,6},{8,9},{9,8},{10,11... | collective-permute-start | bytes 786440 | tf_op jit(solution)/shard_map/ppermute | solution.py:362
  38.2 15.3 %collective-permute-start.3 = (bf16[128,1024]{1,0:T(8,128)(2,1)S(1)}, bf16[128,1024]{1,0:T(8,128)(2,1)S(1)}, u32[]{:S(2)}, u32[]{:S(2)}) collective-permute-start(bf16[128,1024]{1,0:T(8,128)(2,1)S(1)} %pad_maximum_fusion.6), channel_id=1, source_target_pairs={{0,32},{32,0},{64,96},{96,64},{1,33},{33,1},{65,97},{97,65},{2,34}... | collective-permute-start | bytes 786440 | tf_op jit(solution)/shard_map/ppermute | solution.py:362
  41.3 26.6 %all-to-all-start.1 = ((bf16[32,64,128]{2,1,0:T(8,128)(2,1)}), bf16[32,64,128]{2,1,0:T(8,128)(2,1)S(1)}, u32[]{:S(2)}, u32[]{:S(2)}) async-start(bf16[32,64,128]{2,1,0:T(8,128)(2,1)} %shard_map.103), calls=%async_computation.1 | async-start | bytes 1048576 | tf_op jit(solution)/shard_map/all_to_all | solution.py:163
  49.5 13.9 %collective-permute-start.12 = (bf16[256,512]{1,0:T(8,128)(2,1)S(1)}, bf16[256,512]{1,0:T(8,128)(2,1)S(1)}, u32[]{:S(2)}, u32[]{:S(2)}) collective-permute-start(bf16[256,512]{1,0:T(8,128)(2,1)S(1)} %get-tuple-element.55), channel_id=1, source_target_pairs={{0,32},{32,0},{64,96},{96,64},{1,33},{33,1},{65,97},{97,65},{2,34}... | collective-permute-start | bytes 786440 | tf_op jit(solution)/shard_map/ppermute | solution.py:362
  51.4 15.0 %collective-permute-start.10 = (bf16[256,512]{1,0:T(8,128)(2,1)S(1)}, bf16[256,512]{1,0:T(8,128)(2,1)S(1)}, u32[]{:S(2)}, u32[]{:S(2)}) collective-permute-start(bf16[256,512]{1,0:T(8,128)(2,1)S(1)} %get-tuple-element.56), channel_id=1, source_target_pairs={{0,96},{96,0},{32,64},{64,32},{1,97},{97,1},{33,65},{65,33},{2,98}... | collective-permute-start | bytes 786440 | tf_op jit(solution)/shard_map/ppermute | solution.py:362
  54.4 30.5 %collective-permute-start.6 = (bf16[256,512]{1,0:T(8,128)(2,1)}, bf16[256,512]{1,0:T(8,128)(2,1)}, u32[]{:S(2)}, u32[]{:S(2)}) collective-permute-start(bf16[256,512]{1,0:T(8,128)(2,1)} %get-tuple-element.63), channel_id=1, source_target_pairs={{0,1},{1,0},{2,3},{3,2},{4,5},{5,4},{6,7},{7,6},{8,9},{9,8},{10,11... | collective-permute-start | bytes 786440 | tf_op jit(solution)/shard_map/ppermute | solution.py:362
  56.2 29.3 %collective-permute-start.4 = (bf16[256,512]{1,0:T(8,128)(2,1)S(1)}, bf16[256,512]{1,0:T(8,128)(2,1)}, u32[]{:S(2)}, u32[]{:S(2)}) collective-permute-start(bf16[256,512]{1,0:T(8,128)(2,1)S(1)} %get-tuple-element.64), channel_id=1, source_target_pairs={{0,3},{3,0},{1,2},{2,1},{4,7},{7,4},{5,6},{6,5},{8,11},{11,8},{9,1... | collective-permute-start | bytes 786440 | tf_op jit(solution)/shard_map/ppermute | solution.py:362
  64.3 23.5 %collective-permute-start.13 = (bf16[512,512]{1,0:T(8,128)(2,1)}, bf16[512,512]{1,0:T(8,128)(2,1)}, u32[]{:S(2)}, u32[]{:S(2)}) collective-permute-start(bf16[512,512]{1,0:T(8,128)(2,1)} %pad_maximum_fusion.3.refs_1_), channel_id=1, source_target_pairs={{0,96},{96,0},{32,64},{64,32},{1,97},{97,1},{33,65},{65,33},{2,98}... | collective-permute-start | bytes 1572872 | tf_op jit(solution)/shard_map/ppermute | solution.py:362
  67.3 22.0 %collective-permute-start.11 = (bf16[512,512]{1,0:T(8,128)(2,1)}, bf16[512,512]{1,0:T(8,128)(2,1)}, u32[]{:S(2)}, u32[]{:S(2)}) collective-permute-start(bf16[512,512]{1,0:T(8,128)(2,1)} %pad_maximum_fusion.2.refs_1_), channel_id=1, source_target_pairs={{0,32},{32,0},{64,96},{96,64},{1,33},{33,1},{65,97},{97,65},{2,34}... | collective-permute-start | bytes 1572872 | tf_op jit(solution)/shard_map/ppermute | solution.py:362
  68.8 7.7 %copy-start = (bf16[1,512,2048]{2,1,0:T(8,128)(2,1)S(1)}, bf16[1,512,2048]{2,1,0:T(8,128)(2,1)}, u32[]{:S(2)}) copy-start(bf16[1,512,2048]{2,1,0:T(8,128)(2,1)} %param.9) | copy-start | bytes 6291460
  80.3 32.1 %collective-permute-start.29 = (bf16[1024,512]{1,0:T(8,128)(2,1)}, bf16[1024,512]{1,0:T(8,128)(2,1)S(1)}, u32[]{:S(2)}, u32[]{:S(2)}) collective-permute-start(bf16[1024,512]{1,0:T(8,128)(2,1)} %pair_product.7), channel_id=1, source_target_pairs={{0,4},{4,0},{1,5},{5,1},{2,6},{6,2},{3,7},{7,3},{8,12},{12,8},{9,1... | collective-permute-start | bytes 3145736 | tf_op jit(solution)/shard_map/ppermute | solution.py:465
  84.9 27.6 %collective-permute-start.26 = (bf16[1024,512]{1,0:T(8,128)(2,1)}, bf16[1024,512]{1,0:T(8,128)(2,1)}, u32[]{:S(2)}, u32[]{:S(2)}) collective-permute-start(bf16[1024,512]{1,0:T(8,128)(2,1)} %pair_product.6), channel_id=1, source_target_pairs={{0,4},{4,0},{1,5},{5,1},{2,6},{6,2},{3,7},{7,3},{8,12},{12,8},{9,1... | collective-permute-start | bytes 3145736 | tf_op jit(solution)/shard_map/ppermute | solution.py:465
  85.4 30.5 %collective-permute-start.21 = (bf16[1024,512]{1,0:T(8,128)(2,1)}, bf16[1024,512]{1,0:T(8,128)(2,1)}, u32[]{:S(2)}, u32[]{:S(2)}) collective-permute-start(bf16[1024,512]{1,0:T(8,128)(2,1)} %pair_product.5), channel_id=1, source_target_pairs={{0,4},{4,0},{1,5},{5,1},{2,6},{6,2},{3,7},{7,3},{8,12},{12,8},{9,1... | collective-permute-start | bytes 3145736 | tf_op jit(solution)/shard_map/ppermute | solution.py:465
  86.6 6.7 %copy-start.9 = (bf16[512,512]{1,0:T(8,128)(2,1)}, bf16[512,512]{1,0:T(8,128)(2,1)S(1)}, u32[]{:S(2)}) copy-start(bf16[512,512]{1,0:T(8,128)(2,1)S(1)} %pad_maximum_fusion.1.refs_1_) | copy-start | bytes 1572868
  87.8 14.3 %collective-permute-start.7 = (bf16[512,512]{1,0:T(8,128)(2,1)S(1)}, bf16[512,512]{1,0:T(8,128)(2,1)S(1)}, u32[]{:S(2)}, u32[]{:S(2)}) collective-permute-start(bf16[512,512]{1,0:T(8,128)(2,1)S(1)} %pad_maximum_fusion.1.refs_1_), channel_id=1, source_target_pairs={{0,3},{3,0},{1,2},{2,1},{4,7},{7,4},{5,6},{6,5},{8,11},{11,8},{9,1... | collective-permute-start | bytes 1572872 | tf_op jit(solution)/shard_map/ppermute | solution.py:362
  89.3 22.6 %collective-permute-start.5 = (bf16[512,512]{1,0:T(8,128)(2,1)}, bf16[512,512]{1,0:T(8,128)(2,1)}, u32[]{:S(2)}, u32[]{:S(2)}) collective-permute-start(bf16[512,512]{1,0:T(8,128)(2,1)} %pad_maximum_fusion.refs_1_), channel_id=1, source_target_pairs={{0,1},{1,0},{2,3},{3,2},{4,5},{5,4},{6,7},{7,6},{8,9},{9,8},{10,11... | collective-permute-start | bytes 1572872 | tf_op jit(solution)/shard_map/ppermute | solution.py:362
  102.9 23.7 %collective-permute-start.18 = (bf16[1024,512]{1,0:T(8,128)(2,1)}, bf16[1024,512]{1,0:T(8,128)(2,1)}, u32[]{:S(2)}, u32[]{:S(2)}) collective-permute-start(bf16[1024,512]{1,0:T(8,128)(2,1)} %pair_product.4), channel_id=1, source_target_pairs={{0,4},{4,0},{1,5},{5,1},{2,6},{6,2},{3,7},{7,3},{8,12},{12,8},{9,1... | collective-permute-start | bytes 3145736 | tf_op jit(solution)/shard_map/ppermute | solution.py:465
  108.8 7.2 %copy-start.8 = (s32[6]{0:T(128)S(1)}, s32[6]{0:T(128)}, u32[]{:S(2)}) copy-start(s32[6]{0:T(128)} %copy-done.7) | copy-start | bytes 76
  111.9 18.7 %collective-permute-start.17 = (bf16[1024,512]{1,0:T(8,128)(2,1)}, bf16[1024,512]{1,0:T(8,128)(2,1)}, u32[]{:S(2)}, u32[]{:S(2)}) collective-permute-start(bf16[1024,512]{1,0:T(8,128)(2,1)} %last_rows.7.w3), channel_id=1, source_target_pairs={{0,4},{4,0},{1,5},{5,1},{2,6},{6,2},{3,7},{7,3},{8,12},{12,8},{9,1... | collective-permute-start | bytes 3145736 | tf_op jit(solution)/shard_map/ppermute | solution.py:430
  112.4 19.6 %collective-permute-start.16 = (bf16[1024,512]{1,0:T(8,128)(2,1)}, bf16[1024,512]{1,0:T(8,128)(2,1)}, u32[]{:S(2)}, u32[]{:S(2)}) collective-permute-start(bf16[1024,512]{1,0:T(8,128)(2,1)} %last_rows.6.w2), channel_id=1, source_target_pairs={{0,4},{4,0},{1,5},{5,1},{2,6},{6,2},{3,7},{7,3},{8,12},{12,8},{9,1... | collective-permute-start | bytes 3145736 | tf_op jit(solution)/shard_map/ppermute | solution.py:430
  112.5 20.1 %collective-permute-start.15 = (bf16[1024,512]{1,0:T(8,128)(2,1)}, bf16[1024,512]{1,0:T(8,128)(2,1)}, u32[]{:S(2)}, u32[]{:S(2)}) collective-permute-start(bf16[1024,512]{1,0:T(8,128)(2,1)} %last_rows.5.w1), channel_id=1, source_target_pairs={{0,4},{4,0},{1,5},{5,1},{2,6},{6,2},{3,7},{7,3},{8,12},{12,8},{9,1... | collective-permute-start | bytes 3145736 | tf_op jit(solution)/shard_map/ppermute | solution.py:430
  115.9 19.6 %collective-permute-start.14 = (bf16[1024,512]{1,0:T(8,128)(2,1)}, bf16[1024,512]{1,0:T(8,128)(2,1)}, u32[]{:S(2)}, u32[]{:S(2)}) collective-permute-start(bf16[1024,512]{1,0:T(8,128)(2,1)} %last_rows.4.w0), channel_id=1, source_target_pairs={{0,4},{4,0},{1,5},{5,1},{2,6},{6,2},{3,7},{7,3},{8,12},{12,8},{9,1... | collective-permute-start | bytes 3145736 | tf_op jit(solution)/shard_map/ppermute | solution.py:430
  119.7 3.4 %copy-start.5 = (bf16[512,512]{1,0:T(8,128)(2,1)}, bf16[512,512]{1,0:T(8,128)(2,1)S(1)}, u32[]{:S(2)}) copy-start(bf16[512,512]{1,0:T(8,128)(2,1)S(1)} %get-tuple-element.51) | copy-start | bytes 1572868
  126.6 34.0 %collective-permute-start.30 = (bf16[512,512]{1,0:T(8,128)(2,1)}, bf16[512,512]{1,0:T(8,128)(2,1)}, u32[]{:S(2)}, u32[]{:S(2)}) collective-permute-start(bf16[512,512]{1,0:T(8,128)(2,1)} %get-tuple-element.52), channel_id=1, source_target_pairs={{0,96},{96,0},{32,64},{64,32},{1,97},{97,1},{33,65},{65,33},{2,98}... | collective-permute-start | bytes 1572872 | tf_op jit(solution)/shard_map/ppermute | solution.py:362
  130.6 33.0 %collective-permute-start.27 = (bf16[512,512]{1,0:T(8,128)(2,1)}, bf16[512,512]{1,0:T(8,128)(2,1)}, u32[]{:S(2)}, u32[]{:S(2)}) collective-permute-start(bf16[512,512]{1,0:T(8,128)(2,1)} %get-tuple-element.50), channel_id=1, source_target_pairs={{0,32},{32,0},{64,96},{96,64},{1,33},{33,1},{65,97},{97,65},{2,34}... | collective-permute-start | bytes 1572872 | tf_op jit(solution)/shard_map/ppermute | solution.py:362
  132.0 35.0 %collective-permute-start.22 = (bf16[512,512]{1,0:T(8,128)(2,1)}, bf16[512,512]{1,0:T(8,128)(2,1)S(1)}, u32[]{:S(2)}, u32[]{:S(2)}) collective-permute-start(bf16[512,512]{1,0:T(8,128)(2,1)} %get-tuple-element.48), channel_id=1, source_target_pairs={{0,3},{3,0},{1,2},{2,1},{4,7},{7,4},{5,6},{6,5},{8,11},{11,8},{9,1... | collective-permute-start | bytes 1572872 | tf_op jit(solution)/shard_map/ppermute | solution.py:362
  132.5 34.7 %collective-permute-start.19 = (bf16[512,512]{1,0:T(8,128)(2,1)}, bf16[512,512]{1,0:T(8,128)(2,1)S(1)}, u32[]{:S(2)}, u32[]{:S(2)}) collective-permute-start(bf16[512,512]{1,0:T(8,128)(2,1)} %get-tuple-element.46), channel_id=1, source_target_pairs={{0,1},{1,0},{2,3},{3,2},{4,5},{5,4},{6,7},{7,6},{8,9},{9,8},{10,11... | collective-permute-start | bytes 1572872 | tf_op jit(solution)/shard_map/ppermute | solution.py:362
  135.5 25.1 %copy-start.6 = (bf16[512,512]{1,0:T(8,128)(2,1)S(1)}, bf16[512,512]{1,0:T(8,128)(2,1)}, u32[]{:S(2)}) copy-start(bf16[512,512]{1,0:T(8,128)(2,1)} %copy-done.5) | copy-start | bytes 1572868
  153.4 10.2 %copy-start.4 = (bf16[512,512]{1,0:T(8,128)(2,1)S(1)}, bf16[512,512]{1,0:T(8,128)(2,1)}, u32[]{:S(2)}) copy-start(bf16[512,512]{1,0:T(8,128)(2,1)} %copy-done.3) | copy-start | bytes 1572868
  153.5 58.6 %all-to-all-start.2 = ((bf16[32,64,128]{2,1,0:T(8,128)(2,1)}), bf16[32,64,128]{2,1,0:T(8,128)(2,1)}, u32[]{:S(2)}, u32[]{:S(2)}) async-start(bf16[32,64,128]{2,1,0:T(8,128)(2,1)} %bitcast.56), calls=%async_computation.2 | async-start | bytes 1048576 | tf_op jit(solution)/shard_map/all_to_all | solution.py:161
  161.8 12.7 %collective-permute-start.31 = (bf16[256,512]{1,0:T(8,128)(2,1)S(1)}, bf16[256,512]{1,0:T(8,128)(2,1)S(1)}, u32[]{:S(2)}, u32[]{:S(2)}) collective-permute-start(bf16[256,512]{1,0:T(8,128)(2,1)S(1)} %constant_dynamic-slice_fusion.2), channel_id=1, source_target_pairs={{0,32},{32,0},{64,96},{96,64},{1,33},{33,1},{65,97},{97,65},{2,34}... | collective-permute-start | bytes 786440 | tf_op jit(solution)/shard_map/ppermute | solution.py:362
  164.8 11.0 %collective-permute-start.28 = (bf16[256,512]{1,0:T(8,128)(2,1)S(1)}, bf16[256,512]{1,0:T(8,128)(2,1)S(1)}, u32[]{:S(2)}, u32[]{:S(2)}) collective-permute-start(bf16[256,512]{1,0:T(8,128)(2,1)S(1)} %constant_dynamic-slice_fusion.3), channel_id=1, source_target_pairs={{0,96},{96,0},{32,64},{64,32},{1,97},{97,1},{33,65},{65,33},{2,98}... | collective-permute-start | bytes 786440 | tf_op jit(solution)/shard_map/ppermute | solution.py:362
  167.1 8.9 %collective-permute-start.23 = (bf16[256,512]{1,0:T(8,128)(2,1)S(1)}, bf16[256,512]{1,0:T(8,128)(2,1)S(1)}, u32[]{:S(2)}, u32[]{:S(2)}) collective-permute-start(bf16[256,512]{1,0:T(8,128)(2,1)S(1)} %constant_dynamic-slice_fusion.5), channel_id=1, source_target_pairs={{0,1},{1,0},{2,3},{3,2},{4,5},{5,4},{6,7},{7,6},{8,9},{9,8},{10,11... | collective-permute-start | bytes 786440 | tf_op jit(solution)/shard_map/ppermute | solution.py:362
  167.4 8.7 %collective-permute-start.20 = (bf16[256,512]{1,0:T(8,128)(2,1)S(1)}, bf16[256,512]{1,0:T(8,128)(2,1)S(1)}, u32[]{:S(2)}, u32[]{:S(2)}) collective-permute-start(bf16[256,512]{1,0:T(8,128)(2,1)S(1)} %constant_dynamic-slice_fusion.6), channel_id=1, source_target_pairs={{0,3},{3,0},{1,2},{2,1},{4,7},{7,4},{5,6},{6,5},{8,11},{11,8},{9,1... | collective-permute-start | bytes 786440 | tf_op jit(solution)/shard_map/ppermute | solution.py:362
  175.9 7.9 %collective-permute-start.32 = (bf16[2,128,512]{2,1,0:T(8,128)(2,1)S(1)}, bf16[2,128,512]{2,1,0:T(8,128)(2,1)S(1)}, u32[]{:S(2)}, u32[]{:S(2)}) collective-permute-start(bf16[2,128,512]{2,1,0:T(8,128)(2,1)S(1)} %fusion.7), channel_id=1, source_target_pairs={{0,1},{1,0},{2,3},{3,2},{4,5},{5,4},{6,7},{7,6},{8,9},{9,8},{10,11... | collective-permute-start | bytes 786440 | tf_op jit(solution)/shard_map/ppermute | solution.py:362
  176.2 9.9 %collective-permute-start.24 = (bf16[2,128,512]{2,1,0:T(8,128)(2,1)S(1)}, bf16[2,128,512]{2,1,0:T(8,128)(2,1)S(1)}, u32[]{:S(2)}, u32[]{:S(2)}) collective-permute-start(bf16[2,128,512]{2,1,0:T(8,128)(2,1)S(1)} %fusion.9), channel_id=1, source_target_pairs={{0,32},{32,0},{64,96},{96,64},{1,33},{33,1},{65,97},{97,65},{2,34}... | collective-permute-start | bytes 786440 | tf_op jit(solution)/shard_map/ppermute | solution.py:362
  183.9 5.2 %collective-permute-start.33 = (bf16[2,64,512]{2,1,0:T(8,128)(2,1)S(1)}, bf16[2,64,512]{2,1,0:T(8,128)(2,1)S(1)}, u32[]{:S(2)}, u32[]{:S(2)}) collective-permute-start(bf16[2,64,512]{2,1,0:T(8,128)(2,1)S(1)} %constant_dynamic-slice_fusion.1), channel_id=1, source_target_pairs={{0,3},{3,0},{1,2},{2,1},{4,7},{7,4},{5,6},{6,5},{8,11},{11,8},{9,1... | collective-permute-start | bytes 393224 | tf_op jit(solution)/shard_map/ppermute | solution.py:362
  186.2 6.3 %collective-permute-start.25 = (bf16[2,64,512]{2,1,0:T(8,128)(2,1)S(1)}, bf16[2,64,512]{2,1,0:T(8,128)(2,1)S(1)}, u32[]{:S(2)}, u32[]{:S(2)}) collective-permute-start(bf16[2,64,512]{2,1,0:T(8,128)(2,1)S(1)} %constant_dynamic-slice_fusion.4), channel_id=1, source_target_pairs={{0,96},{96,0},{32,64},{64,32},{1,97},{97,1},{33,65},{65,33},{2,98}... | collective-permute-start | bytes 393224 | tf_op jit(solution)/shard_map/ppermute | solution.py:362
  192.5 26.1 %collective-permute-start.34 = (bf16[4,32,512]{2,1,0:T(8,128)(2,1)S(1)}, bf16[4,32,512]{2,1,0:T(8,128)(2,1)S(1)}, u32[]{:S(2)}, u32[]{:S(2)}) collective-permute-start(bf16[4,32,512]{2,1,0:T(8,128)(2,1)S(1)} %fusion.12), channel_id=1, source_target_pairs={{0,8},{8,0},{16,24},{24,16},{1,9},{9,1},{17,25},{25,17},{2,10},{10... | collective-permute-start | bytes 393224 | tf_op jit(solution)/shard_map/ppermute | solution.py:362
  212.1 9.7 %copy-start.14 = (bf16[512,2048]{1,0:T(8,128)(2,1)S(1)}, bf16[512,2048]{1,0:T(8,128)(2,1)}, u32[]{:S(2)}) copy-start(bf16[512,2048]{1,0:T(8,128)(2,1)} %get-tuple-element.33) | copy-start | bytes 6291460
  214.1 16.8 %all-to-all-start.3 = ((bf16[32,64,128]{2,1,0:T(8,128)(2,1)}), bf16[32,64,128]{2,1,0:T(8,128)(2,1)S(1)}, u32[]{:S(2)}, u32[]{:S(2)}) async-start(bf16[32,64,128]{2,1,0:T(8,128)(2,1)} %shard_map.106), calls=%async_computation.3 | async-start | bytes 1048576 | tf_op jit(solution)/shard_map/all_to_all | solution.py:163
  218.7 12.1 %collective-permute-start.35 = (bf16[4,16,512]{2,1,0:T(8,128)(2,1)S(1)}, bf16[4,16,512]{2,1,0:T(8,128)(2,1)S(1)}, u32[]{:S(2)}, u32[]{:S(2)}) collective-permute-start(bf16[4,16,512]{2,1,0:T(8,128)(2,1)S(1)} %constant_dynamic-slice_fusion), channel_id=1, source_target_pairs={{0,24},{24,0},{8,16},{16,8},{1,25},{25,1},{9,17},{17,9},{2,26},{26... | collective-permute-start | bytes 196616 | tf_op jit(solution)/shard_map/ppermute | solution.py:362
  (7 other events, 9.8 us)

commit v3 on v1

--- a/solution.py
+++ b/solution.py
@@ -74,8 +74,14 @@
     )
 
 
+COLORS = 2
+WIDTH = FEATURES // COLORS
+SLAB = 16
+PLACES = 64
+CYCLES = (((0, 1), (1, 0), (2, 3), (3, 2)), ((0, 3), (3, 0), (1, 2), (2, 1)))
 PAIR_SPEC = spec((BLOCK, PAIR), lambda i: (0, i))
 STATE_SPEC = spec((GROUP, HEAD_DIM, HEAD_DIM), lambda i: (i, 0, 0))
+SCORE_SPEC = spec((GROUP, 3, HALF, HALF), lambda i: (i, 0, 0, 0))
 WIDE_LOW = jax.ShapeDtypeStruct((BLOCK, FEATURES), BF16)
 WIDE = jax.ShapeDtypeStruct((BLOCK, FEATURES), F32)
 STATE_LOW = jax.ShapeDtypeStruct((HEADS, HEAD_DIM, HEAD_DIM), BF16)
@@ -101,7 +107,7 @@
     )(key, value)
 
 
-def inside_body(query, feat_key, value, feat_query, inside):
+def inside_body(query, feat_key, value, feat_query, inside, scores):
     for i in range(GROUP):
         low = silu_low(query[:, head(i)])
         feat_query[:, head(i)] = low
@@ -110,6 +116,7 @@
         first = causal(dot_nt(low[:HALF], keys[:HALF]))
         below = dot_nt(low[HALF:], keys[:HALF]).astype(BF16)
         second = causal(dot_nt(low[HALF:], keys[HALF:]))
+        scores[i, 0], scores[i, 1], scores[i, 2] = first, below, second
         inside[:HALF, head(i)] = dot_nn(first, values[:HALF])
         inside[HALF:, head(i)] = dot_nn(below, values[:HALF]) + dot_nn(second, values[HALF:])
 
@@ -119,10 +126,10 @@
         inside_body,
         (HEADS // GROUP,),
         [PAIR_SPEC] * 3,
-        [PAIR_SPEC] * 2,
-        [WIDE_LOW, WIDE],
+        [PAIR_SPEC, PAIR_SPEC, SCORE_SPEC],
+        [WIDE_LOW, WIDE, jax.ShapeDtypeStruct((HEADS, 3, HALF, HALF), BF16)],
         1 << 32,
-        12 * MIB,
+        18 * MIB,
     )(query, feat_key, value)
 
 
@@ -163,7 +170,7 @@
 EDGE_SPEC = spec((ROWS, HEAD_DIM), lambda i: (i, 0))
 GAIN_SPEC = spec((1, FEATURES), lambda i: (0, 0))
 ALL_STATES = spec((HEADS, HEAD_DIM, HEAD_DIM), lambda i: (0, 0, 0))
-SPLIT_SPEC = spec((2, ROWS, FEATURES // 2), lambda i: (0, i, 0))
+SPLIT_SPEC = spec((2, FEATURES // 2, ROWS), lambda i: (0, 0, i))
 
 
 def attend_body(inside, feat_query, state, gain, mixed, split, normed, inverse):
@@ -185,8 +192,10 @@
             mixed[:, head(j)] = low
             lows.append(low)
         at = head(i // 2)
-        split[0, :, at] = jnp.concatenate([lows[0][:, :part], lows[1][:, :part]], axis=1)
-        split[1, :, at] = jnp.concatenate([lows[0][:, part:], lows[1][:, part:]], axis=1)
+        turned = [low.T for low in lows]
+        for side in range(2):
+            rows = slice(side * part, (side + 1) * part)
+            split[side, at] = jnp.concatenate([turned[0][rows], turned[1][rows]], axis=0)
 
 
 def attend(inside, feat_query, state, gain):
@@ -197,13 +206,17 @@
         [ROW_SPEC, SPLIT_SPEC, ROW_SPEC, EDGE_SPEC],
         [
             WIDE_LOW,
-            jax.ShapeDtypeStruct((2, BLOCK, FEATURES // 2), BF16),
+            jax.ShapeDtypeStruct((2, FEATURES // 2, BLOCK), BF16),
             WIDE,
             jax.ShapeDtypeStruct((BLOCK, HEAD_DIM), F32),
         ],
         1 << 29,
         15 * MIB,
     )(inside, feat_query, state, gain)
+
+
+CHUNK = 2 * HEAD_DIM
+CHUNKS = FEATURES // CHUNK
 
 
 CHUNK = 2 * HEAD_DIM
@@ -264,16 +277,16 @@
     )(grad_result, weight, normed, inverse, gain, feat_query)
 
 
-def back_body(query, feat_query, feat_key, value, grad, state, grad_query, part_key, part_value):
+def back_body(
+    query, feat_query, feat_key, value, grad, state, scores, grad_query, part_key, part_value
+):
     for i in range(GROUP):
         at = head(i)
         q0, q1 = feat_query[:HALF, at], feat_query[HALF:, at]
         k0, k1 = feat_key[:HALF, at], feat_key[HALF:, at]
         v0, v1 = value[:HALF, at], value[HALF:, at]
         g0, g1 = grad[:HALF, at], grad[HALF:, at]
-        s00 = causal(dot_nt(q0, k0))
-        s10 = dot_nt(q1, k0).astype(BF16)
-        s11 = causal(dot_nt(q1, k1))
+        s00, s10, s11 = scores[i, 0], scores[i, 1], scores[i, 2]
         part_value[:HALF, at] = dot_tn(s00, g0) + dot_tn(s10, g1)
         part_value[HALF:, at] = dot_tn(s11, g1)
         d00 = causal(dot_nt(g0, v0))
@@ -287,16 +300,16 @@
         grad_query[HALF:, at] = (fq1 * silu_slope(query[HALF:, at])).astype(BF16)
 
 
-def back_inside(query, feat_query, feat_key, value, grad, state):
+def back_inside(query, feat_query, feat_key, value, grad, state, scores):
     return call(
         back_body,
         (HEADS // GROUP,),
-        [PAIR_SPEC] * 5 + [STATE_SPEC],
+        [PAIR_SPEC] * 5 + [STATE_SPEC, SCORE_SPEC],
         [PAIR_SPEC] * 3,
         [WIDE_LOW, WIDE, WIDE],
         3 << 32,
         20 * MIB,
-    )(query, feat_query, feat_key, value, grad, state)
+    )(query, feat_query, feat_key, value, grad, state, scores)
 
 
 def finish_body(key, feat_key, value, part_key, part_value, later, grad_key, grad_value):
@@ -319,13 +332,6 @@
     )(key, feat_key, value, part_key, part_value, later)
 
 
-COLORS = 4
-WIDTH = FEATURES // COLORS
-SLAB = 16
-PLACES = 64
-CYCLES = (((0, 1), (1, 0), (2, 3), (3, 2)), ((0, 3), (3, 0), (1, 2), (2, 1)))
-
-
 def on_ring(low, high):
     return low + high * (3 - 2 * low)
 
@@ -341,101 +347,109 @@
     return lax.ppermute(sent, axis, CYCLES[which])
 
 
-def product_body(place, left, right, out):
-    out[...] = dot_tn(left[0], right[...]).astype(BF16)
-
-
-def first_body(color, place, left, right, got, kept, sent, acc):
-    acc[...] = (dot_tn(left[0], right[...]) + got[...].astype(F32)).astype(BF16)
+def product_body(place, mine, other, right, *outs):
+    for left, parts in ((other, outs[:COLORS]), (mine, outs[COLORS:])):
+        for c, out in enumerate(parts):
+            out[...] = dot_nn(left[0], right[:, c * WIDTH : (c + 1) * WIDTH]).astype(BF16)
+
+
+def slab_at(color, side, s):
+    other, rest = s // 16, s % 16
+    x = on_ring(side, other) if color == 0 else on_ring(other, side)
+    return pl.multiple_of((rest * 4 + x) * SLAB, SLAB)
+
+
+def first_body(color, place, mine, got, kept, sent):
     bit = place[2 + color]
     for side, out in ((bit, kept), (1 - bit, sent)):
         for s in range(PLACES // 2):
-            other, rest, z = s // 16, (s // 4) % 4, s % 4
-            z = on_ring(z // 2, z % 2)
-            far = on_ring(rest // 2, rest % 2)
-            near = on_ring(side, other) if color % 2 == 0 else on_ring(other, side)
-            y, x = (far, near) if color < 2 else (near, far)
-            at = pl.multiple_of((y * 16 + z * 4 + x) * SLAB, SLAB)
-            out[s * SLAB : (s + 1) * SLAB] = acc[pl.ds(at, SLAB)]
+            rows = pl.ds(slab_at(color, side, s), SLAB)
+            total = mine[rows].astype(F32) + got[rows].astype(F32)
+            out[s * SLAB : (s + 1) * SLAB] = total.astype(BF16)
+
+
+def second_body(color, place, kept, got, rest, sent):
+    bit = place[2 + color]
+    rows = kept.shape[0] // 2
+    for side, out in ((bit, rest), (1 - bit, sent)):
+        at = pl.ds(pl.multiple_of(side * rows, rows), rows)
+        out[...] = (kept[at].astype(F32) + got[at].astype(F32)).astype(BF16)
+
+
+def placed_call(body, place, args, in_specs, out_specs, out_shape, flops, moved, grid):
+    return pl.pallas_call(
+        body,
+        grid_spec=pltpu.PrefetchScalarGridSpec(
+            num_scalar_prefetch=1, grid=(grid,), in_specs=in_specs, out_specs=out_specs
+        ),
+        out_shape=out_shape,
+        compiler_params=pltpu.CompilerParams(vmem_limit_bytes=60 * MIB),
+        cost_estimate=pl.CostEstimate(flops=flops, bytes_accessed=moved, transcendentals=0),
+    )(place, *args)
 
 
 def gradient_rows(split, grad_result):
     core = lax.axis_index("seq_2")
-    xs, ys, zs = my_bits("dp"), my_bits("seq_0"), my_bits("seq_1")
-    place = jnp.stack([core, 1 - core, xs[0], xs[1], ys[0], ys[1]]).astype(jnp.int32)
+    bits = my_bits("dp")
+    place = jnp.stack([core, 1 - core, bits[0], bits[1]]).astype(jnp.int32)
     half = FEATURES // 2
-
-    def grid_spec(which, color, more, outs):
-        return pltpu.PrefetchScalarGridSpec(
-            num_scalar_prefetch=1,
-            grid=(1,),
-            in_specs=[
-                pl.BlockSpec((1, BLOCK, half), lambda i, p: (p[which], 0, 0)),
-                pl.BlockSpec((BLOCK, WIDTH), lambda i, p: (0, color)),
-            ]
-            + more,
-            out_specs=outs,
-            scratch_shapes=[pltpu.VMEM((half, WIDTH), BF16)] if more else [],
+    rows = half // 4
+
+    def block(share):
+        return pl.BlockSpec((half // share, WIDTH), lambda i, p: (0, 0))
+
+    def low(share):
+        return jax.ShapeDtypeStruct((half // share, WIDTH), BF16)
+
+    products = placed_call(
+        product_body,
+        place,
+        (split, split, grad_result),
+        [
+            pl.BlockSpec((1, rows, BLOCK), lambda i, p: (p[0], i, 0)),
+            pl.BlockSpec((1, rows, BLOCK), lambda i, p: (p[1], i, 0)),
+            pl.BlockSpec((BLOCK, FEATURES), lambda i, p: (0, 0)),
+        ],
+        [pl.BlockSpec((rows, WIDTH), lambda i, p: (i, 0))] * (2 * COLORS),
+        [low(1)] * (2 * COLORS),
+        1 << 32,
+        12 * MIB,
+        4,
+    )
+    gots = [lax.ppermute(p, "seq_2", [(0, 1), (1, 0)]) for p in products[:COLORS]]
+    firsts = []
+    for color in range(COLORS):
+        kept, sent = placed_call(
+            lambda *refs, color=color: first_body(color, *refs),
+            place,
+            (products[COLORS + color], gots[color]),
+            [block(1)] * 2,
+            [block(2)] * 2,
+            [low(2)] * 2,
+            1 << 26,
+            6 * MIB,
+            1,
         )
-
-    whole = pl.BlockSpec((half, WIDTH), lambda i, p: (0, 0))
-    part = pl.BlockSpec((half // 2, WIDTH), lambda i, p: (0, 0))
-    params = pltpu.CompilerParams(vmem_limit_bytes=32 * MIB)
-    cost = pl.CostEstimate(flops=1 << 30, bytes_accessed=4 * MIB, transcendentals=0)
-
-    gots = []
-    for color in range(COLORS):
-        sent = pl.pallas_call(
-            product_body,
-            grid_spec=grid_spec(1, color, [], whole),
-            out_shape=jax.ShapeDtypeStruct((half, WIDTH), BF16),
-            compiler_params=params,
-            cost_estimate=cost,
-            name="pair_product",
-        )(place, split, grad_result)
-        gots.append(lax.ppermute(sent, "seq_2", [(0, 1), (1, 0)]))
-    order = ((xs, "dp"), (ys, "seq_0"))
-    keeps = []
-    for color in range(COLORS):
-        kept, sent = pl.pallas_call(
-            lambda *refs, color=color: first_body(color, *refs),
-            grid_spec=grid_spec(0, color, [whole], [part, part]),
-            out_shape=[jax.ShapeDtypeStruct((half // 2, WIDTH), BF16)] * 2,
-            compiler_params=params,
-            cost_estimate=cost,
-            name="first_halves",
-        )(place, split, grad_result, gots[color])
-        keeps.append((kept, hop(sent, order[color // 2][1], color % 2)))
-
-    def halves(total, bit, axis):
-        count = total.shape[axis] // 2
-        kept = lax.dynamic_slice_in_dim(total, bit * count, count, axis)
-        sent = lax.dynamic_slice_in_dim(total, (1 - bit) * count, count, axis)
-        return (kept, sent)
-
-    def add(kept, got):
-        return (kept.astype(F32) + got.astype(F32)).astype(BF16)
-
+        firsts.append((kept, hop(sent, "dp", color)))
     seconds = []
-    for color, (kept, got) in enumerate(keeps):
-        bits, axis = order[color // 2]
-        which = 1 - color % 2
-        kept, sent = halves(add(kept, got), bits[which], 0)
-        seconds.append((kept, hop(sent, axis, which)))
-    joined = []
-    for near in range(2):
-        bits, axis = order[1 - near]
-        total = jnp.stack([add(*seconds[2 * near]), add(*seconds[2 * near + 1])])
-        for which in range(2):
-            kept, sent = halves(total, bits[which], 1)
-            total = add(kept, hop(sent, axis, which))
-        joined.append(total)
-    total = jnp.concatenate(joined, axis=0)
-    kept, sent = halves(total, zs[0], 1)
-    total = add(kept, hop(sent, "seq_1", 0))
-    kept, sent = halves(total, zs[1], 1)
-    total = kept.astype(F32) + hop(sent, "seq_1", 1).astype(F32)
-    return jnp.concatenate([total[c] for c in range(COLORS)], axis=1)
+    for color, (kept, got) in enumerate(firsts):
+        rest, sent = placed_call(
+            lambda *refs, color=color: second_body(1 - color, *refs),
+            place,
+            (kept, got),
+            [block(2)] * 2,
+            [block(4)] * 2,
+            [low(4)] * 2,
+            1 << 26,
+            3 * MIB,
+            1,
+        )
+        seconds.append((rest, hop(sent, "dp", 1 - color)))
+    total = jnp.concatenate(
+        [(rest.astype(F32) + got.astype(F32)).astype(BF16) for rest, got in seconds], axis=1
+    )
+    total = lax.psum_scatter(total, ("seq_0", "seq_1"), scatter_dimension=0, tiled=True)
+    return total.astype(F32)
 
 
 def layer(query_input, key_input, value_input, grad_output, out_weight, norm_gain):
@@ -444,7 +458,7 @@
     full_weight = lax.all_gather(out_weight, SEQ_DP, axis=0, tiled=True)
     feat_key, block_kv = block_states(key, value)
     prefix = scanned(block_kv, False)
-    feat_query, inside = inside_blocks(query, feat_key, value)
+    feat_query, inside, scores = inside_blocks(query, feat_key, value)
     mixed, split, normed, inverse = attend(inside, feat_query, prefix, gain)
     grad_weight = gradient_rows(split, grad_result)
     grad_att, block_grad = norm_back(
@@ -453,7 +467,7 @@
     later = scanned(block_grad, True)
     result = dot_nn(mixed, full_weight).astype(BF16)
     grad_query, part_key, part_value = back_inside(
-        query, feat_query, feat_key, value, grad_att, prefix
+        query, feat_query, feat_key, value, grad_att, prefix, scores
     )
     grad_key, grad_value = finish(key, feat_key, value, part_key, part_value, later)
     return (result[None], grad_query[None], grad_key[None], grad_value[None], grad_weight)

time: 209 us -> 280 us (1.34)
  the two profiles are of different devices: /device:TPU:1 before, /device:TPU:2 now
where the time goes in v3:
time: 280 us; the launch traced here: 278 us
  waiting for transfers between devices  124 us (44%)
  Pallas kernels  87 us (31%)
  starting transfers between devices  30.9 us (11%)
  between operations  15.6 us (6%)
  matrix products  9.05 us (3%)
  local copies, waits for them, and re-layouts  6.47 us (2%)
  other arithmetic  4.65 us (2%)
    reduce_scatter x1, waiting for transfers between devices, gradient_rows(): lax.psum_scatter(total, ('seq_0', 'seq_1'), scatter_dimension=0, tiled=True)  75 us
    ppermute x4, waiting for transfers between devices, hop(): return lax.ppermute(sent, axis, CYCLES[which])  30.3 us
    pallas_call x5, Pallas kernels, placed_call(): pl.pallas_call(body, grid_spec=pltpu.PrefetchScalarGridSpec(num_scalar_pr...  24.8 us
    pallas_call x1, Pallas kernels, back_inside(): call(back_body, (HEADS // GROUP,), [PAIR_SPEC] * 5 + [STATE_SPEC, SCORE_S...  14.7 us
    pallas_call x1, Pallas kernels, norm_back(): call(norm_back_body, (CHUNKS,), [whole, spec((CHUNK, FEATURES), lambda i:...  14 us
    all_to_all x2, starting transfers between devices, scanned(): pieces = lax.all_to_all(pieces, SEQ, 0, 0, tiled=True)  13.1 us
    all_to_all x2, starting transfers between devices, scanned(): sums = lax.all_to_all(sums, SEQ, 0, 0, tiled=True)  11.3 us
    all_to_all x2, waiting for transfers between devices, scanned(): pieces = lax.all_to_all(pieces, SEQ, 0, 0, tiled=True)  11.1 us
  transfers between devices with their start and end apart: 12, of which 9 were waited for; matrix products, arithmetic and copies ran while one was open for 4% of the time, Pallas kernels for 14%

profile of v3, /device:TPU:2, one launch (start us, length us, event | category | flops | bytes accessed | tf_op | source)
XLA Modules:
  0.0 277.6 jit_solution(1775237150242935755)
XLA Ops:
  8.0 4.7 %shard_map.101 = (bf16[512,2048]{1,0:T(8,128)(2,1)}, bf16[16,128,128]{2,1,0:T(8,128)(2,1)}) custom-call(bf16[512,2048]{1,0:T(8,128)(2,1)} %bitcast.20, bf16[512,2048]{1,0:T(8,128)(2,1)} %bitcast.22), custom_call_target="tpu_custom_call" | custom-call | flops 536870912 | bytes 7340032 | tf_op jit(solution)/shard_map/pallas_call | solution.py:99
  12.7 8.3 %all-to-all-start = ((bf16[32,64,128]{2,1,0:T(8,128)(2,1)}), bf16[32,64,128]{2,1,0:T(8,128)(2,1)S(1)}, u32[]{:S(2)}, u32[]{:S(2)}) async-start(bf16[32,64,128]{2,1,0:T(8,128)(2,1)} %bitcast.29), calls=%async_computation | async-start | bytes 1048576 | tf_op jit(solution)/shard_map/all_to_all | solution.py:163
  21.1 11.1 %all-to-all-done.a = bf16[32,64,128]{2,1,0:T(8,128)(2,1)S(1)} async-done(((bf16[32,64,128]{2,1,0:T(8,128)(2,1)}), bf16[32,64,128]{2,1,0:T(8,128)(2,1)S(1)}, u32[]{:S(2)}, u32[]{:S(2)}) %all-to-all-start) | async-done | bytes 524320 | tf_op jit(solution)/shard_map/all_to_all | solution.py:163
  32.2 0.8 copy-done.1
  32.9 1.8 shard_map.103
  34.7 4.1 %all-to-all-start.1 = ((bf16[32,64,128]{2,1,0:T(8,128)(2,1)}), bf16[32,64,128]{2,1,0:T(8,128)(2,1)S(1)}, u32[]{:S(2)}, u32[]{:S(2)}) async-start(bf16[32,64,128]{2,1,0:T(8,128)(2,1)} %shard_map.103), calls=%async_computation.1 | async-start | bytes 1048576 | tf_op jit(solution)/shard_map/all_to_all | solution.py:165
  38.9 0.0 reduce-scatter.2.cloned.1.call-start
  38.9 0.7 pad_add_fusion.place.refs_0_
  39.6 9.3 %shard_map.102 = (bf16[512,2048]{1,0:T(8,128)(2,1)}, f32[512,2048]{1,0:T(8,128)}, bf16[16,3,256,256]{3,2,1,0:T(8,128)(2,1)}) custom-call(bf16[512,2048]{1,0:T(8,128)(2,1)} %bitcast.35, bf16[512,2048]{1,0:T(8,128)(2,1)} %get-tuple-element.33.feat_key, bf16[512,2048]{1,0:T(8,128)(2,1)} %bitcast.23), custom_call_target="tpu_custom_call" | custom-call | flops 4294967296 | bytes 18874368 | tf_op jit(solution)/shard_map/pallas_call | solution.py:125
  48.9 1.0 all-to-all-done.1
  50.0 0.8 copy-done.3
  50.8 7.5 %shard_map.104 = (bf16[512,2048]{1,0:T(8,128)(2,1)}, bf16[2,1024,512]{2,1,0:T(8,128)(2,1)}, f32[512,2048]{1,0:T(8,128)}, f32[512,128]{1,0:T(8,128)}) custom-call(f32[512,2048]{1,0:T(8,128)} %get-tuple-element.34.inside, bf16[512,2048]{1,0:T(8,128)(2,1)} %get-tuple-element.35.feat_query, bf16[16,128,128]{2,1,0:T(8,128)(2,1)} %bitcast.26, f32[1,2048]{1,0:T(1,128)} %bitcast.31), custom_call_target="tpu_custom_call" | custom-call | flops 536870912 | bytes 15728640 | tf_op jit(solution)/shard_map/pallas_call | solution.py:202
  58.3 8.9 %shard_map.109 = (bf16[1024,1024]{1,0:T(8,128)(2,1)}, bf16[1024,1024]{1,0:T(8,128)(2,1)}, bf16[1024,1024]{1,0:T(8,128)(2,1)}, bf16[1024,1024]{1,0:T(8,128)(2,1)}) custom-call(s32[4]{0:T(128)} %pad_add_fusion.place.refs_0_, bf16[2,1024,512]{2,1,0:T(8,128)(2,1)} %get-tuple-element.48.mine.other, bf16[2,1024,512]{2,1,0:T(8,128)(2,1)} %get-tuple-element.48.mine.other, ...), custom_call_target="tpu_custom_call" | custom-call | flops 4294967296 | bytes 12582912 | tf_op jit(solution)/shard_map/pallas_call | solution.py:380
  67.2 0.8 collective-permute-start.3
  68.0 0.1 collective-permute-start
  68.1 4.0 %collective-permute-done.3.refs_2_ = bf16[1024,1024]{1,0:T(8,128)(2,1)} collective-permute-done((bf16[1024,1024]{1,0:T(8,128)(2,1)}, bf16[1024,1024]{1,0:T(8,128)(2,1)}, u32[]{:S(2)}, u32[]{:S(2)}) %collective-permute-start.3) | collective-permute-done | bytes 2097184 | tf_op jit(solution)/shard_map/ppermute | solution.py:419
  72.1 4.6 %shard_map.112 = (bf16[512,1024]{1,0:T(8,128)(2,1)}, bf16[512,1024]{1,0:T(8,128)(2,1)}) custom-call(s32[4]{0:T(128)} %pad_add_fusion.place.refs_0_, bf16[1024,1024]{1,0:T(8,128)(2,1)} %get-tuple-element.55.refs_1_, bf16[1024,1024]{1,0:T(8,128)(2,1)} %collective-permute-done.3.refs_2_), custom_call_target="tpu_custom_call" | custom-call | flops 67108864 | bytes 6291456 | tf_op jit(solution)/shard_map/pallas_call | solution.py:380
  76.7 1.5 collective-permute-start.4
  78.2 1.3 copy-done
  79.5 4.6 %shard_map.110 = (bf16[512,1024]{1,0:T(8,128)(2,1)}, bf16[512,1024]{1,0:T(8,128)(2,1)}) custom-call(s32[4]{0:T(128)} %pad_add_fusion.place.refs_0_, bf16[1024,1024]{1,0:T(8,128)(2,1)} %get-tuple-element.49.refs_1_, bf16[1024,1024]{1,0:T(8,128)(2,1)} %copy-done), custom_call_target="tpu_custom_call" | custom-call | flops 67108864 | bytes 6291456 | tf_op jit(solution)/shard_map/pallas_call | solution.py:380
  84.1 1.8 collective-permute-start.1
  85.9 16.4 %collective-permute-done.4.refs_2_ = bf16[512,1024]{1,0:T(8,128)(2,1)S(1)} collective-permute-done((bf16[512,1024]{1,0:T(8,128)(2,1)}, bf16[512,1024]{1,0:T(8,128)(2,1)S(1)}, u32[]{:S(2)}, u32[]{:S(2)}) %collective-permute-start.4) | collective-permute-done | bytes 1048608 | tf_op jit(solution)/shard_map/ppermute | solution.py:347
  102.4 1.0 copy-done.6
  103.4 3.3 %shard_map.113 = (bf16[256,1024]{1,0:T(8,128)(2,1)}, bf16[256,1024]{1,0:T(8,128)(2,1)}) custom-call(s32[4]{0:T(128)} %pad_add_fusion.place.refs_0_, bf16[512,1024]{1,0:T(8,128)(2,1)} %get-tuple-element.57.refs_1_, bf16[512,1024]{1,0:T(8,128)(2,1)} %copy-done.6), custom_call_target="tpu_custom_call" | custom-call | flops 67108864 | bytes 3145728 | tf_op jit(solution)/shard_map/pallas_call | solution.py:380
  106.7 1.7 collective-permute-start.5
  108.4 1.7 collective-permute-done.1.refs_2_
  110.1 1.0 copy-done.5
  111.1 3.3 %shard_map.111 = (bf16[256,1024]{1,0:T(8,128)(2,1)}, bf16[256,1024]{1,0:T(8,128)(2,1)}) custom-call(s32[4]{0:T(128)} %pad_add_fusion.place.refs_0_, bf16[512,1024]{1,0:T(8,128)(2,1)} %get-tuple-element.51.refs_1_, bf16[512,1024]{1,0:T(8,128)(2,1)} %copy-done.5), custom_call_target="tpu_custom_call" | custom-call | flops 67108864 | bytes 3145728 | tf_op jit(solution)/shard_map/pallas_call | solution.py:380
  114.4 0.5 collective-permute-start.2
  114.9 5.9 %collective-permute-done.5 = bf16[256,1024]{1,0:T(8,128)(2,1)S(1)} collective-permute-done((bf16[256,1024]{1,0:T(8,128)(2,1)}, bf16[256,1024]{1,0:T(8,128)(2,1)S(1)}, u32[]{:S(2)}, u32[]{:S(2)}) %collective-permute-start.5) | collective-permute-done | bytes 524320 | tf_op jit(solution)/shard_map/ppermute | solution.py:347
  120.8 0.2 add_convert_fusion
  121.0 6.2 %collective-permute-done.2 = bf16[256,1024]{1,0:T(8,128)(2,1)S(1)} collective-permute-done((bf16[256,1024]{1,0:T(8,128)(2,1)}, bf16[256,1024]{1,0:T(8,128)(2,1)S(1)}, u32[]{:S(2)}, u32[]{:S(2)}) %collective-permute-start.2) | collective-permute-done | bytes 524320 | tf_op jit(solution)/shard_map/ppermute | solution.py:347
  127.2 1.2 add_convert_fusion.1
  128.5 1.1 pad_maximum_fusion
  129.5 0.0 all-gather.2.cloned.1.call-start
  129.6 0.5 all-gather.2.cloned.1.call-update
  130.1 75.0 %reduce-scatter.2.cloned.1.call-done = bf16[16,2048]{1,0:T(8,128)(2,1)} async-done(((bf16[256,2048]{1,0:T(8,128)(2,1)}), bf16[16,2048]{1,0:T(8,128)(2,1)}) %reduce-scatter.2.cloned.1.call-update) | async-done | bytes 65552 | tf_op jit(solution)/shard_map/reduce_scatter | solution.py:451
  205.1 1.5 convert_element_type.33
  206.6 14.0 %shard_map.105 = (bf16[512,2048]{1,0:T(8,128)(2,1)}, bf16[16,128,128]{2,1,0:T(8,128)(2,1)}) custom-call(bf16[512,2048]{1,0:T(8,128)(2,1)} %bitcast.34, bf16[2048,2048]{1,0:T(8,128)(2,1)} %all-gather.2.cloned.1.call-done.weight, f32[512,2048]{1,0:T(8,128)} %get-tuple-element.38.normed, f32[512,128]{1,0:T(8,128)} %get-tuple-element.39.inverse, ...), custom_call_target="tpu_custom_call" | custom-call | flops 5368709120 | bytes 18874368 | tf_op jit(solution)/shard_map/pallas_call | solution.py:256
  220.6 4.7 %all-to-all-start.2 = ((bf16[32,64,128]{2,1,0:T(8,128)(2,1)}), bf16[32,64,128]{2,1,0:T(8,128)(2,1)S(1)}, u32[]{:S(2)}, u32[]{:S(2)}) async-start(bf16[32,64,128]{2,1,0:T(8,128)(2,1)} %bitcast.30), calls=%async_computation.2 | async-start | bytes 1048576 | tf_op jit(solution)/shard_map/all_to_all | solution.py:163
  225.4 14.7 %shard_map.106 = (bf16[512,2048]{1,0:T(8,128)(2,1)}, f32[512,2048]{1,0:T(8,128)}, f32[512,2048]{1,0:T(8,128)}) custom-call(bf16[512,2048]{1,0:T(8,128)(2,1)} %bitcast.36, bf16[512,2048]{1,0:T(8,128)(2,1)} %get-tuple-element.35.feat_query, bf16[512,2048]{1,0:T(8,128)(2,1)} %get-tuple-element.33.feat_key, bf16[512,2048]{1,0:T(8,128)(2,1)} %bitcast.24, ...), custom_call_target="tpu_custom_call" | custom-call | flops 12884901888 | bytes 20971520 | tf_op jit(solution)/shard_map/pallas_call | solution.py:304
  240.1 0.8 copy-done.2
  240.9 1.9 shard_map.107
  242.8 7.2 %all-to-all-start.3 = ((bf16[32,64,128]{2,1,0:T(8,128)(2,1)}), bf16[32,64,128]{2,1,0:T(8,128)(2,1)S(1)}, u32[]{:S(2)}, u32[]{:S(2)}) async-start(bf16[32,64,128]{2,1,0:T(8,128)(2,1)} %shard_map.107), calls=%async_computation.3 | async-start | bytes 1048576 | tf_op jit(solution)/shard_map/all_to_all | solution.py:165
  250.0 9.0 %fusion = bf16[1,512,2048]{2,1,0:T(8,128)(2,1)} fusion(bf16[512,2048]{1,0:T(8,128)(2,1)S(1)} %copy-done.8, bf16[2048,2048]{1,0:T(8,128)(2,1)} %all-gather.2.cloned.1.call-done.weight), kind=kOutput, calls=%fused_computation.1 | convolution fusion | flops 4296015872 | bytes 12582912 | tf_op jit(solution)/shard_map/dot_general | solution.py:32
  259.0 2.0 all-to-all-done.3
  261.1 0.8 copy-done.4
  261.8 8.3 %shard_map.108 = (bf16[512,2048]{1,0:T(8,128)(2,1)}, bf16[512,2048]{1,0:T(8,128)(2,1)}) custom-call(bf16[512,2048]{1,0:T(8,128)(2,1)} %bitcast.21, bf16[512,2048]{1,0:T(8,128)(2,1)} %get-tuple-element.33.feat_key, bf16[512,2048]{1,0:T(8,128)(2,1)} %bitcast.25, f32[512,2048]{1,0:T(8,128)} %get-tuple-element.43.part_key, ...), custom_call_target="tpu_custom_call" | custom-call | flops 1073741824 | bytes 18874368 | tf_op jit(solution)/shard_map/pallas_call | solution.py:324
  (15 shorter events, 0.0 us)
Async XLA Ops:
  12.7 19.4 %all-to-all-start = ((bf16[32,64,128]{2,1,0:T(8,128)(2,1)}), bf16[32,64,128]{2,1,0:T(8,128)(2,1)S(1)}, u32[]{:S(2)}, u32[]{:S(2)}) async-start(bf16[32,64,128]{2,1,0:T(8,128)(2,1)} %bitcast.29), calls=%async_computation | async-start | bytes 1048576 | tf_op jit(solution)/shard_map/all_to_all | solution.py:163
  32.2 0.8 copy-start.1
  34.7 15.2 %all-to-all-start.1 = ((bf16[32,64,128]{2,1,0:T(8,128)(2,1)}), bf16[32,64,128]{2,1,0:T(8,128)(2,1)S(1)}, u32[]{:S(2)}, u32[]{:S(2)}) async-start(bf16[32,64,128]{2,1,0:T(8,128)(2,1)} %shard_map.103), calls=%async_computation.1 | async-start | bytes 1048576 | tf_op jit(solution)/shard_map/all_to_all | solution.py:165
  38.9 166.2 %reduce-scatter.2.cloned.1.call-start = ((), (), s32[]{:S(2)}) async-start(), calls=%async_computation.6 | async-start | bytes 1114112 | tf_op jit(solution)/shard_map/reduce_scatter | solution.py:451
  50.0 0.8 copy-start.3
  67.2 4.9 %collective-permute-start.3 = (bf16[1024,1024]{1,0:T(8,128)(2,1)}, bf16[1024,1024]{1,0:T(8,128)(2,1)}, u32[]{:S(2)}, u32[]{:S(2)}) collective-permute-start(bf16[1024,1024]{1,0:T(8,128)(2,1)} %get-tuple-element.56), channel_id=1, source_target_pairs={{0,4},{4,0},{1,5},{5,1},{2,6},{6,2},{3,7},{7,3},{8,12},{12,8},{9,1... | collective-permute-start | bytes 6291464 | tf_op jit(solution)/shard_map/ppermute | solution.py:419
  68.0 10.2 %collective-permute-start = (bf16[1024,1024]{1,0:T(8,128)(2,1)}, bf16[1024,1024]{1,0:T(8,128)(2,1)S(1)}, u32[]{:S(2)}, u32[]{:S(2)}) collective-permute-start(bf16[1024,1024]{1,0:T(8,128)(2,1)} %get-tuple-element.50), channel_id=1, source_target_pairs={{0,4},{4,0},{1,5},{5,1},{2,6},{6,2},{3,7},{7,3},{8,12},{12,8},{9,1... | collective-permute-start | bytes 6291464 | tf_op jit(solution)/shard_map/ppermute | solution.py:419
  76.7 25.6 %collective-permute-start.4 = (bf16[512,1024]{1,0:T(8,128)(2,1)}, bf16[512,1024]{1,0:T(8,128)(2,1)S(1)}, u32[]{:S(2)}, u32[]{:S(2)}) collective-permute-start(bf16[512,1024]{1,0:T(8,128)(2,1)} %get-tuple-element.58), channel_id=1, source_target_pairs={{0,3},{3,0},{1,2},{2,1},{4,7},{7,4},{5,6},{6,5},{8,11},{11,8},{9,1... | collective-permute-start | bytes 3145736 | tf_op jit(solution)/shard_map/ppermute | solution.py:347
  78.2 1.3 copy-start
  84.1 26.0 %collective-permute-start.1 = (bf16[512,1024]{1,0:T(8,128)(2,1)}, bf16[512,1024]{1,0:T(8,128)(2,1)S(1)}, u32[]{:S(2)}, u32[]{:S(2)}) collective-permute-start(bf16[512,1024]{1,0:T(8,128)(2,1)} %get-tuple-element.52), channel_id=1, source_target_pairs={{0,1},{1,0},{2,3},{3,2},{4,5},{5,4},{6,7},{7,6},{8,9},{9,8},{10,11... | collective-permute-start | bytes 3145736 | tf_op jit(solution)/shard_map/ppermute | solution.py:347
  102.4 1.0 copy-start.6
  106.7 14.1 %copy-start.7 = (bf16[256,1024]{1,0:T(8,128)(2,1)S(1)}, bf16[256,1024]{1,0:T(8,128)(2,1)}, u32[]{:S(2)}) copy-start(bf16[256,1024]{1,0:T(8,128)(2,1)} %get-tuple-element.59) | copy-start | bytes 1572868
  106.7 14.1 %collective-permute-start.5 = (bf16[256,1024]{1,0:T(8,128)(2,1)}, bf16[256,1024]{1,0:T(8,128)(2,1)S(1)}, u32[]{:S(2)}, u32[]{:S(2)}) collective-permute-start(bf16[256,1024]{1,0:T(8,128)(2,1)} %get-tuple-element.60), channel_id=1, source_target_pairs={{0,1},{1,0},{2,3},{3,2},{4,5},{5,4},{6,7},{7,6},{8,9},{9,8},{10,11... | collective-permute-start | bytes 1572872 | tf_op jit(solution)/shard_map/ppermute | solution.py:347
  110.1 1.0 copy-start.5
  114.4 12.8 %collective-permute-start.2 = (bf16[256,1024]{1,0:T(8,128)(2,1)}, bf16[256,1024]{1,0:T(8,128)(2,1)S(1)}, u32[]{:S(2)}, u32[]{:S(2)}) collective-permute-start(bf16[256,1024]{1,0:T(8,128)(2,1)} %get-tuple-element.54), channel_id=1, source_target_pairs={{0,3},{3,0},{1,2},{2,1},{4,7},{7,4},{5,6},{6,5},{8,11},{11,8},{9,1... | collective-permute-start | bytes 1572872 | tf_op jit(solution)/shard_map/ppermute | solution.py:347
  129.5 77.1 %all-gather.2.cloned.1.call-start = ((), (), s32[]{:S(2)}) async-start(), calls=%async_computation.5 | async-start | bytes 8454144 | tf_op jit(solution)/shard_map/all_gather | solution.py:458
  220.6 19.5 %all-to-all-start.2 = ((bf16[32,64,128]{2,1,0:T(8,128)(2,1)}), bf16[32,64,128]{2,1,0:T(8,128)(2,1)S(1)}, u32[]{:S(2)}, u32[]{:S(2)}) async-start(bf16[32,64,128]{2,1,0:T(8,128)(2,1)} %bitcast.30), calls=%async_computation.2 | async-start | bytes 1048576 | tf_op jit(solution)/shard_map/all_to_all | solution.py:163
  240.1 9.9 %copy-start.8 = (bf16[512,2048]{1,0:T(8,128)(2,1)S(1)}, bf16[512,2048]{1,0:T(8,128)(2,1)}, u32[]{:S(2)}) copy-start(bf16[512,2048]{1,0:T(8,128)(2,1)} %get-tuple-element.37) | copy-start | bytes 6291460
  240.1 0.8 copy-start.2
  242.8 18.3 %all-to-all-start.3 = ((bf16[32,64,128]{2,1,0:T(8,128)(2,1)}), bf16[32,64,128]{2,1,0:T(8,128)(2,1)S(1)}, u32[]{:S(2)}, u32[]{:S(2)}) async-start(bf16[32,64,128]{2,1,0:T(8,128)(2,1)} %shard_map.107), calls=%async_computation.3 | async-start | bytes 1048576 | tf_op jit(solution)/shard_map/all_to_all | solution.py:165
  261.1 0.8 copy-start.4
Sparse Core Ops, SparseCore 0:
  129.7 75.4 reduce-scatter.1
Sparse Core Ops, SparseCore 1:
  133.2 68.1 all-gather.1

commit v4 on v3

--- a/solution.py
+++ b/solution.py
@@ -61,7 +61,7 @@
     return pl.BlockSpec(shape, index)
 
 
-def call(body, grid, in_specs, out_specs, out_shape, flops, moved, scratch=()):
+def call(body, grid, in_specs, out_specs, out_shape, flops, moved, scratch=(), limit=60):
     return pl.pallas_call(
         body,
         grid=grid,
@@ -69,12 +69,13 @@
         out_specs=out_specs,
         out_shape=out_shape,
         scratch_shapes=scratch,
-        compiler_params=pltpu.CompilerParams(vmem_limit_bytes=60 * 1024 * 1024),
+        compiler_params=pltpu.CompilerParams(vmem_limit_bytes=limit * 1024 * 1024),
         cost_estimate=pl.CostEstimate(flops=flops, bytes_accessed=moved, transcendentals=0),
     )
 
 
 COLORS = 2
+STRIPES = 4
 WIDTH = FEATURES // COLORS
 SLAB = 16
 PLACES = 64
@@ -152,6 +153,7 @@
         jax.ShapeDtypeStruct(pieces.shape, BF16),
         1 << 23,
         MIB,
+        limit=8,
     )(pieces)
 
 
@@ -347,16 +349,16 @@
     return lax.ppermute(sent, axis, CYCLES[which])
 
 
-def product_body(place, mine, other, right, *outs):
-    for left, parts in ((other, outs[:COLORS]), (mine, outs[COLORS:])):
-        for c, out in enumerate(parts):
-            out[...] = dot_nn(left[0], right[:, c * WIDTH : (c + 1) * WIDTH]).astype(BF16)
+def product_body(place, left, right, *outs):
+    for c, out in enumerate(outs):
+        out[...] = dot_nn(left[0], right[:, c * WIDTH : (c + 1) * WIDTH]).astype(BF16)
 
 
 def slab_at(color, side, s):
     other, rest = s // 16, s % 16
+    y, z = rest // 4, on_ring((rest % 4) // 2, rest % 2)
     x = on_ring(side, other) if color == 0 else on_ring(other, side)
-    return pl.multiple_of((rest * 4 + x) * SLAB, SLAB)
+    return pl.multiple_of((y * 16 + z * 4 + x) * SLAB, SLAB)
 
 
 def first_body(color, place, mine, got, kept, sent):
@@ -376,14 +378,21 @@
         out[...] = (kept[at].astype(F32) + got[at].astype(F32)).astype(BF16)
 
 
+def third_body(place, kept0, got0, kept1, got1, out):
+    for c, (kept, got) in enumerate(((kept0, got0), (kept1, got1))):
+        total = kept[...].astype(F32) + got[...].astype(F32)
+        out[:, c * WIDTH : (c + 1) * WIDTH] = total.astype(BF16)
+
+
 def placed_call(body, place, args, in_specs, out_specs, out_shape, flops, moved, grid):
+    limit = 16 if flops == 1 << 26 else 60
     return pl.pallas_call(
         body,
         grid_spec=pltpu.PrefetchScalarGridSpec(
             num_scalar_prefetch=1, grid=(grid,), in_specs=in_specs, out_specs=out_specs
         ),
         out_shape=out_shape,
-        compiler_params=pltpu.CompilerParams(vmem_limit_bytes=60 * MIB),
+        compiler_params=pltpu.CompilerParams(vmem_limit_bytes=limit * MIB),
         cost_estimate=pl.CostEstimate(flops=flops, bytes_accessed=moved, transcendentals=0),
     )(place, *args)
 
@@ -396,39 +405,43 @@
     rows = half // 4
 
     def block(share):
-        return pl.BlockSpec((half // share, WIDTH), lambda i, p: (0, 0))
+        return pl.BlockSpec((half // share, WIDTH // STRIPES), lambda i, p: (0, i))
 
     def low(share):
         return jax.ShapeDtypeStruct((half // share, WIDTH), BF16)
 
-    products = placed_call(
-        product_body,
-        place,
-        (split, split, grad_result),
-        [
-            pl.BlockSpec((1, rows, BLOCK), lambda i, p: (p[0], i, 0)),
-            pl.BlockSpec((1, rows, BLOCK), lambda i, p: (p[1], i, 0)),
-            pl.BlockSpec((BLOCK, FEATURES), lambda i, p: (0, 0)),
-        ],
-        [pl.BlockSpec((rows, WIDTH), lambda i, p: (i, 0))] * (2 * COLORS),
-        [low(1)] * (2 * COLORS),
-        1 << 32,
-        12 * MIB,
-        4,
-    )
-    gots = [lax.ppermute(p, "seq_2", [(0, 1), (1, 0)]) for p in products[:COLORS]]
+    def products(which):
+        return placed_call(
+            product_body,
+            place,
+            (split, grad_result),
+            [
+                pl.BlockSpec((1, rows, BLOCK), lambda i, p: (p[which], i, 0)),
+                pl.BlockSpec((BLOCK, FEATURES), lambda i, p: (0, 0)),
+            ],
+            [pl.BlockSpec((rows, WIDTH), lambda i, p: (i, 0))] * COLORS,
+            [low(1)] * COLORS,
+            1 << 31,
+            7 * MIB,
+            half // rows,
+        )
+
+    gots = []
+    for sent in products(1):
+        gots.append(lax.ppermute(sent, "seq_2", [(0, 1), (1, 0)]))
+    mine = products(0)
     firsts = []
     for color in range(COLORS):
         kept, sent = placed_call(
             lambda *refs, color=color: first_body(color, *refs),
             place,
-            (products[COLORS + color], gots[color]),
+            (mine[color], gots[color]),
             [block(1)] * 2,
             [block(2)] * 2,
             [low(2)] * 2,
-            1 << 26,
+            1 << 27,
             6 * MIB,
-            1,
+            STRIPES,
         )
         firsts.append((kept, hop(sent, "dp", color)))
     seconds = []
@@ -442,14 +455,27 @@
             [low(4)] * 2,
             1 << 26,
             3 * MIB,
-            1,
+            STRIPES,
         )
         seconds.append((rest, hop(sent, "dp", 1 - color)))
-    total = jnp.concatenate(
-        [(rest.astype(F32) + got.astype(F32)).astype(BF16) for rest, got in seconds], axis=1
+    total = placed_call(
+        third_body,
+        place,
+        seconds[0] + seconds[1],
+        [pl.BlockSpec((half // 4, WIDTH), lambda i, p: (0, 0))] * 4,
+        pl.BlockSpec((half // 4, FEATURES), lambda i, p: (0, 0)),
+        jax.ShapeDtypeStruct((half // 4, FEATURES), BF16),
+        1 << 26,
+        3 * MIB,
+        1,
     )
-    total = lax.psum_scatter(total, ("seq_0", "seq_1"), scatter_dimension=0, tiled=True)
-    return total.astype(F32)
+    total = lax.psum_scatter(total, "seq_0", scatter_dimension=0, tiled=True)
+    for which, bit in enumerate(my_bits("seq_1")):
+        count = total.shape[0] // 2
+        kept = lax.dynamic_slice_in_dim(total, bit * count, count, 0).astype(F32)
+        sent = lax.dynamic_slice_in_dim(total, (1 - bit) * count, count, 0)
+        total = kept + hop(sent.astype(BF16), "seq_1", which).astype(F32)
+    return total
 
 
 def layer(query_input, key_input, value_input, grad_output, out_weight, norm_gain):

time: 280 us -> 270 us (0.964)
  waiting for transfers between devices: 124 us -> 111 us
  starting transfers between devices: 30.9 us -> 37.1 us
    reduce_scatter x1, waiting for transfers between devices: 75 us -> 23 us  [gradient_rows(): total = lax.psum_scatter(total, 'seq_0', scatter_dimension=0, tiled=True)]
    all_gather x1, waiting for transfers between devices: 0.01 us -> 34.9 us  [layer(): full_weight = lax.all_gather(out_weight, SEQ_DP, axis=0, tiled=True)]
    ppermute x4 -> x6, waiting for transfers between devices: 30.3 us -> 38.1 us  [hop(): return lax.ppermute(sent, axis, CYCLES[which])]
    ppermute x4 -> x6, starting transfers between devices: 5.48 us -> 11.6 us  [hop(): return lax.ppermute(sent, axis, CYCLES[which])]
    ppermute x2, waiting for transfers between devices: 4.05 us -> 0.01 us  [gradient_rows(): gots.append(lax.ppermute(sent, 'seq_2', [(0, 1), (1, 0)]))]
    unnamed x18 -> x14, local copies, waits for them, and re-layouts: 6.47 us -> 2.96 us
    convert_element_type x3 -> x0, other arithmetic: 2.92 us -> none  [the longest x1 1.5 us: gradient_rows(): return total.astype(F32)]
    pallas_call x5 -> x7, Pallas kernels: 24.8 us -> 27.2 us  [placed_call(): pl.pallas_call(body, grid_spec=pltpu.PrefetchScalarGridSpec(num_scalar_pr...]
  transfers between devices with their start and end apart: 12 -> 14, of which waited for: 9 -> 11; matrix products, arithmetic and copies ran while one was open for 4% -> 5% of each run, Pallas kernels for 14% -> 16%
where the time goes in v4:
time: 270 us; the launch traced here: 266 us
  waiting for transfers between devices  111 us (41%)
  Pallas kernels  87.5 us (32%)
  starting transfers between devices  37.1 us (14%)
  between operations  15.6 us (6%)
  matrix products  9.05 us (3%)
  local copies, waits for them, and re-layouts  3.89 us (1%)
    ppermute x6, waiting for transfers between devices, hop(): return lax.ppermute(sent, axis, CYCLES[which])  38.1 us
    all_gather x1, waiting for transfers between devices, layer(): full_weight = lax.all_gather(out_weight, SEQ_DP, axis=0, tiled=True)  34.9 us
    pallas_call x7, Pallas kernels, placed_call(): pl.pallas_call(body, grid_spec=pltpu.PrefetchScalarGridSpec(num_scalar_pr...  27.2 us
    reduce_scatter x1, waiting for transfers between devices, gradient_rows(): total = lax.psum_scatter(total, 'seq_0', scatter_dimension=0, tiled=True)  23 us
    pallas_call x1, Pallas kernels, back_inside(): call(back_body, (HEADS // GROUP,), [PAIR_SPEC] * 5 + [STATE_SPEC, SCORE_S...  14.7 us
    pallas_call x1, Pallas kernels, norm_back(): call(norm_back_body, (CHUNKS,), [whole, spec((CHUNK, FEATURES), lambda i:...  14 us
    all_to_all x2, starting transfers between devices, scanned(): pieces = lax.all_to_all(pieces, SEQ, 0, 0, tiled=True)  13.3 us
    ppermute x6, starting transfers between devices, hop(): return lax.ppermute(sent, axis, CYCLES[which])  11.6 us
  transfers between devices with their start and end apart: 14, of which 11 were waited for; matrix products, arithmetic and copies ran while one was open for 5% of the time, Pallas kernels for 16%

profile of v4, /device:TPU:2, one launch (start us, length us, event | category | flops | bytes accessed | tf_op | source)
XLA Modules:
  0.0 266.1 jit_solution(13588147779726839924)
XLA Ops:
  8.0 4.8 %shard_map.101 = (bf16[512,2048]{1,0:T(8,128)(2,1)}, bf16[16,128,128]{2,1,0:T(8,128)(2,1)}) custom-call(bf16[512,2048]{1,0:T(8,128)(2,1)} %bitcast.20, bf16[512,2048]{1,0:T(8,128)(2,1)} %bitcast.22), custom_call_target="tpu_custom_call" | custom-call | flops 536870912 | bytes 7340032 | tf_op jit(solution)/shard_map/pallas_call | solution.py:100
  12.7 8.3 %all-to-all-start = ((bf16[32,64,128]{2,1,0:T(8,128)(2,1)}), bf16[32,64,128]{2,1,0:T(8,128)(2,1)S(1)}, u32[]{:S(2)}, u32[]{:S(2)}) async-start(bf16[32,64,128]{2,1,0:T(8,128)(2,1)} %bitcast.29), calls=%async_computation | async-start | bytes 1048576 | tf_op jit(solution)/shard_map/all_to_all | solution.py:165
  21.1 11.1 %all-to-all-done.a = bf16[32,64,128]{2,1,0:T(8,128)(2,1)S(1)} async-done(((bf16[32,64,128]{2,1,0:T(8,128)(2,1)}), bf16[32,64,128]{2,1,0:T(8,128)(2,1)S(1)}, u32[]{:S(2)}, u32[]{:S(2)}) %all-to-all-start) | async-done | bytes 524320 | tf_op jit(solution)/shard_map/all_to_all | solution.py:165
  32.2 0.9 shard_map.103
  33.1 4.1 %all-to-all-start.1 = ((bf16[32,64,128]{2,1,0:T(8,128)(2,1)}), bf16[32,64,128]{2,1,0:T(8,128)(2,1)S(1)}, u32[]{:S(2)}, u32[]{:S(2)}) async-start(bf16[32,64,128]{2,1,0:T(8,128)(2,1)} %shard_map.103), calls=%async_computation.1 | async-start | bytes 1048576 | tf_op jit(solution)/shard_map/all_to_all | solution.py:167
  37.2 0.0 reduce-scatter.2.cloned.1.call-start
  37.3 0.6 pad_add_fusion.place.refs_0_
  37.8 9.2 %shard_map.102 = (bf16[512,2048]{1,0:T(8,128)(2,1)}, f32[512,2048]{1,0:T(8,128)}, bf16[16,3,256,256]{3,2,1,0:T(8,128)(2,1)}) custom-call(bf16[512,2048]{1,0:T(8,128)(2,1)} %bitcast.36, bf16[512,2048]{1,0:T(8,128)(2,1)} %get-tuple-element.33.feat_key, bf16[512,2048]{1,0:T(8,128)(2,1)} %bitcast.23), custom_call_target="tpu_custom_call" | custom-call | flops 4294967296 | bytes 18874368 | tf_op jit(solution)/shard_map/pallas_call | solution.py:126
  47.1 1.2 all-to-all-done.1
  48.3 0.8 copy-done.4
  49.1 7.5 %shard_map.104 = (bf16[512,2048]{1,0:T(8,128)(2,1)}, bf16[2,1024,512]{2,1,0:T(8,128)(2,1)}, f32[512,2048]{1,0:T(8,128)}, f32[512,128]{1,0:T(8,128)}) custom-call(f32[512,2048]{1,0:T(8,128)} %get-tuple-element.34.inside, bf16[512,2048]{1,0:T(8,128)(2,1)} %get-tuple-element.35.feat_query, bf16[16,128,128]{2,1,0:T(8,128)(2,1)} %bitcast.26, f32[1,2048]{1,0:T(1,128)} %bitcast.31), custom_call_target="tpu_custom_call" | custom-call | flops 536870912 | bytes 15728640 | tf_op jit(solution)/shard_map/pallas_call | solution.py:204
  56.6 6.5 %shard_map.110 = (bf16[1024,1024]{1,0:T(8,128)(2,1)}, bf16[1024,1024]{1,0:T(8,128)(2,1)}) custom-call(s32[4]{0:T(128)} %pad_add_fusion.place.refs_0_, bf16[2,1024,512]{2,1,0:T(8,128)(2,1)} %get-tuple-element.48.left, bf16[512,2048]{1,0:T(8,128)(2,1)} %bitcast.33), custom_call_target="tpu_custom_call" | custom-call | flops 2147483648 | bytes 7340032 | tf_op jit(solution)/shard_map/pallas_call | solution.py:389
  63.1 0.8 collective-permute-start
  63.9 6.5 %shard_map.109 = (bf16[1024,1024]{1,0:T(8,128)(2,1)}, bf16[1024,1024]{1,0:T(8,128)(2,1)}) custom-call(s32[4]{0:T(128)} %pad_add_fusion.place.refs_0_, bf16[2,1024,512]{2,1,0:T(8,128)(2,1)} %get-tuple-element.48.left, bf16[512,2048]{1,0:T(8,128)(2,1)} %bitcast.34), custom_call_target="tpu_custom_call" | custom-call | flops 2147483648 | bytes 7340032 | tf_op jit(solution)/shard_map/pallas_call | solution.py:389
  70.4 1.3 copy-done.3
  71.8 5.0 %shard_map.111 = (bf16[512,1024]{1,0:T(8,128)(2,1)}, bf16[512,1024]{1,0:T(8,128)(2,1)}) custom-call(s32[4]{0:T(128)} %pad_add_fusion.place.refs_0_, bf16[1024,1024]{1,0:T(8,128)(2,1)} %get-tuple-element.49.refs_1_, bf16[1024,1024]{1,0:T(8,128)(2,1)} %copy-done.3), custom_call_target="tpu_custom_call" | custom-call | flops 134217728 | bytes 6291456 | tf_op jit(solution)/shard_map/pallas_call | solution.py:389
  76.7 0.5 collective-permute-start.1
  77.3 5.0 %shard_map.113 = (bf16[512,1024]{1,0:T(8,128)(2,1)}, bf16[512,1024]{1,0:T(8,128)(2,1)}) custom-call(s32[4]{0:T(128)} %pad_add_fusion.place.refs_0_, bf16[1024,1024]{1,0:T(8,128)(2,1)} %get-tuple-element.55.refs_1_, bf16[1024,1024]{1,0:T(8,128)(2,1)} %collective-permute-done.3.refs_2_), custom_call_target="tpu_custom_call" | custom-call | flops 134217728 | bytes 6291456 | tf_op jit(solution)/shard_map/pallas_call | solution.py:389
  82.3 2.2 collective-permute-start.4
  84.4 18.1 %collective-permute-done.1.refs_2_ = bf16[512,1024]{1,0:T(8,128)(2,1)S(1)} collective-permute-done((bf16[512,1024]{1,0:T(8,128)(2,1)}, bf16[512,1024]{1,0:T(8,128)(2,1)S(1)}, u32[]{:S(2)}, u32[]{:S(2)}) %collective-permute-start.1) | collective-permute-done | bytes 1048608 | tf_op jit(solution)/shard_map/ppermute | solution.py:349
  102.5 1.2 shard_map.112
  103.8 1.6 collective-permute-start.2
  105.3 3.3 %collective-permute-done.4.refs_2_ = bf16[512,1024]{1,0:T(8,128)(2,1)S(1)} collective-permute-done((bf16[512,1024]{1,0:T(8,128)(2,1)}, bf16[512,1024]{1,0:T(8,128)(2,1)S(1)}, u32[]{:S(2)}, u32[]{:S(2)}) %collective-permute-start.4) | collective-permute-done | bytes 1048608 | tf_op jit(solution)/shard_map/ppermute | solution.py:349
  108.7 1.2 shard_map.114
  109.9 2.6 collective-permute-start.5
  112.6 6.9 %collective-permute-done.2.got0 = bf16[256,1024]{1,0:T(8,128)(2,1)S(1)} collective-permute-done((bf16[256,1024]{1,0:T(8,128)(2,1)S(1)}, bf16[256,1024]{1,0:T(8,128)(2,1)S(1)}, u32[]{:S(2)}, u32[]{:S(2)}) %collective-permute-start.2) | collective-permute-done | bytes 524320 | tf_op jit(solution)/shard_map/ppermute | solution.py:349
  119.4 3.8 %collective-permute-done.5.got1 = bf16[256,1024]{1,0:T(8,128)(2,1)S(1)} collective-permute-done((bf16[256,1024]{1,0:T(8,128)(2,1)S(1)}, bf16[256,1024]{1,0:T(8,128)(2,1)S(1)}, u32[]{:S(2)}, u32[]{:S(2)}) %collective-permute-start.5) | collective-permute-done | bytes 524320 | tf_op jit(solution)/shard_map/ppermute | solution.py:349
  123.3 1.7 shard_map.115
  125.1 0.0 all-gather.2.cloned.1.call-start
  125.1 0.5 all-gather.2.cloned.1.call-update
  125.6 23.0 %reduce-scatter.2.cloned.1.call-done = bf16[64,2048]{1,0:T(8,128)(2,1)} async-done(((bf16[256,2048]{1,0:T(8,128)(2,1)}), bf16[64,2048]{1,0:T(8,128)(2,1)}) %reduce-scatter.2.cloned.1.call-update) | async-done | bytes 262160 | tf_op jit(solution)/shard_map/reduce_scatter | solution.py:472
  148.6 0.9 constant_dynamic-slice_fusion
  149.5 1.6 collective-permute-start.6
  151.1 3.5 %collective-permute-done.6 = bf16[32,2048]{1,0:T(8,128)(2,1)S(1)} collective-permute-done((bf16[32,2048]{1,0:T(8,128)(2,1)S(1)}, bf16[32,2048]{1,0:T(8,128)(2,1)S(1)}, u32[]{:S(2)}, u32[]{:S(2)}) %collective-permute-start.6) | collective-permute-done | bytes 131104 | tf_op jit(solution)/shard_map/ppermute | solution.py:349
  154.6 0.9 convert_add_fusion
  155.6 3.1 %collective-permute-start.7 = (bf16[16,2048]{1,0:T(8,128)(2,1)S(1)}, bf16[16,2048]{1,0:T(8,128)(2,1)S(1)}, u32[]{:S(2)}, u32[]{:S(2)}) collective-permute-start(bf16[16,2048]{1,0:T(8,128)(2,1)S(1)} %dynamic-slice_convert_fusion), channel_id=1, source_target_pairs={{0,24},{24,0},{8,16},{16,8},{1,25},{25,1},{9,17},{17,9},{2,26},{26... | collective-permute-start | bytes 196616 | tf_op jit(solution)/shard_map/ppermute | solution.py:349
  158.6 2.5 collective-permute-done.7
  161.1 0.7 convert_add_fusion.1
  161.8 34.9 %all-gather.2.cloned.1.call-done.weight = bf16[2048,2048]{1,0:T(8,128)(2,1)} async-done(((bf16[16,2048]{1,0:T(8,128)(2,1)}), bf16[2048,2048]{1,0:T(8,128)(2,1)}) %all-gather.2.cloned.1.call-update) | async-done | bytes 8388624 | tf_op jit(solution)/shard_map/all_gather | solution.py:484
  196.7 14.0 %shard_map.105 = (bf16[512,2048]{1,0:T(8,128)(2,1)}, bf16[16,128,128]{2,1,0:T(8,128)(2,1)}) custom-call(bf16[512,2048]{1,0:T(8,128)(2,1)} %bitcast.35, bf16[2048,2048]{1,0:T(8,128)(2,1)} %all-gather.2.cloned.1.call-done.weight, f32[512,2048]{1,0:T(8,128)} %get-tuple-element.38.normed, f32[512,128]{1,0:T(8,128)} %get-tuple-element.39.inverse, ...), custom_call_target="tpu_custom_call" | custom-call | flops 5368709120 | bytes 18874368 | tf_op jit(solution)/shard_map/pallas_call | solution.py:258
  210.7 4.9 %all-to-all-start.2 = ((bf16[32,64,128]{2,1,0:T(8,128)(2,1)}), bf16[32,64,128]{2,1,0:T(8,128)(2,1)S(1)}, u32[]{:S(2)}, u32[]{:S(2)}) async-start(bf16[32,64,128]{2,1,0:T(8,128)(2,1)} %bitcast.30), calls=%async_computation.2 | async-start | bytes 1048576 | tf_op jit(solution)/shard_map/all_to_all | solution.py:165
  215.6 14.7 %shard_map.106 = (bf16[512,2048]{1,0:T(8,128)(2,1)}, f32[512,2048]{1,0:T(8,128)}, f32[512,2048]{1,0:T(8,128)}) custom-call(bf16[512,2048]{1,0:T(8,128)(2,1)} %bitcast.37, bf16[512,2048]{1,0:T(8,128)(2,1)} %get-tuple-element.35.feat_query, bf16[512,2048]{1,0:T(8,128)(2,1)} %get-tuple-element.33.feat_key, bf16[512,2048]{1,0:T(8,128)(2,1)} %bitcast.24, ...), custom_call_target="tpu_custom_call" | custom-call | flops 12884901888 | bytes 20971520 | tf_op jit(solution)/shard_map/pallas_call | solution.py:306
  230.4 0.9 shard_map.107
  231.3 7.2 %all-to-all-start.3 = ((bf16[32,64,128]{2,1,0:T(8,128)(2,1)}), bf16[32,64,128]{2,1,0:T(8,128)(2,1)S(1)}, u32[]{:S(2)}, u32[]{:S(2)}) async-start(bf16[32,64,128]{2,1,0:T(8,128)(2,1)} %shard_map.107), calls=%async_computation.3 | async-start | bytes 1048576 | tf_op jit(solution)/shard_map/all_to_all | solution.py:167
  238.5 9.0 %fusion = bf16[1,512,2048]{2,1,0:T(8,128)(2,1)} fusion(bf16[512,2048]{1,0:T(8,128)(2,1)S(1)} %copy-done.6, bf16[2048,2048]{1,0:T(8,128)(2,1)} %all-gather.2.cloned.1.call-done.weight), kind=kOutput, calls=%fused_computation.1 | convolution fusion | flops 4296015872 | bytes 12582912 | tf_op jit(solution)/shard_map/dot_general | solution.py:32
  247.5 2.0 all-to-all-done.3
  249.5 0.8 copy-done.5
  250.3 8.3 %shard_map.108 = (bf16[512,2048]{1,0:T(8,128)(2,1)}, bf16[512,2048]{1,0:T(8,128)(2,1)}) custom-call(bf16[512,2048]{1,0:T(8,128)(2,1)} %bitcast.21, bf16[512,2048]{1,0:T(8,128)(2,1)} %get-tuple-element.33.feat_key, bf16[512,2048]{1,0:T(8,128)(2,1)} %bitcast.25, f32[512,2048]{1,0:T(8,128)} %get-tuple-element.43.part_key, ...), custom_call_target="tpu_custom_call" | custom-call | flops 1073741824 | bytes 18874368 | tf_op jit(solution)/shard_map/pallas_call | solution.py:326
  (17 shorter events, 0.1 us)
Async XLA Ops:
  12.7 19.4 %all-to-all-start = ((bf16[32,64,128]{2,1,0:T(8,128)(2,1)}), bf16[32,64,128]{2,1,0:T(8,128)(2,1)S(1)}, u32[]{:S(2)}, u32[]{:S(2)}) async-start(bf16[32,64,128]{2,1,0:T(8,128)(2,1)} %bitcast.29), calls=%async_computation | async-start | bytes 1048576 | tf_op jit(solution)/shard_map/all_to_all | solution.py:165
  33.1 15.2 %all-to-all-start.1 = ((bf16[32,64,128]{2,1,0:T(8,128)(2,1)}), bf16[32,64,128]{2,1,0:T(8,128)(2,1)S(1)}, u32[]{:S(2)}, u32[]{:S(2)}) async-start(bf16[32,64,128]{2,1,0:T(8,128)(2,1)} %shard_map.103), calls=%async_computation.1 | async-start | bytes 1048576 | tf_op jit(solution)/shard_map/all_to_all | solution.py:167
  37.2 111.4 %reduce-scatter.2.cloned.1.call-start = ((), (), s32[]{:S(2)}) async-start(), calls=%async_computation.6 | async-start | bytes 1310720 | tf_op jit(solution)/shard_map/reduce_scatter | solution.py:472
  48.3 0.8 copy-start.4
  63.1 7.3 %collective-permute-start = (bf16[1024,1024]{1,0:T(8,128)(2,1)}, bf16[1024,1024]{1,0:T(8,128)(2,1)S(1)}, u32[]{:S(2)}, u32[]{:S(2)}) collective-permute-start(bf16[1024,1024]{1,0:T(8,128)(2,1)} %get-tuple-element.50), channel_id=1, source_target_pairs={{0,4},{4,0},{1,5},{5,1},{2,6},{6,2},{3,7},{7,3},{8,12},{12,8},{9,1... | collective-permute-start | bytes 6291464 | tf_op jit(solution)/shard_map/ppermute | solution.py:431
  63.9 13.3 %collective-permute-start.3 = (bf16[1024,1024]{1,0:T(8,128)(2,1)}, bf16[1024,1024]{1,0:T(8,128)(2,1)}, u32[]{:S(2)}, u32[]{:S(2)}) collective-permute-start(bf16[1024,1024]{1,0:T(8,128)(2,1)} %get-tuple-element.56), channel_id=1, source_target_pairs={{0,4},{4,0},{1,5},{5,1},{2,6},{6,2},{3,7},{7,3},{8,12},{12,8},{9,1... | collective-permute-start | bytes 6291464 | tf_op jit(solution)/shard_map/ppermute | solution.py:431
  70.4 1.3 copy-start.3
  76.7 25.8 %collective-permute-start.1 = (bf16[512,1024]{1,0:T(8,128)(2,1)}, bf16[512,1024]{1,0:T(8,128)(2,1)S(1)}, u32[]{:S(2)}, u32[]{:S(2)}) collective-permute-start(bf16[512,1024]{1,0:T(8,128)(2,1)} %get-tuple-element.52), channel_id=1, source_target_pairs={{0,1},{1,0},{2,3},{3,2},{4,5},{5,4},{6,7},{7,6},{8,9},{9,8},{10,11... | collective-permute-start | bytes 3145736 | tf_op jit(solution)/shard_map/ppermute | solution.py:349
  77.3 25.2 %copy-start = (bf16[512,1024]{1,0:T(8,128)(2,1)S(1)}, bf16[512,1024]{1,0:T(8,128)(2,1)}, u32[]{:S(2)}) copy-start(bf16[512,1024]{1,0:T(8,128)(2,1)} %get-tuple-element.51.refs_1_) | copy-start | bytes 3145732
  77.3 25.2 %copy-start.2 = (s32[4]{0:T(128)S(1)}, s32[4]{0:T(128)}, u32[]{:S(2)}) copy-start(s32[4]{0:T(128)} %pad_add_fusion.place.refs_0_) | copy-start | bytes 52
  82.3 26.4 %copy-start.1 = (bf16[512,1024]{1,0:T(8,128)(2,1)S(1)}, bf16[512,1024]{1,0:T(8,128)(2,1)}, u32[]{:S(2)}) copy-start(bf16[512,1024]{1,0:T(8,128)(2,1)} %get-tuple-element.57.refs_1_) | copy-start | bytes 3145732
  82.3 26.4 %collective-permute-start.4 = (bf16[512,1024]{1,0:T(8,128)(2,1)}, bf16[512,1024]{1,0:T(8,128)(2,1)S(1)}, u32[]{:S(2)}, u32[]{:S(2)}) collective-permute-start(bf16[512,1024]{1,0:T(8,128)(2,1)} %get-tuple-element.58), channel_id=1, source_target_pairs={{0,3},{3,0},{1,2},{2,1},{4,7},{7,4},{5,6},{6,5},{8,11},{11,8},{9,1... | collective-permute-start | bytes 3145736 | tf_op jit(solution)/shard_map/ppermute | solution.py:349
  103.8 15.7 %collective-permute-start.2 = (bf16[256,1024]{1,0:T(8,128)(2,1)S(1)}, bf16[256,1024]{1,0:T(8,128)(2,1)S(1)}, u32[]{:S(2)}, u32[]{:S(2)}) collective-permute-start(bf16[256,1024]{1,0:T(8,128)(2,1)S(1)} %get-tuple-element.54), channel_id=1, source_target_pairs={{0,3},{3,0},{1,2},{2,1},{4,7},{7,4},{5,6},{6,5},{8,11},{11,8},{9,1... | collective-permute-start | bytes 1572872 | tf_op jit(solution)/shard_map/ppermute | solution.py:349
  109.9 13.4 %collective-permute-start.5 = (bf16[256,1024]{1,0:T(8,128)(2,1)S(1)}, bf16[256,1024]{1,0:T(8,128)(2,1)S(1)}, u32[]{:S(2)}, u32[]{:S(2)}) collective-permute-start(bf16[256,1024]{1,0:T(8,128)(2,1)S(1)} %get-tuple-element.60), channel_id=1, source_target_pairs={{0,1},{1,0},{2,3},{3,2},{4,5},{5,4},{6,7},{7,6},{8,9},{9,8},{10,11... | collective-permute-start | bytes 1572872 | tf_op jit(solution)/shard_map/ppermute | solution.py:349
  125.1 71.6 %all-gather.2.cloned.1.call-start = ((), (), s32[]{:S(2)}) async-start(), calls=%async_computation.5 | async-start | bytes 8454144 | tf_op jit(solution)/shard_map/all_gather | solution.py:484
  149.5 5.0 %collective-permute-start.6 = (bf16[32,2048]{1,0:T(8,128)(2,1)S(1)}, bf16[32,2048]{1,0:T(8,128)(2,1)S(1)}, u32[]{:S(2)}, u32[]{:S(2)}) collective-permute-start(bf16[32,2048]{1,0:T(8,128)(2,1)S(1)} %constant_dynamic-slice_fusion), channel_id=1, source_target_pairs={{0,8},{8,0},{16,24},{24,16},{1,9},{9,1},{17,25},{25,17},{2,10},{10... | collective-permute-start | bytes 393224 | tf_op jit(solution)/shard_map/ppermute | solution.py:349
  155.6 5.6 %collective-permute-start.7 = (bf16[16,2048]{1,0:T(8,128)(2,1)S(1)}, bf16[16,2048]{1,0:T(8,128)(2,1)S(1)}, u32[]{:S(2)}, u32[]{:S(2)}) collective-permute-start(bf16[16,2048]{1,0:T(8,128)(2,1)S(1)} %dynamic-slice_convert_fusion), channel_id=1, source_target_pairs={{0,24},{24,0},{8,16},{16,8},{1,25},{25,1},{9,17},{17,9},{2,26},{26... | collective-permute-start | bytes 196616 | tf_op jit(solution)/shard_map/ppermute | solution.py:349
  210.7 19.7 %all-to-all-start.2 = ((bf16[32,64,128]{2,1,0:T(8,128)(2,1)}), bf16[32,64,128]{2,1,0:T(8,128)(2,1)S(1)}, u32[]{:S(2)}, u32[]{:S(2)}) async-start(bf16[32,64,128]{2,1,0:T(8,128)(2,1)} %bitcast.30), calls=%async_computation.2 | async-start | bytes 1048576 | tf_op jit(solution)/shard_map/all_to_all | solution.py:165
  230.3 8.1 %copy-start.6 = (bf16[512,2048]{1,0:T(8,128)(2,1)S(1)}, bf16[512,2048]{1,0:T(8,128)(2,1)}, u32[]{:S(2)}) copy-start(bf16[512,2048]{1,0:T(8,128)(2,1)} %get-tuple-element.37) | copy-start | bytes 6291460
  231.3 18.3 %all-to-all-start.3 = ((bf16[32,64,128]{2,1,0:T(8,128)(2,1)}), bf16[32,64,128]{2,1,0:T(8,128)(2,1)S(1)}, u32[]{:S(2)}, u32[]{:S(2)}) async-start(bf16[32,64,128]{2,1,0:T(8,128)(2,1)} %shard_map.107), calls=%async_computation.3 | async-start | bytes 1048576 | tf_op jit(solution)/shard_map/all_to_all | solution.py:167
  249.5 0.8 copy-start.5
Sparse Core Ops, SparseCore 0:
  125.2 23.4 reduce-scatter.1
Sparse Core Ops, SparseCore 1:
  128.7 67.9 all-gather.1

commit v5 on v4

--- a/solution.py
+++ b/solution.py
@@ -61,7 +61,7 @@
     return pl.BlockSpec(shape, index)
 
 
-def call(body, grid, in_specs, out_specs, out_shape, flops, moved, scratch=(), limit=60):
+def call(body, grid, in_specs, out_specs, out_shape, flops, moved, scratch=(), limit=60, aliases=()):
     return pl.pallas_call(
         body,
         grid=grid,
@@ -69,6 +69,7 @@
         out_specs=out_specs,
         out_shape=out_shape,
         scratch_shapes=scratch,
+        input_output_aliases=dict(aliases),
         compiler_params=pltpu.CompilerParams(vmem_limit_bytes=limit * 1024 * 1024),
         cost_estimate=pl.CostEstimate(flops=flops, bytes_accessed=moved, transcendentals=0),
     )
@@ -239,7 +240,7 @@
     products[...] += product[:, :HEAD_DIM] + product[:, HEAD_DIM:]
     hats[step] = hat
     norms[step] = normed[...]
-    feats[step] = feat_query[...]
+    feats[step] = feat_query[...].T
 
     @pl.when(step == CHUNKS - 1)
     def _():
@@ -249,7 +250,7 @@
             c, at = i // 2, head(i % 2)
             low = ((hats[c, :, at] - norms[c, :, at] * mean) * scale).astype(BF16)
             grad_att[:, head(i)] = low
-            state[i] = dot_tn(feats[c, :, at], low).astype(BF16)
+            state[i] = dot_nn(feats[c, at], low).astype(BF16)
 
 
 def norm_back(grad_result, weight, normed, inverse, gain, feat_query):
@@ -273,7 +274,7 @@
         scratch=[
             pltpu.VMEM((CHUNKS, BLOCK, CHUNK), F32),
             pltpu.VMEM((CHUNKS, BLOCK, CHUNK), F32),
-            pltpu.VMEM((CHUNKS, BLOCK, CHUNK), BF16),
+            pltpu.VMEM((CHUNKS, CHUNK, BLOCK), BF16),
             pltpu.VMEM((BLOCK, HEAD_DIM), F32),
         ],
     )(grad_result, weight, normed, inverse, gain, feat_query)
@@ -302,16 +303,39 @@
         grad_query[HALF:, at] = (fq1 * silu_slope(query[HALF:, at])).astype(BF16)
 
 
-def back_inside(query, feat_query, feat_key, value, grad, state, scores):
+ANY = pl.BlockSpec(memory_space=pl.ANY)
+
+
+def parted(body, args, out_shape, flops, moved, first, count, olds):
+    pair = spec((BLOCK, PAIR), lambda i: (0, i + first))
+    state = spec((GROUP, HEAD_DIM, HEAD_DIM), lambda i: (i + first, 0, 0))
+    score = spec((GROUP, 3, HALF, HALF), lambda i: (i + first, 0, 0, 0))
+    kinds = {2: pair, 3: state, 4: score}
+    given = len(args)
+
+    def run(*refs):
+        body(*refs[:given], *refs[given + len(olds) :])
+
     return call(
-        back_body,
-        (HEADS // GROUP,),
-        [PAIR_SPEC] * 5 + [STATE_SPEC, SCORE_SPEC],
-        [PAIR_SPEC] * 3,
-        [WIDE_LOW, WIDE, WIDE],
-        3 << 32,
-        20 * MIB,
-    )(query, feat_query, feat_key, value, grad, state, scores)
+        run,
+        (count,),
+        [kinds[a.ndim] for a in args] + [ANY] * len(olds),
+        [pair] * len(out_shape),
+        out_shape,
+        flops,
+        moved,
+        aliases=[(given + i, i) for i in range(len(olds))],
+    )(*args, *olds)
+
+
+STEPS = HEADS // GROUP
+BACK = 3
+FINAL = STEPS - 1
+
+
+def back_inside(args, first, count, olds=()):
+    shapes = [WIDE_LOW, WIDE, WIDE]
+    return parted(back_body, args, shapes, 3 << 30, 5 * MIB, first, count, olds)
 
 
 def finish_body(key, feat_key, value, part_key, part_value, later, grad_key, grad_value):
@@ -322,20 +346,9 @@
         grad_value[:, at] = (part_value[:, at] + dot_nn(feat_key[:, at], later[i])).astype(BF16)
 
 
-def finish(key, feat_key, value, part_key, part_value, later):
-    return call(
-        finish_body,
-        (HEADS // GROUP,),
-        [PAIR_SPEC] * 5 + [STATE_SPEC],
-        [PAIR_SPEC] * 2,
-        [WIDE_LOW, WIDE_LOW],
-        1 << 30,
-        18 * MIB,
-    )(key, feat_key, value, part_key, part_value, later)
-
-
-def on_ring(low, high):
-    return low + high * (3 - 2 * low)
+def finish(args, first, count, olds=()):
+    shapes = [WIDE_LOW, WIDE_LOW]
+    return parted(finish_body, args, shapes, 1 << 29, 9 * MIB, first, count, olds)
 
 
 def my_bits(axis):
@@ -349,33 +362,37 @@
     return lax.ppermute(sent, axis, CYCLES[which])
 
 
-def product_body(place, left, right, *outs):
-    for c, out in enumerate(outs):
-        out[...] = dot_nn(left[0], right[:, c * WIDTH : (c + 1) * WIDTH]).astype(BF16)
-
-
-def slab_at(color, side, s):
-    other, rest = s // 16, s % 16
-    y, z = rest // 4, on_ring((rest % 4) // 2, rest % 2)
-    x = on_ring(side, other) if color == 0 else on_ring(other, side)
-    return pl.multiple_of((y * 16 + z * 4 + x) * SLAB, SLAB)
+def product_body(place, left, right, out):
+    out[...] = dot_nn(left[0], right[...]).astype(BF16)
 
 
 def first_body(color, place, mine, got, kept, sent):
-    bit = place[2 + color]
-    for side, out in ((bit, kept), (1 - bit, sent)):
-        for s in range(PLACES // 2):
-            rows = pl.ds(slab_at(color, side, s), SLAB)
-            total = mine[rows].astype(F32) + got[rows].astype(F32)
-            out[s * SLAB : (s + 1) * SLAB] = total.astype(BF16)
+    turned = place[2 + color] == 1
+    places = PLACES // 4
+    for rest in range(places):
+        rows = slice(rest * 4 * SLAB, (rest + 1) * 4 * SLAB)
+        total = mine[rows].astype(F32) + got[rows].astype(F32)
+        x0, x1, x2, x3 = (total[i * SLAB : (i + 1) * SLAB] for i in range(4))
+        near = ((x0, x1), (x3, x2)) if color == 0 else ((x0, x3), (x1, x2))
+        for other, (low, high) in enumerate(near):
+            at = slice((other * places + rest) * SLAB, (other * places + rest + 1) * SLAB)
+            kept[at] = jnp.where(turned, high, low).astype(BF16)
+            sent[at] = jnp.where(turned, low, high).astype(BF16)
 
 
 def second_body(color, place, kept, got, rest, sent):
-    bit = place[2 + color]
+    turned = place[2 + color] == 1
     rows = kept.shape[0] // 2
-    for side, out in ((bit, rest), (1 - bit, sent)):
-        at = pl.ds(pl.multiple_of(side * rows, rows), rows)
-        out[...] = (kept[at].astype(F32) + got[at].astype(F32)).astype(BF16)
+    low = kept[:rows].astype(F32) + got[:rows].astype(F32)
+    high = kept[rows:].astype(F32) + got[rows:].astype(F32)
+    rest[...] = jnp.where(turned, high, low).astype(BF16)
+    sent[...] = jnp.where(turned, low, high).astype(BF16)
+
+
+def pick_body(place, rows, *outs):
+    for k, out in enumerate(outs):
+        at = (place[4] + k) % 4
+        out[...] = rows[pl.ds(pl.multiple_of(at * SLAB, SLAB), SLAB)]
 
 
 def third_body(place, kept0, got0, kept1, got1, out):
@@ -400,9 +417,9 @@
 def gradient_rows(split, grad_result):
     core = lax.axis_index("seq_2")
     bits = my_bits("dp")
-    place = jnp.stack([core, 1 - core, bits[0], bits[1]]).astype(jnp.int32)
+    ring = lax.axis_index("seq_1")
+    place = jnp.stack([core, 1 - core, bits[0], bits[1], ring]).astype(jnp.int32)
     half = FEATURES // 2
-    rows = half // 4
 
     def block(share):
         return pl.BlockSpec((half // share, WIDTH // STRIPES), lambda i, p: (0, i))
@@ -410,26 +427,27 @@
     def low(share):
         return jax.ShapeDtypeStruct((half // share, WIDTH), BF16)
 
-    def products(which):
+    def product(which, color):
+        columns = WIDTH // 2
         return placed_call(
             product_body,
             place,
             (split, grad_result),
             [
-                pl.BlockSpec((1, rows, BLOCK), lambda i, p: (p[which], i, 0)),
-                pl.BlockSpec((BLOCK, FEATURES), lambda i, p: (0, 0)),
+                pl.BlockSpec((1, half, BLOCK), lambda i, p: (p[which], 0, 0)),
+                pl.BlockSpec((BLOCK, columns), lambda i, p: (0, 2 * color + i)),
             ],
-            [pl.BlockSpec((rows, WIDTH), lambda i, p: (i, 0))] * COLORS,
-            [low(1)] * COLORS,
-            1 << 31,
-            7 * MIB,
-            half // rows,
+            pl.BlockSpec((half, columns), lambda i, p: (0, i)),
+            low(1),
+            1 << 30,
+            4 * MIB,
+            2,
         )
 
     gots = []
-    for sent in products(1):
-        gots.append(lax.ppermute(sent, "seq_2", [(0, 1), (1, 0)]))
-    mine = products(0)
+    for color in range(COLORS):
+        gots.append(lax.ppermute(product(1, color), "seq_2", [(0, 1), (1, 0)]))
+    mine = [product(0, color) for color in range(COLORS)]
     firsts = []
     for color in range(COLORS):
         kept, sent = placed_call(
@@ -470,11 +488,22 @@
         1,
     )
     total = lax.psum_scatter(total, "seq_0", scatter_dimension=0, tiled=True)
-    for which, bit in enumerate(my_bits("seq_1")):
-        count = total.shape[0] // 2
-        kept = lax.dynamic_slice_in_dim(total, bit * count, count, 0).astype(F32)
-        sent = lax.dynamic_slice_in_dim(total, (1 - bit) * count, count, 0)
-        total = kept + hop(sent.astype(BF16), "seq_1", which).astype(F32)
+    slab = pl.BlockSpec((SLAB, FEATURES), lambda i, p: (0, 0))
+    slabs = placed_call(
+        pick_body,
+        place,
+        (total,),
+        [pl.BlockSpec((4 * SLAB, FEATURES), lambda i, p: (0, 0))],
+        [slab] * 4,
+        [jax.ShapeDtypeStruct((SLAB, FEATURES), BF16)] * 4,
+        1 << 26,
+        MIB,
+        1,
+    )
+    total = slabs[0].astype(F32)
+    for k in range(1, 4):
+        got = lax.ppermute(slabs[k], "seq_1", [(i, (i + k) % 4) for i in range(4)])
+        total = total + got.astype(F32)
     return total
 
 
@@ -492,10 +521,12 @@
     )
     later = scanned(block_grad, True)
     result = dot_nn(mixed, full_weight).astype(BF16)
-    grad_query, part_key, part_value = back_inside(
-        query, feat_query, feat_key, value, grad_att, prefix, scores
-    )
-    grad_key, grad_value = finish(key, feat_key, value, part_key, part_value, later)
+    args = (query, feat_query, feat_key, value, grad_att, prefix, scores)
+    outs = back_inside(args, 0, BACK)
+    grad_query, part_key, part_value = back_inside(args, BACK, STEPS - BACK, outs)
+    args = (key, feat_key, value, part_key, part_value, later)
+    outs = finish(args, 0, FINAL)
+    grad_key, grad_value = finish(args, FINAL, STEPS - FINAL, outs)
     return (result[None], grad_query[None], grad_key[None], grad_value[None], grad_weight)
 
 

time: 270 us -> 279 us (1.033)
  blocking collectives: 0 us -> 19.4 us
  waiting for transfers between devices: 111 us -> 98.4 us
  Pallas kernels: 87.5 us -> 99.5 us
  starting transfers between devices: 37.1 us -> 28.3 us
    all_to_all x0 -> x1, blocking collectives: none -> 19.4 us  [scanned(): pieces = lax.all_to_all(pieces, SEQ, 0, 0, tiled=True)]
    all_to_all x2 -> x1, waiting for transfers between devices: 11.1 us -> 1.84 us  [scanned(): pieces = lax.all_to_all(pieces, SEQ, 0, 0, tiled=True)]
    all_to_all x2 -> x1, starting transfers between devices: 13.3 us -> 4.95 us  [scanned(): pieces = lax.all_to_all(pieces, SEQ, 0, 0, tiled=True)]
    pallas_call x7 -> x10, Pallas kernels: 27.2 us -> 33.3 us  [placed_call(): pl.pallas_call(body, grid_spec=pltpu.PrefetchScalarGridSpec(num_scalar_pr...]
    ppermute x6 -> x4, waiting for transfers between devices: 38.1 us -> 32 us  [hop(): return lax.ppermute(sent, axis, CYCLES[which])]
    ppermute x2 -> x5, starting transfers between devices: 0.79 us -> 6.72 us  [the longest x3 5.93 us: gradient_rows(): got = lax.ppermute(slabs[k], 'seq_1', [(i, (i + k) % 4) for i in range(4)])]
    pallas_call x2 -> x4, Pallas kernels: 23 us -> 28.9 us  [parted(): call(run, (count,), [kinds[a.ndim] for a in args] + [ANY] * len(olds), [p...]
    ppermute x6 -> x4, starting transfers between devices: 11.6 us -> 6.99 us  [hop(): return lax.ppermute(sent, axis, CYCLES[which])]
  transfers between devices with their start and end apart: 14 -> 14, of which waited for: 11 -> 10; matrix products, arithmetic and copies ran while one was open for 5% -> 4% of each run, Pallas kernels for 16% -> 20%
where the time goes in v5:
time: 279 us; the launch traced here: 275 us
  Pallas kernels  99.5 us (36%)
  waiting for transfers between devices  98.4 us (35%)
  starting transfers between devices  28.3 us (10%)
  blocking collectives  19.4 us (7%)
  between operations  15.6 us (6%)
  matrix products  9.05 us (3%)
  local copies, waits for them, and re-layouts  4.58 us (2%)
    all_gather x1, waiting for transfers between devices, layer(): full_weight = lax.all_gather(out_weight, SEQ_DP, axis=0, tiled=True)  36.9 us
    pallas_call x10, Pallas kernels, placed_call(): pl.pallas_call(body, grid_spec=pltpu.PrefetchScalarGridSpec(num_scalar_pr...  33.3 us
    ppermute x4, waiting for transfers between devices, hop(): return lax.ppermute(sent, axis, CYCLES[which])  32 us
    pallas_call x4, Pallas kernels, parted(): call(run, (count,), [kinds[a.ndim] for a in args] + [ANY] * len(olds), [p...  28.9 us
    reduce_scatter x1, waiting for transfers between devices, gradient_rows(): total = lax.psum_scatter(total, 'seq_0', scatter_dimension=0, tiled=True)  23.1 us
    all_to_all x1, blocking collectives, scanned(): pieces = lax.all_to_all(pieces, SEQ, 0, 0, tiled=True)  19.4 us
    pallas_call x1, Pallas kernels, norm_back(): call(norm_back_body, (CHUNKS,), [whole, spec((CHUNK, FEATURES), lambda i:...  14 us
    all_to_all x2, starting transfers between devices, scanned(): sums = lax.all_to_all(sums, SEQ, 0, 0, tiled=True)  9.51 us
  transfers between devices with their start and end apart: 14, of which 10 were waited for; matrix products, arithmetic and copies ran while one was open for 4% of the time, Pallas kernels for 20%

profile of v5, /device:TPU:2, one launch (start us, length us, event | category | flops | bytes accessed | tf_op | source)
XLA Modules:
  0.0 275.4 jit_solution(12538215218232008035)
XLA Ops:
  8.0 4.7 %shard_map.101 = (bf16[512,2048]{1,0:T(8,128)(2,1)}, bf16[16,128,128]{2,1,0:T(8,128)(2,1)}) custom-call(bf16[512,2048]{1,0:T(8,128)(2,1)} %bitcast.32, bf16[512,2048]{1,0:T(8,128)(2,1)} %bitcast.21), custom_call_target="tpu_custom_call" | custom-call | flops 536870912 | bytes 7340032 | tf_op jit(solution)/shard_map/pallas_call | solution.py:101
  12.7 19.4 %all_to_all.20.a = bf16[32,64,128]{2,1,0:T(8,128)(2,1)S(1)} all-to-all(bf16[32,64,128]{2,1,0:T(8,128)(2,1)} %bitcast.47), channel_id=1, replica_groups=mesh['seq_0'=4,'seq_1'=4,'seq_2'=2,'dp'=4] {'seq_0','seq_1','seq_2'}, dimensions={0} | all-to-all | bytes 1048576 | tf_op jit(solution)/shard_map/all_to_all | solution.py:166
  32.1 0.9 shard_map.103
  33.0 4.1 %all-to-all-start.1 = ((bf16[32,64,128]{2,1,0:T(8,128)(2,1)}), bf16[32,64,128]{2,1,0:T(8,128)(2,1)S(1)}, u32[]{:S(2)}, u32[]{:S(2)}) async-start(bf16[32,64,128]{2,1,0:T(8,128)(2,1)} %shard_map.103), calls=%async_computation.1 | async-start | bytes 1048576 | tf_op jit(solution)/shard_map/all_to_all | solution.py:168
  37.2 0.7 stack.31.place.refs_0_
  37.9 9.2 %shard_map.102 = (bf16[512,2048]{1,0:T(8,128)(2,1)}, f32[512,2048]{1,0:T(8,128)}, bf16[16,3,256,256]{3,2,1,0:T(8,128)(2,1)}) custom-call(bf16[512,2048]{1,0:T(8,128)(2,1)} %bitcast.38, bf16[512,2048]{1,0:T(8,128)(2,1)} %get-tuple-element.38.feat_key.refs_2_.refs_1_, bf16[512,2048]{1,0:T(8,128)(2,1)} %bitcast.22), custom_call_target="tpu_custom_call" | custom-call | flops 4294967296 | bytes 18874368 | tf_op jit(solution)/shard_map/pallas_call | solution.py:127
  47.2 1.1 all-to-all-done.1
  48.3 0.8 copy-done.4
  49.0 7.5 %shard_map.104 = (bf16[512,2048]{1,0:T(8,128)(2,1)}, bf16[2,1024,512]{2,1,0:T(8,128)(2,1)}, f32[512,2048]{1,0:T(8,128)}, f32[512,128]{1,0:T(8,128)}) custom-call(f32[512,2048]{1,0:T(8,128)} %get-tuple-element.39.inside, bf16[512,2048]{1,0:T(8,128)(2,1)} %get-tuple-element.40.feat_query.refs_1_, bf16[16,128,128]{2,1,0:T(8,128)(2,1)} %bitcast.35, ...), custom_call_target="tpu_custom_call" | custom-call | flops 536870912 | bytes 15728640 | tf_op jit(solution)/shard_map/pallas_call | solution.py:205
  56.5 4.6 %shard_map.112 = bf16[1024,1024]{1,0:T(8,128)(2,1)} custom-call(s32[5]{0:T(128)} %stack.31.place.refs_0_, bf16[2,1024,512]{2,1,0:T(8,128)(2,1)} %get-tuple-element.58.left, bf16[512,2048]{1,0:T(8,128)(2,1)} %bitcast.27), custom_call_target="tpu_custom_call" | custom-call | flops 1073741824 | bytes 4194304 | tf_op jit(solution)/shard_map/pallas_call | solution.py:406
  61.1 0.8 collective-permute-start
  61.9 4.5 %shard_map.116 = bf16[1024,1024]{1,0:T(8,128)(2,1)} custom-call(s32[5]{0:T(128)} %stack.31.place.refs_0_, bf16[2,1024,512]{2,1,0:T(8,128)(2,1)} %get-tuple-element.58.left, bf16[512,2048]{1,0:T(8,128)(2,1)} %bitcast.28), custom_call_target="tpu_custom_call" | custom-call | flops 1073741824 | bytes 4194304 | tf_op jit(solution)/shard_map/pallas_call | solution.py:406
  66.4 4.6 %shard_map.115.refs_1_ = bf16[1024,1024]{1,0:T(8,128)(2,1)} custom-call(s32[5]{0:T(128)} %stack.31.place.refs_0_, bf16[2,1024,512]{2,1,0:T(8,128)(2,1)} %get-tuple-element.58.left, bf16[512,2048]{1,0:T(8,128)(2,1)} %bitcast.29), custom_call_target="tpu_custom_call" | custom-call | flops 1073741824 | bytes 4194304 | tf_op jit(solution)/shard_map/pallas_call | solution.py:406
  71.0 4.5 %shard_map.111.refs_1_ = bf16[1024,1024]{1,0:T(8,128)(2,1)} custom-call(s32[5]{0:T(128)} %stack.31.place.refs_0_, bf16[2,1024,512]{2,1,0:T(8,128)(2,1)} %get-tuple-element.58.left, bf16[512,2048]{1,0:T(8,128)(2,1)} %bitcast.30), custom_call_target="tpu_custom_call" | custom-call | flops 1073741824 | bytes 4194304 | tf_op jit(solution)/shard_map/pallas_call | solution.py:406
  75.5 1.3 copy-done.6
  76.8 5.2 %shard_map.113 = (bf16[512,1024]{1,0:T(8,128)(2,1)}, bf16[512,1024]{1,0:T(8,128)(2,1)}) custom-call(s32[5]{0:T(128)} %stack.31.place.refs_0_, bf16[1024,1024]{1,0:T(8,128)(2,1)} %shard_map.111.refs_1_, bf16[1024,1024]{1,0:T(8,128)(2,1)} %copy-done.6), custom_call_target="tpu_custom_call" | custom-call | flops 134217728 | bytes 6291456 | tf_op jit(solution)/shard_map/pallas_call | solution.py:406
  82.0 0.6 collective-permute-start.1
  82.6 5.1 %shard_map.117 = (bf16[512,1024]{1,0:T(8,128)(2,1)}, bf16[512,1024]{1,0:T(8,128)(2,1)}) custom-call(s32[5]{0:T(128)} %stack.31.place.refs_0_, bf16[1024,1024]{1,0:T(8,128)(2,1)} %shard_map.115.refs_1_, bf16[1024,1024]{1,0:T(8,128)(2,1)} %collective-permute-done.3.refs_2_), custom_call_target="tpu_custom_call" | custom-call | flops 134217728 | bytes 6291456 | tf_op jit(solution)/shard_map/pallas_call | solution.py:406
  87.7 2.2 collective-permute-start.4
  89.8 18.0 %collective-permute-done.1.refs_2_ = bf16[512,1024]{1,0:T(8,128)(2,1)S(1)} collective-permute-done((bf16[512,1024]{1,0:T(8,128)(2,1)}, bf16[512,1024]{1,0:T(8,128)(2,1)S(1)}, u32[]{:S(2)}, u32[]{:S(2)}) %collective-permute-start.1) | collective-permute-done | bytes 1048608 | tf_op jit(solution)/shard_map/ppermute | solution.py:362
  107.8 1.3 shard_map.114
  109.2 1.6 collective-permute-start.2
  110.8 3.3 %collective-permute-done.4.refs_2_ = bf16[512,1024]{1,0:T(8,128)(2,1)S(1)} collective-permute-done((bf16[512,1024]{1,0:T(8,128)(2,1)}, bf16[512,1024]{1,0:T(8,128)(2,1)S(1)}, u32[]{:S(2)}, u32[]{:S(2)}) %collective-permute-start.4) | collective-permute-done | bytes 1048608 | tf_op jit(solution)/shard_map/ppermute | solution.py:362
  114.0 1.3 shard_map.118
  115.4 2.6 collective-permute-start.5
  118.0 6.8 %collective-permute-done.2.got0 = bf16[256,1024]{1,0:T(8,128)(2,1)S(1)} collective-permute-done((bf16[256,1024]{1,0:T(8,128)(2,1)S(1)}, bf16[256,1024]{1,0:T(8,128)(2,1)S(1)}, u32[]{:S(2)}, u32[]{:S(2)}) %collective-permute-start.2) | collective-permute-done | bytes 524320 | tf_op jit(solution)/shard_map/ppermute | solution.py:362
  124.8 3.9 %collective-permute-done.5.got1 = bf16[256,1024]{1,0:T(8,128)(2,1)S(1)} collective-permute-done((bf16[256,1024]{1,0:T(8,128)(2,1)S(1)}, bf16[256,1024]{1,0:T(8,128)(2,1)S(1)}, u32[]{:S(2)}, u32[]{:S(2)}) %collective-permute-start.5) | collective-permute-done | bytes 524320 | tf_op jit(solution)/shard_map/ppermute | solution.py:362
  128.7 1.7 shard_map.119
  131.1 23.1 %reduce-scatter.2.cloned.1.call-done.rows = bf16[64,2048]{1,0:T(8,128)(2,1)} async-done(((bf16[256,2048]{1,0:T(8,128)(2,1)}), bf16[64,2048]{1,0:T(8,128)(2,1)}) %reduce-scatter.2.cloned.1.call-update) | async-done | bytes 262160 | tf_op jit(solution)/shard_map/reduce_scatter | solution.py:490
  154.2 0.9 copy-done.2
  155.7 1.6 collective-permute-start.6
  157.3 2.9 %collective-permute-start.7 = (bf16[16,2048]{1,0:T(8,128)(2,1)S(1)}, bf16[16,2048]{1,0:T(8,128)(2,1)S(1)}, u32[]{:S(2)}, u32[]{:S(2)}) collective-permute-start(bf16[16,2048]{1,0:T(8,128)(2,1)S(1)} %get-tuple-element.69), channel_id=1, source_target_pairs={{0,16},{8,24},{16,0},{24,8},{1,17},{9,25},{17,1},{25,9},{2,18},{10... | collective-permute-start | bytes 196616 | tf_op jit(solution)/shard_map/ppermute | solution.py:505
  160.2 1.4 collective-permute-start.8
  161.6 1.5 collective-permute-done.7
  163.2 1.3 collective-permute-done.8
  164.5 0.7 convert_add_fusion
  165.2 36.9 %all-gather.2.cloned.1.call-done.weight = bf16[2048,2048]{1,0:T(8,128)(2,1)} async-done(((bf16[16,2048]{1,0:T(8,128)(2,1)}), bf16[2048,2048]{1,0:T(8,128)(2,1)}) %all-gather.2.cloned.1.call-update) | async-done | bytes 8388624 | tf_op jit(solution)/shard_map/all_gather | solution.py:513
  202.1 14.0 %shard_map.105 = (bf16[512,2048]{1,0:T(8,128)(2,1)}, bf16[16,128,128]{2,1,0:T(8,128)(2,1)}) custom-call(bf16[512,2048]{1,0:T(8,128)(2,1)} %bitcast.31, bf16[2048,2048]{1,0:T(8,128)(2,1)} %all-gather.2.cloned.1.call-done.weight, f32[512,2048]{1,0:T(8,128)} %get-tuple-element.43.normed, f32[512,128]{1,0:T(8,128)} %get-tuple-element.44.inverse, ...), custom_call_target="tpu_custom_call" | custom-call | flops 5368709120 | bytes 18874368 | tf_op jit(solution)/shard_map/pallas_call | solution.py:259
  216.1 4.9 %all-to-all-start.2 = ((bf16[32,64,128]{2,1,0:T(8,128)(2,1)}), bf16[32,64,128]{2,1,0:T(8,128)(2,1)S(1)}, u32[]{:S(2)}, u32[]{:S(2)}) async-start(bf16[32,64,128]{2,1,0:T(8,128)(2,1)} %bitcast.46), calls=%async_computation.2 | async-start | bytes 1048576 | tf_op jit(solution)/shard_map/all_to_all | solution.py:166
  221.0 9.0 %fusion = bf16[1,512,2048]{2,1,0:T(8,128)(2,1)} fusion(bf16[512,2048]{1,0:T(8,128)(2,1)S(1)} %copy-done.7, bf16[2048,2048]{1,0:T(8,128)(2,1)} %all-gather.2.cloned.1.call-done.weight), kind=kOutput, calls=%fused_computation.1 | convolution fusion | flops 4296015872 | bytes 12582912 | tf_op jit(solution)/shard_map/dot_general | solution.py:32
  230.1 1.8 all-to-all-done.2.a
  231.9 0.9 shard_map.108
  232.8 5.4 %all-to-all-start.3 = ((bf16[32,64,128]{2,1,0:T(8,128)(2,1)}), bf16[32,64,128]{2,1,0:T(8,128)(2,1)S(1)}, u32[]{:S(2)}, u32[]{:S(2)}) async-start(bf16[32,64,128]{2,1,0:T(8,128)(2,1)} %shard_map.108), calls=%async_computation.3 | async-start | bytes 1048576 | tf_op jit(solution)/shard_map/all_to_all | solution.py:168
  238.2 12.0 %shard_map.106 = (bf16[512,2048]{1,0:T(8,128)(2,1)}, f32[512,2048]{1,0:T(8,128)}, f32[512,2048]{1,0:T(8,128)}) custom-call(bf16[512,2048]{1,0:T(8,128)(2,1)} %bitcast.39, bf16[512,2048]{1,0:T(8,128)(2,1)} %get-tuple-element.40.feat_query.refs_1_, bf16[512,2048]{1,0:T(8,128)(2,1)} %get-tuple-element.38.feat_key.refs_2_.refs_1_, bf16[512,2048]{1,0:T(8,128)(2,1)} %bitcast.23, ...), custom_call_target="tpu_custom_call" | custom-call | flops 3221225472 | bytes 5242880 | tf_op jit(solution)/shard_map/pallas_call | solution.py:319
  250.2 6.2 %shard_map.107 = (bf16[512,2048]{1,0:T(8,128)(2,1)}, f32[512,2048]{1,0:T(8,128)}, f32[512,2048]{1,0:T(8,128)}) custom-call(bf16[512,2048]{1,0:T(8,128)(2,1)} %bitcast.40, bf16[512,2048]{1,0:T(8,128)(2,1)} %get-tuple-element.40.feat_query.refs_1_, ...), custom_call_target="tpu_custom_call", output_to_operand_aliasing={{0}: (7, {}), {1}: (8, {}), {2}: (9, {})} | custom-call | flops 3221225472 | bytes 5242880 | tf_op jit(solution)/shard_map/pallas_call | solution.py:319
  256.4 0.8 copy-done.5
  257.2 7.1 %shard_map.109 = (bf16[512,2048]{1,0:T(8,128)(2,1)}, bf16[512,2048]{1,0:T(8,128)(2,1)}) custom-call(bf16[512,2048]{1,0:T(8,128)(2,1)} %bitcast.33, bf16[512,2048]{1,0:T(8,128)(2,1)} %get-tuple-element.38.feat_key.refs_2_.refs_1_, bf16[512,2048]{1,0:T(8,128)(2,1)} %bitcast.25, f32[512,2048]{1,0:T(8,128)} %get-tuple-element.51.refs_3_, ...), custom_call_target="tpu_custom_call" | custom-call | flops 536870912 | bytes 9437184 | tf_op jit(solution)/shard_map/pallas_call | solution.py:319
  264.4 3.6 %shard_map.110 = (bf16[512,2048]{1,0:T(8,128)(2,1)}, bf16[512,2048]{1,0:T(8,128)(2,1)}) custom-call(bf16[512,2048]{1,0:T(8,128)(2,1)} %bitcast.34, bf16[512,2048]{1,0:T(8,128)(2,1)} %get-tuple-element.38.feat_key.refs_2_.refs_1_, bf16[512,2048]{1,0:T(8,128)(2,1)} %bitcast.26, ...), custom_call_target="tpu_custom_call", output_to_operand_aliasing={{0}: (6, {}), {1}: (7, {})} | custom-call | flops 536870912 | bytes 9437184 | tf_op jit(solution)/shard_map/pallas_call | solution.py:319
  (22 shorter events, 1.2 us)
Async XLA Ops:
  33.0 15.2 %all-to-all-start.1 = ((bf16[32,64,128]{2,1,0:T(8,128)(2,1)}), bf16[32,64,128]{2,1,0:T(8,128)(2,1)S(1)}, u32[]{:S(2)}, u32[]{:S(2)}) async-start(bf16[32,64,128]{2,1,0:T(8,128)(2,1)} %shard_map.103), calls=%async_computation.1 | async-start | bytes 1048576 | tf_op jit(solution)/shard_map/all_to_all | solution.py:168
  37.2 117.0 %reduce-scatter.2.cloned.1.call-start = ((), (), s32[]{:S(2)}) async-start(), calls=%async_computation.6 | async-start | bytes 1310720 | tf_op jit(solution)/shard_map/reduce_scatter | solution.py:490
  48.3 0.8 copy-start.4
  61.1 14.4 %collective-permute-start = (bf16[1024,1024]{1,0:T(8,128)(2,1)}, bf16[1024,1024]{1,0:T(8,128)(2,1)S(1)}, u32[]{:S(2)}, u32[]{:S(2)}) collective-permute-start(bf16[1024,1024]{1,0:T(8,128)(2,1)} %shard_map.112), channel_id=1, source_target_pairs={{0,4},{4,0},{1,5},{5,1},{2,6},{6,2},{3,7},{7,3},{8,12},{12,8},{9,1... | collective-permute-start | bytes 6291464 | tf_op jit(solution)/shard_map/ppermute | solution.py:449
  66.4 16.2 %collective-permute-start.3 = (bf16[1024,1024]{1,0:T(8,128)(2,1)}, bf16[1024,1024]{1,0:T(8,128)(2,1)}, u32[]{:S(2)}, u32[]{:S(2)}) collective-permute-start(bf16[1024,1024]{1,0:T(8,128)(2,1)} %shard_map.116), channel_id=1, source_target_pairs={{0,4},{4,0},{1,5},{5,1},{2,6},{6,2},{3,7},{7,3},{8,12},{12,8},{9,1... | collective-permute-start | bytes 6291464 | tf_op jit(solution)/shard_map/ppermute | solution.py:449
  75.5 1.3 copy-start.6
  82.0 25.9 %copy-start.1 = (bf16[512,1024]{1,0:T(8,128)(2,1)S(1)}, bf16[512,1024]{1,0:T(8,128)(2,1)}, u32[]{:S(2)}) copy-start(bf16[512,1024]{1,0:T(8,128)(2,1)} %get-tuple-element.59.refs_1_) | copy-start | bytes 3145732
  82.0 25.9 %copy-start.3 = (s32[5]{0:T(128)S(1)}, s32[5]{0:T(128)}, u32[]{:S(2)}) copy-start(s32[5]{0:T(128)} %stack.31.place.refs_0_) | copy-start | bytes 64
  82.0 25.9 %collective-permute-start.1 = (bf16[512,1024]{1,0:T(8,128)(2,1)}, bf16[512,1024]{1,0:T(8,128)(2,1)S(1)}, u32[]{:S(2)}, u32[]{:S(2)}) collective-permute-start(bf16[512,1024]{1,0:T(8,128)(2,1)} %get-tuple-element.60), channel_id=1, source_target_pairs={{0,1},{1,0},{2,3},{3,2},{4,5},{5,4},{6,7},{7,6},{8,9},{9,8},{10,11... | collective-permute-start | bytes 3145736 | tf_op jit(solution)/shard_map/ppermute | solution.py:362
  87.7 26.4 %copy-start = (bf16[512,1024]{1,0:T(8,128)(2,1)S(1)}, bf16[512,1024]{1,0:T(8,128)(2,1)}, u32[]{:S(2)}) copy-start(bf16[512,1024]{1,0:T(8,128)(2,1)} %get-tuple-element.63.refs_1_) | copy-start | bytes 3145732
  87.7 26.4 %collective-permute-start.4 = (bf16[512,1024]{1,0:T(8,128)(2,1)}, bf16[512,1024]{1,0:T(8,128)(2,1)S(1)}, u32[]{:S(2)}, u32[]{:S(2)}) collective-permute-start(bf16[512,1024]{1,0:T(8,128)(2,1)} %get-tuple-element.64), channel_id=1, source_target_pairs={{0,3},{3,0},{1,2},{2,1},{4,7},{7,4},{5,6},{6,5},{8,11},{11,8},{9,1... | collective-permute-start | bytes 3145736 | tf_op jit(solution)/shard_map/ppermute | solution.py:362
  109.2 15.6 %collective-permute-start.2 = (bf16[256,1024]{1,0:T(8,128)(2,1)S(1)}, bf16[256,1024]{1,0:T(8,128)(2,1)S(1)}, u32[]{:S(2)}, u32[]{:S(2)}) collective-permute-start(bf16[256,1024]{1,0:T(8,128)(2,1)S(1)} %get-tuple-element.62), channel_id=1, source_target_pairs={{0,3},{3,0},{1,2},{2,1},{4,7},{7,4},{5,6},{6,5},{8,11},{11,8},{9,1... | collective-permute-start | bytes 1572872 | tf_op jit(solution)/shard_map/ppermute | solution.py:362
  115.4 13.4 %collective-permute-start.5 = (bf16[256,1024]{1,0:T(8,128)(2,1)S(1)}, bf16[256,1024]{1,0:T(8,128)(2,1)S(1)}, u32[]{:S(2)}, u32[]{:S(2)}) collective-permute-start(bf16[256,1024]{1,0:T(8,128)(2,1)S(1)} %get-tuple-element.66), channel_id=1, source_target_pairs={{0,1},{1,0},{2,3},{3,2},{4,5},{5,4},{6,7},{7,6},{8,9},{9,8},{10,11... | collective-permute-start | bytes 1572872 | tf_op jit(solution)/shard_map/ppermute | solution.py:362
  130.5 71.6 %all-gather.2.cloned.1.call-start = ((), (), s32[]{:S(2)}) async-start(), calls=%async_computation.5 | async-start | bytes 8454144 | tf_op jit(solution)/shard_map/all_gather | solution.py:513
  154.2 1.0 copy-start.2
  155.7 5.9 %collective-permute-start.6 = (bf16[16,2048]{1,0:T(8,128)(2,1)S(1)}, bf16[16,2048]{1,0:T(8,128)(2,1)S(1)}, u32[]{:S(2)}, u32[]{:S(2)}) collective-permute-start(bf16[16,2048]{1,0:T(8,128)(2,1)S(1)} %get-tuple-element.68), channel_id=1, source_target_pairs={{0,8},{8,16},{16,24},{24,0},{1,9},{9,17},{17,25},{25,1},{2,10},{10... | collective-permute-start | bytes 196616 | tf_op jit(solution)/shard_map/ppermute | solution.py:505
  157.3 5.8 %collective-permute-start.7 = (bf16[16,2048]{1,0:T(8,128)(2,1)S(1)}, bf16[16,2048]{1,0:T(8,128)(2,1)S(1)}, u32[]{:S(2)}, u32[]{:S(2)}) collective-permute-start(bf16[16,2048]{1,0:T(8,128)(2,1)S(1)} %get-tuple-element.69), channel_id=1, source_target_pairs={{0,16},{8,24},{16,0},{24,8},{1,17},{9,25},{17,1},{25,9},{2,18},{10... | collective-permute-start | bytes 196616 | tf_op jit(solution)/shard_map/ppermute | solution.py:505
  160.2 4.3 %collective-permute-start.8 = (bf16[16,2048]{1,0:T(8,128)(2,1)S(1)}, bf16[16,2048]{1,0:T(8,128)(2,1)S(1)}, u32[]{:S(2)}, u32[]{:S(2)}) collective-permute-start(bf16[16,2048]{1,0:T(8,128)(2,1)S(1)} %get-tuple-element.70), channel_id=1, source_target_pairs={{0,24},{8,0},{16,8},{24,16},{1,25},{9,1},{17,9},{25,17},{2,26},{10... | collective-permute-start | bytes 196616 | tf_op jit(solution)/shard_map/ppermute | solution.py:505
  202.1 18.9 %copy-start.7 = (bf16[512,2048]{1,0:T(8,128)(2,1)S(1)}, bf16[512,2048]{1,0:T(8,128)(2,1)}, u32[]{:S(2)}) copy-start(bf16[512,2048]{1,0:T(8,128)(2,1)} %get-tuple-element.42) | copy-start | bytes 6291460
  216.1 15.8 %all-to-all-start.2 = ((bf16[32,64,128]{2,1,0:T(8,128)(2,1)}), bf16[32,64,128]{2,1,0:T(8,128)(2,1)S(1)}, u32[]{:S(2)}, u32[]{:S(2)}) async-start(bf16[32,64,128]{2,1,0:T(8,128)(2,1)} %bitcast.46), calls=%async_computation.2 | async-start | bytes 1048576 | tf_op jit(solution)/shard_map/all_to_all | solution.py:166
  232.8 23.6 %all-to-all-start.3 = ((bf16[32,64,128]{2,1,0:T(8,128)(2,1)}), bf16[32,64,128]{2,1,0:T(8,128)(2,1)S(1)}, u32[]{:S(2)}, u32[]{:S(2)}) async-start(bf16[32,64,128]{2,1,0:T(8,128)(2,1)} %shard_map.108), calls=%async_computation.3 | async-start | bytes 1048576 | tf_op jit(solution)/shard_map/all_to_all | solution.py:168
  256.4 0.8 copy-start.5
Sparse Core Ops, SparseCore 0:
  130.6 23.4 reduce-scatter.1
Sparse Core Ops, SparseCore 1:
  134.1 67.9 all-gather.1

commit v6 on v5

--- a/solution.py
+++ b/solution.py
@@ -215,6 +215,7 @@
         ],
         1 << 29,
         15 * MIB,
+        limit=60,
     )(inside, feat_query, state, gain)
 
 
@@ -277,6 +278,7 @@
             pltpu.VMEM((CHUNKS, CHUNK, BLOCK), BF16),
             pltpu.VMEM((BLOCK, HEAD_DIM), F32),
         ],
+        limit=60,
     )(grad_result, weight, normed, inverse, gain, feat_query)
 
 
@@ -290,13 +292,13 @@
         v0, v1 = value[:HALF, at], value[HALF:, at]
         g0, g1 = grad[:HALF, at], grad[HALF:, at]
         s00, s10, s11 = scores[i, 0], scores[i, 1], scores[i, 2]
-        part_value[:HALF, at] = dot_tn(s00, g0) + dot_tn(s10, g1)
-        part_value[HALF:, at] = dot_tn(s11, g1)
+        part_value[:HALF, at] = (dot_tn(s00, g0) + dot_tn(s10, g1)).astype(BF16)
+        part_value[HALF:, at] = dot_tn(s11, g1).astype(BF16)
         d00 = causal(dot_nt(g0, v0))
         d10 = dot_nt(g1, v0).astype(BF16)
         d11 = causal(dot_nt(g1, v1))
-        part_key[:HALF, at] = dot_tn(d00, q0) + dot_tn(d10, q1)
-        part_key[HALF:, at] = dot_tn(d11, q1)
+        part_key[:HALF, at] = (dot_tn(d00, q0) + dot_tn(d10, q1)).astype(BF16)
+        part_key[HALF:, at] = dot_tn(d11, q1).astype(BF16)
         fq0 = dot_nn(d00, k0) + dot_nt(g0, state[i])
         fq1 = dot_nn(d10, k0) + dot_nn(d11, k1) + dot_nt(g1, state[i])
         grad_query[:HALF, at] = (fq0 * silu_slope(query[:HALF, at])).astype(BF16)
@@ -330,20 +332,21 @@
 
 STEPS = HEADS // GROUP
 BACK = 3
-FINAL = STEPS - 1
+FINAL = STEPS // 2
 
 
 def back_inside(args, first, count, olds=()):
-    shapes = [WIDE_LOW, WIDE, WIDE]
+    shapes = [WIDE_LOW] * 3
     return parted(back_body, args, shapes, 3 << 30, 5 * MIB, first, count, olds)
 
 
 def finish_body(key, feat_key, value, part_key, part_value, later, grad_key, grad_value):
     for i in range(GROUP):
         at = head(i)
-        fk = part_key[:, at] + dot_nt(value[:, at], later[i])
+        fk = part_key[:, at].astype(F32) + dot_nt(value[:, at], later[i])
         grad_key[:, at] = (fk * silu_slope(key[:, at])).astype(BF16)
-        grad_value[:, at] = (part_value[:, at] + dot_nn(feat_key[:, at], later[i])).astype(BF16)
+        wide = part_value[:, at].astype(F32) + dot_nn(feat_key[:, at], later[i])
+        grad_value[:, at] = wide.astype(BF16)
 
 
 def finish(args, first, count, olds=()):
@@ -362,8 +365,14 @@
     return lax.ppermute(sent, axis, CYCLES[which])
 
 
-def product_body(place, left, right, out):
-    out[...] = dot_nn(left[0], right[...]).astype(BF16)
+def product_body(place, left, right, *outs):
+    step = pl.program_id(0)
+    low = dot_nn(left[0], right[...]).astype(BF16)
+    for c, out in enumerate(outs):
+
+        @pl.when(step // 2 == c)
+        def _():
+            out[...] = low
 
 
 def first_body(color, place, mine, got, kept, sent):
@@ -402,7 +411,7 @@
 
 
 def placed_call(body, place, args, in_specs, out_specs, out_shape, flops, moved, grid):
-    limit = 16 if flops == 1 << 26 else 60
+    limit = 16
     return pl.pallas_call(
         body,
         grid_spec=pltpu.PrefetchScalarGridSpec(
@@ -427,7 +436,7 @@
     def low(share):
         return jax.ShapeDtypeStruct((half // share, WIDTH), BF16)
 
-    def product(which, color):
+    def products(which):
         columns = WIDTH // 2
         return placed_call(
             product_body,
@@ -435,19 +444,22 @@
             (split, grad_result),
             [
                 pl.BlockSpec((1, half, BLOCK), lambda i, p: (p[which], 0, 0)),
-                pl.BlockSpec((BLOCK, columns), lambda i, p: (0, 2 * color + i)),
+                pl.BlockSpec((BLOCK, columns), lambda i, p: (0, i)),
             ],
-            pl.BlockSpec((half, columns), lambda i, p: (0, i)),
-            low(1),
-            1 << 30,
-            4 * MIB,
-            2,
+            [
+                pl.BlockSpec((half, columns), lambda i, p: (0, jnp.minimum(i, 1))),
+                pl.BlockSpec((half, columns), lambda i, p: (0, jnp.maximum(i - 2, 0))),
+            ],
+            [low(1)] * COLORS,
+            1 << 31,
+            7 * MIB,
+            4,
         )
 
     gots = []
-    for color in range(COLORS):
-        gots.append(lax.ppermute(product(1, color), "seq_2", [(0, 1), (1, 0)]))
-    mine = [product(0, color) for color in range(COLORS)]
+    for sent in products(1):
+        gots.append(lax.ppermute(sent, "seq_2", [(0, 1), (1, 0)]))
+    mine = products(0)
     firsts = []
     for color in range(COLORS):
         kept, sent = placed_call(

time: 279 us -> 259 us (0.928)
  Pallas kernels: 99.5 us -> 80.5 us
    pallas_call x10 -> x8, Pallas kernels: 33.3 us -> 17.7 us  [placed_call(): pl.pallas_call(body, grid_spec=pltpu.PrefetchScalarGridSpec(num_scalar_pr...]
    pallas_call x4, Pallas kernels: 28.9 us -> 25.4 us  [parted(): call(run, (count,), [kinds[a.ndim] for a in args] + [ANY] * len(olds), [p...]
  transfers between devices with their start and end apart: 14 -> 14, of which waited for: 10 -> 10; matrix products, arithmetic and copies ran while one was open for 4% -> 4% of each run, Pallas kernels for 20% -> 15%
where the time goes in v6:
time: 259 us; the launch traced here: 256 us
  waiting for transfers between devices  99.7 us (38%)
  Pallas kernels  80.5 us (31%)
  starting transfers between devices  26.8 us (10%)
  blocking collectives  19.4 us (7%)
  between operations  15.6 us (6%)
  matrix products  9.05 us (3%)
  local copies, waits for them, and re-layouts  4.21 us (2%)
    all_gather x1, waiting for transfers between devices, layer(): full_weight = lax.all_gather(out_weight, SEQ_DP, axis=0, tiled=True)  36.1 us
    ppermute x4, waiting for transfers between devices, hop(): return lax.ppermute(sent, axis, CYCLES[which])  32 us
    pallas_call x4, Pallas kernels, parted(): call(run, (count,), [kinds[a.ndim] for a in args] + [ANY] * len(olds), [p...  25.4 us
    reduce_scatter x1, waiting for transfers between devices, gradient_rows(): total = lax.psum_scatter(total, 'seq_0', scatter_dimension=0, tiled=True)  22.6 us
    all_to_all x1, blocking collectives, scanned(): pieces = lax.all_to_all(pieces, SEQ, 0, 0, tiled=True)  19.4 us
    pallas_call x8, Pallas kernels, placed_call(): pl.pallas_call(body, grid_spec=pltpu.PrefetchScalarGridSpec(num_scalar_pr...  17.7 us
    pallas_call x1, Pallas kernels, norm_back(): call(norm_back_body, (CHUNKS,), [whole, spec((CHUNK, FEATURES), lambda i:...  14 us
    all_to_all x2, starting transfers between devices, scanned(): sums = lax.all_to_all(sums, SEQ, 0, 0, tiled=True)  9.51 us
  transfers between devices with their start and end apart: 14, of which 10 were waited for; matrix products, arithmetic and copies ran while one was open for 4% of the time, Pallas kernels for 15%

profile of v6, /device:TPU:2, one launch (start us, length us, event | category | flops | bytes accessed | tf_op | source)
XLA Modules:
  0.0 256.1 jit_solution(12892509137843326699)
XLA Ops:
  8.0 4.7 %shard_map.101 = (bf16[512,2048]{1,0:T(8,128)(2,1)}, bf16[16,128,128]{2,1,0:T(8,128)(2,1)}) custom-call(bf16[512,2048]{1,0:T(8,128)(2,1)} %bitcast.30, bf16[512,2048]{1,0:T(8,128)(2,1)} %bitcast.24), custom_call_target="tpu_custom_call" | custom-call | flops 536870912 | bytes 7340032 | tf_op jit(solution)/shard_map/pallas_call | solution.py:101
  12.7 19.4 %all_to_all.20.a = bf16[32,64,128]{2,1,0:T(8,128)(2,1)S(1)} all-to-all(bf16[32,64,128]{2,1,0:T(8,128)(2,1)} %bitcast.45), channel_id=1, replica_groups=mesh['seq_0'=4,'seq_1'=4,'seq_2'=2,'dp'=4] {'seq_0','seq_1','seq_2'}, dimensions={0} | all-to-all | bytes 1048576 | tf_op jit(solution)/shard_map/all_to_all | solution.py:166
  32.1 0.9 shard_map.103
  33.0 4.1 %all-to-all-start.1 = ((bf16[32,64,128]{2,1,0:T(8,128)(2,1)}), bf16[32,64,128]{2,1,0:T(8,128)(2,1)S(1)}, u32[]{:S(2)}, u32[]{:S(2)}) async-start(bf16[32,64,128]{2,1,0:T(8,128)(2,1)} %shard_map.103), calls=%async_computation.1 | async-start | bytes 1048576 | tf_op jit(solution)/shard_map/all_to_all | solution.py:168
  37.3 9.2 %shard_map.102 = (bf16[512,2048]{1,0:T(8,128)(2,1)}, f32[512,2048]{1,0:T(8,128)}, bf16[16,3,256,256]{3,2,1,0:T(8,128)(2,1)}) custom-call(bf16[512,2048]{1,0:T(8,128)(2,1)} %bitcast.33, bf16[512,2048]{1,0:T(8,128)(2,1)} %get-tuple-element.42.feat_key.refs_2_.refs_1_, bf16[512,2048]{1,0:T(8,128)(2,1)} %bitcast.25), custom_call_target="tpu_custom_call" | custom-call | flops 4294967296 | bytes 18874368 | tf_op jit(solution)/shard_map/pallas_call | solution.py:127
  46.6 1.7 all-to-all-done.1
  48.3 0.8 copy-done.3
  49.1 7.6 %shard_map.104 = (bf16[512,2048]{1,0:T(8,128)(2,1)}, bf16[2,1024,512]{2,1,0:T(8,128)(2,1)}, f32[512,2048]{1,0:T(8,128)}, f32[512,128]{1,0:T(8,128)}) custom-call(f32[512,2048]{1,0:T(8,128)} %get-tuple-element.43.inside, bf16[512,2048]{1,0:T(8,128)(2,1)} %get-tuple-element.44.feat_query.refs_1_, bf16[16,128,128]{2,1,0:T(8,128)(2,1)} %bitcast.36, ...), custom_call_target="tpu_custom_call" | custom-call | flops 536870912 | bytes 15728640 | tf_op jit(solution)/shard_map/pallas_call | solution.py:205
  56.7 1.6 copy-done.2
  58.3 4.4 %shard_map.112 = (bf16[1024,1024]{1,0:T(8,128)(2,1)S(1)}, bf16[1024,1024]{1,0:T(8,128)(2,1)S(1)}) custom-call(s32[5]{0:T(128)S(1)} %stack.31.place.refs_0_, bf16[2,1024,512]{2,1,0:T(8,128)(2,1)S(1)} %copy-done.2, bf16[512,2048]{1,0:T(8,128)(2,1)S(1)} %bitcast.22), custom_call_target="tpu_custom_call" | custom-call | flops 2147483648 | bytes 7340032 | tf_op jit(solution)/shard_map/pallas_call | solution.py:415
  62.7 0.9 collective-permute-start
  63.5 0.1 collective-permute-start.3
  63.6 4.4 %shard_map.111 = (bf16[1024,1024]{1,0:T(8,128)(2,1)S(1)}, bf16[1024,1024]{1,0:T(8,128)(2,1)S(1)}) custom-call(s32[5]{0:T(128)S(1)} %stack.31.place.refs_0_, bf16[2,1024,512]{2,1,0:T(8,128)(2,1)S(1)} %copy-done.2, bf16[512,2048]{1,0:T(8,128)(2,1)S(1)} %bitcast.23), custom_call_target="tpu_custom_call" | custom-call | flops 2147483648 | bytes 7340032 | tf_op jit(solution)/shard_map/pallas_call | solution.py:415
  68.0 2.0 shard_map.113
  70.0 0.6 collective-permute-start.1
  70.7 2.0 shard_map.115
  72.7 2.2 collective-permute-start.4
  74.9 20.7 %collective-permute-done.1.refs_2_ = bf16[512,1024]{1,0:T(8,128)(2,1)S(1)} collective-permute-done((bf16[512,1024]{1,0:T(8,128)(2,1)S(1)}, bf16[512,1024]{1,0:T(8,128)(2,1)S(1)}, u32[]{:S(2)}, u32[]{:S(2)}) %collective-permute-start.1) | collective-permute-done | bytes 1048608 | tf_op jit(solution)/shard_map/ppermute | solution.py:365
  95.6 1.3 shard_map.114
  96.9 1.6 collective-permute-start.2
  98.5 1.3 shard_map.116
  99.9 2.2 collective-permute-start.5
  102.1 8.3 %collective-permute-done.2.got0 = bf16[256,1024]{1,0:T(8,128)(2,1)S(1)} collective-permute-done((bf16[256,1024]{1,0:T(8,128)(2,1)S(1)}, bf16[256,1024]{1,0:T(8,128)(2,1)S(1)}, u32[]{:S(2)}, u32[]{:S(2)}) %collective-permute-start.2) | collective-permute-done | bytes 524320 | tf_op jit(solution)/shard_map/ppermute | solution.py:365
  110.4 3.0 %collective-permute-done.5.got1 = bf16[256,1024]{1,0:T(8,128)(2,1)S(1)} collective-permute-done((bf16[256,1024]{1,0:T(8,128)(2,1)S(1)}, bf16[256,1024]{1,0:T(8,128)(2,1)S(1)}, u32[]{:S(2)}, u32[]{:S(2)}) %collective-permute-start.5) | collective-permute-done | bytes 524320 | tf_op jit(solution)/shard_map/ppermute | solution.py:365
  113.4 1.7 shard_map.117
  115.3 0.5 all-gather.2.cloned.1.call-update
  115.8 22.6 %reduce-scatter.2.cloned.1.call-done.rows = bf16[64,2048]{1,0:T(8,128)(2,1)} async-done(((bf16[256,2048]{1,0:T(8,128)(2,1)}), bf16[64,2048]{1,0:T(8,128)(2,1)}) %reduce-scatter.2.cloned.1.call-update) | async-done | bytes 262160 | tf_op jit(solution)/shard_map/reduce_scatter | solution.py:502
  138.4 0.9 copy-done
  139.3 0.6 shard_map.118
  139.9 3.1 %collective-permute-start.8 = (bf16[16,2048]{1,0:T(8,128)(2,1)S(1)}, bf16[16,2048]{1,0:T(8,128)(2,1)S(1)}, u32[]{:S(2)}, u32[]{:S(2)}) collective-permute-start(bf16[16,2048]{1,0:T(8,128)(2,1)S(1)} %get-tuple-element.78), channel_id=1, source_target_pairs={{0,24},{8,0},{16,8},{24,16},{1,25},{9,1},{17,9},{25,17},{2,26},{10... | collective-permute-start | bytes 196616 | tf_op jit(solution)/shard_map/ppermute | solution.py:517
  143.0 0.6 collective-permute-start.7
  143.6 1.0 collective-permute-start.6
  144.6 0.3 collective-permute-done.8
  144.9 3.9 %collective-permute-done.7 = bf16[16,2048]{1,0:T(8,128)(2,1)S(1)} collective-permute-done((bf16[16,2048]{1,0:T(8,128)(2,1)S(1)}, bf16[16,2048]{1,0:T(8,128)(2,1)S(1)}, u32[]{:S(2)}, u32[]{:S(2)}) %collective-permute-start.7) | collective-permute-done | bytes 65568 | tf_op jit(solution)/shard_map/ppermute | solution.py:517
  148.8 0.7 collective-permute-done.6
  149.4 0.7 convert_add_fusion
  150.1 36.1 %all-gather.2.cloned.1.call-done.weight = bf16[2048,2048]{1,0:T(8,128)(2,1)} async-done(((bf16[16,2048]{1,0:T(8,128)(2,1)}), bf16[2048,2048]{1,0:T(8,128)(2,1)}) %all-gather.2.cloned.1.call-update) | async-done | bytes 8388624 | tf_op jit(solution)/shard_map/all_gather | solution.py:525
  186.3 14.0 %shard_map.105 = (bf16[512,2048]{1,0:T(8,128)(2,1)}, bf16[16,128,128]{2,1,0:T(8,128)(2,1)}) custom-call(bf16[512,2048]{1,0:T(8,128)(2,1)} %bitcast.21, bf16[2048,2048]{1,0:T(8,128)(2,1)} %all-gather.2.cloned.1.call-done.weight, f32[512,2048]{1,0:T(8,128)} %get-tuple-element.47.normed, f32[512,128]{1,0:T(8,128)} %get-tuple-element.48.inverse, ...), custom_call_target="tpu_custom_call" | custom-call | flops 5368709120 | bytes 18874368 | tf_op jit(solution)/shard_map/pallas_call | solution.py:260
  200.3 4.9 %all-to-all-start.2 = ((bf16[32,64,128]{2,1,0:T(8,128)(2,1)}), bf16[32,64,128]{2,1,0:T(8,128)(2,1)S(1)}, u32[]{:S(2)}, u32[]{:S(2)}) async-start(bf16[32,64,128]{2,1,0:T(8,128)(2,1)} %bitcast.44), calls=%async_computation.2 | async-start | bytes 1048576 | tf_op jit(solution)/shard_map/all_to_all | solution.py:166
  205.2 9.0 %fusion = bf16[1,512,2048]{2,1,0:T(8,128)(2,1)} fusion(bf16[512,2048]{1,0:T(8,128)(2,1)S(1)} %copy-done.5, bf16[2048,2048]{1,0:T(8,128)(2,1)} %all-gather.2.cloned.1.call-done.weight), kind=kOutput, calls=%fused_computation.1 | convolution fusion | flops 4296015872 | bytes 12582912 | tf_op jit(solution)/shard_map/dot_general | solution.py:32
  214.3 1.8 all-to-all-done.2.a
  216.1 0.9 shard_map.108
  217.0 5.4 %all-to-all-start.3 = ((bf16[32,64,128]{2,1,0:T(8,128)(2,1)}), bf16[32,64,128]{2,1,0:T(8,128)(2,1)S(1)}, u32[]{:S(2)}, u32[]{:S(2)}) async-start(bf16[32,64,128]{2,1,0:T(8,128)(2,1)} %shard_map.108), calls=%async_computation.3 | async-start | bytes 1048576 | tf_op jit(solution)/shard_map/all_to_all | solution.py:168
  222.4 11.2 %shard_map.106 = (bf16[512,2048]{1,0:T(8,128)(2,1)}, bf16[512,2048]{1,0:T(8,128)(2,1)}, bf16[512,2048]{1,0:T(8,128)(2,1)}) custom-call(bf16[512,2048]{1,0:T(8,128)(2,1)} %bitcast.34, bf16[512,2048]{1,0:T(8,128)(2,1)} %get-tuple-element.44.feat_query.refs_1_, bf16[512,2048]{1,0:T(8,128)(2,1)} %get-tuple-element.42.feat_key.refs_2_.refs_1_, ...), custom_call_target="tpu_custom_call" | custom-call | flops 3221225472 | bytes 5242880 | tf_op jit(solution)/shard_map/pallas_call | solution.py:321
  233.6 5.9 %shard_map.107 = (bf16[512,2048]{1,0:T(8,128)(2,1)}, bf16[512,2048]{1,0:T(8,128)(2,1)}, bf16[512,2048]{1,0:T(8,128)(2,1)}) custom-call(bf16[512,2048]{1,0:T(8,128)(2,1)} %bitcast.35, bf16[512,2048]{1,0:T(8,128)(2,1)} %get-tuple-element.44.feat_query.refs_1_, ...), custom_call_target="tpu_custom_call", output_to_operand_aliasing={{0}: (7, {}), {1}: (8, {}), {2}: (9, {})} | custom-call | flops 3221225472 | bytes 5242880 | tf_op jit(solution)/shard_map/pallas_call | solution.py:321
  239.5 0.8 copy-done.4
  240.3 4.1 %shard_map.109 = (bf16[512,2048]{1,0:T(8,128)(2,1)}, bf16[512,2048]{1,0:T(8,128)(2,1)}) custom-call(bf16[512,2048]{1,0:T(8,128)(2,1)} %bitcast.31, bf16[512,2048]{1,0:T(8,128)(2,1)} %get-tuple-element.42.feat_key.refs_2_.refs_1_, bf16[512,2048]{1,0:T(8,128)(2,1)} %bitcast.28, bf16[512,2048]{1,0:T(8,128)(2,1)} %get-tuple-element.55.refs_3_, ...), custom_call_target="tpu_custom_call" | custom-call | flops 536870912 | bytes 9437184 | tf_op jit(solution)/shard_map/pallas_call | solution.py:321
  244.5 4.2 %shard_map.110 = (bf16[512,2048]{1,0:T(8,128)(2,1)}, bf16[512,2048]{1,0:T(8,128)(2,1)}) custom-call(bf16[512,2048]{1,0:T(8,128)(2,1)} %bitcast.32, bf16[512,2048]{1,0:T(8,128)(2,1)} %get-tuple-element.42.feat_key.refs_2_.refs_1_, bf16[512,2048]{1,0:T(8,128)(2,1)} %bitcast.29, ...), custom_call_target="tpu_custom_call", output_to_operand_aliasing={{0}: (6, {}), {1}: (7, {})} | custom-call | flops 536870912 | bytes 9437184 | tf_op jit(solution)/shard_map/pallas_call | solution.py:321
  (16 shorter events, 0.2 us)
Async XLA Ops:
  33.0 15.2 %all-to-all-start.1 = ((bf16[32,64,128]{2,1,0:T(8,128)(2,1)}), bf16[32,64,128]{2,1,0:T(8,128)(2,1)S(1)}, u32[]{:S(2)}, u32[]{:S(2)}) async-start(bf16[32,64,128]{2,1,0:T(8,128)(2,1)} %shard_map.103), calls=%async_computation.1 | async-start | bytes 1048576 | tf_op jit(solution)/shard_map/all_to_all | solution.py:168
  37.2 101.2 %reduce-scatter.2.cloned.1.call-start = ((), (), s32[]{:S(2)}) async-start(), calls=%async_computation.6 | async-start | bytes 1310720 | tf_op jit(solution)/shard_map/reduce_scatter | solution.py:502
  48.3 0.8 copy-start.3
  49.1 7.6 %copy-start.1 = (bf16[1,512,2048]{2,1,0:T(8,128)(2,1)S(1)}, bf16[1,512,2048]{2,1,0:T(8,128)(2,1)}, u32[]{:S(2)}) copy-start(bf16[1,512,2048]{2,1,0:T(8,128)(2,1)} %param.9) | copy-start | bytes 6291460
  56.7 1.6 copy-start.2
  62.7 5.3 %collective-permute-start = (bf16[1024,1024]{1,0:T(8,128)(2,1)S(1)}, bf16[1024,1024]{1,0:T(8,128)(2,1)S(1)}, u32[]{:S(2)}, u32[]{:S(2)}) collective-permute-start(bf16[1024,1024]{1,0:T(8,128)(2,1)S(1)} %get-tuple-element.64), channel_id=1, source_target_pairs={{0,4},{4,0},{1,5},{5,1},{2,6},{6,2},{3,7},{7,3},{8,12},{12,8},{9,1... | collective-permute-start | bytes 6291464 | tf_op jit(solution)/shard_map/ppermute | solution.py:461
  63.5 7.1 %collective-permute-start.3 = (bf16[1024,1024]{1,0:T(8,128)(2,1)S(1)}, bf16[1024,1024]{1,0:T(8,128)(2,1)S(1)}, u32[]{:S(2)}, u32[]{:S(2)}) collective-permute-start(bf16[1024,1024]{1,0:T(8,128)(2,1)S(1)} %get-tuple-element.70), channel_id=1, source_target_pairs={{0,4},{4,0},{1,5},{5,1},{2,6},{6,2},{3,7},{7,3},{8,12},{12,8},{9,1... | collective-permute-start | bytes 6291464 | tf_op jit(solution)/shard_map/ppermute | solution.py:461
  70.0 25.6 %collective-permute-start.1 = (bf16[512,1024]{1,0:T(8,128)(2,1)S(1)}, bf16[512,1024]{1,0:T(8,128)(2,1)S(1)}, u32[]{:S(2)}, u32[]{:S(2)}) collective-permute-start(bf16[512,1024]{1,0:T(8,128)(2,1)S(1)} %get-tuple-element.66), channel_id=1, source_target_pairs={{0,1},{1,0},{2,3},{3,2},{4,5},{5,4},{6,7},{7,6},{8,9},{9,8},{10,11... | collective-permute-start | bytes 3145736 | tf_op jit(solution)/shard_map/ppermute | solution.py:365
  72.7 25.8 %collective-permute-start.4 = (bf16[512,1024]{1,0:T(8,128)(2,1)S(1)}, bf16[512,1024]{1,0:T(8,128)(2,1)S(1)}, u32[]{:S(2)}, u32[]{:S(2)}) collective-permute-start(bf16[512,1024]{1,0:T(8,128)(2,1)S(1)} %get-tuple-element.72), channel_id=1, source_target_pairs={{0,3},{3,0},{1,2},{2,1},{4,7},{7,4},{5,6},{6,5},{8,11},{11,8},{9,1... | collective-permute-start | bytes 3145736 | tf_op jit(solution)/shard_map/ppermute | solution.py:365
  96.9 13.5 %collective-permute-start.2 = (bf16[256,1024]{1,0:T(8,128)(2,1)S(1)}, bf16[256,1024]{1,0:T(8,128)(2,1)S(1)}, u32[]{:S(2)}, u32[]{:S(2)}) collective-permute-start(bf16[256,1024]{1,0:T(8,128)(2,1)S(1)} %get-tuple-element.68), channel_id=1, source_target_pairs={{0,3},{3,0},{1,2},{2,1},{4,7},{7,4},{5,6},{6,5},{8,11},{11,8},{9,1... | collective-permute-start | bytes 1572872 | tf_op jit(solution)/shard_map/ppermute | solution.py:365
  99.9 13.6 %collective-permute-start.5 = (bf16[256,1024]{1,0:T(8,128)(2,1)S(1)}, bf16[256,1024]{1,0:T(8,128)(2,1)S(1)}, u32[]{:S(2)}, u32[]{:S(2)}) collective-permute-start(bf16[256,1024]{1,0:T(8,128)(2,1)S(1)} %get-tuple-element.74), channel_id=1, source_target_pairs={{0,1},{1,0},{2,3},{3,2},{4,5},{5,4},{6,7},{7,6},{8,9},{9,8},{10,11... | collective-permute-start | bytes 1572872 | tf_op jit(solution)/shard_map/ppermute | solution.py:365
  115.2 71.1 %all-gather.2.cloned.1.call-start = ((), (), s32[]{:S(2)}) async-start(), calls=%async_computation.5 | async-start | bytes 8454144 | tf_op jit(solution)/shard_map/all_gather | solution.py:525
  138.4 1.0 copy-start
  139.9 5.0 %collective-permute-start.8 = (bf16[16,2048]{1,0:T(8,128)(2,1)S(1)}, bf16[16,2048]{1,0:T(8,128)(2,1)S(1)}, u32[]{:S(2)}, u32[]{:S(2)}) collective-permute-start(bf16[16,2048]{1,0:T(8,128)(2,1)S(1)} %get-tuple-element.78), channel_id=1, source_target_pairs={{0,24},{8,0},{16,8},{24,16},{1,25},{9,1},{17,9},{25,17},{2,26},{10... | collective-permute-start | bytes 196616 | tf_op jit(solution)/shard_map/ppermute | solution.py:517
  143.0 5.8 %collective-permute-start.7 = (bf16[16,2048]{1,0:T(8,128)(2,1)S(1)}, bf16[16,2048]{1,0:T(8,128)(2,1)S(1)}, u32[]{:S(2)}, u32[]{:S(2)}) collective-permute-start(bf16[16,2048]{1,0:T(8,128)(2,1)S(1)} %get-tuple-element.77), channel_id=1, source_target_pairs={{0,16},{8,24},{16,0},{24,8},{1,17},{9,25},{17,1},{25,9},{2,18},{10... | collective-permute-start | bytes 196616 | tf_op jit(solution)/shard_map/ppermute | solution.py:517
  143.6 5.9 %collective-permute-start.6 = (bf16[16,2048]{1,0:T(8,128)(2,1)S(1)}, bf16[16,2048]{1,0:T(8,128)(2,1)S(1)}, u32[]{:S(2)}, u32[]{:S(2)}) collective-permute-start(bf16[16,2048]{1,0:T(8,128)(2,1)S(1)} %get-tuple-element.76), channel_id=1, source_target_pairs={{0,8},{8,16},{16,24},{24,0},{1,9},{9,17},{17,25},{25,1},{2,10},{10... | collective-permute-start | bytes 196616 | tf_op jit(solution)/shard_map/ppermute | solution.py:517
  186.3 19.0 %copy-start.5 = (bf16[512,2048]{1,0:T(8,128)(2,1)S(1)}, bf16[512,2048]{1,0:T(8,128)(2,1)}, u32[]{:S(2)}) copy-start(bf16[512,2048]{1,0:T(8,128)(2,1)} %get-tuple-element.46) | copy-start | bytes 6291460
  200.3 15.8 %all-to-all-start.2 = ((bf16[32,64,128]{2,1,0:T(8,128)(2,1)}), bf16[32,64,128]{2,1,0:T(8,128)(2,1)S(1)}, u32[]{:S(2)}, u32[]{:S(2)}) async-start(bf16[32,64,128]{2,1,0:T(8,128)(2,1)} %bitcast.44), calls=%async_computation.2 | async-start | bytes 1048576 | tf_op jit(solution)/shard_map/all_to_all | solution.py:166
  217.0 22.5 %all-to-all-start.3 = ((bf16[32,64,128]{2,1,0:T(8,128)(2,1)}), bf16[32,64,128]{2,1,0:T(8,128)(2,1)S(1)}, u32[]{:S(2)}, u32[]{:S(2)}) async-start(bf16[32,64,128]{2,1,0:T(8,128)(2,1)} %shard_map.108), calls=%async_computation.3 | async-start | bytes 1048576 | tf_op jit(solution)/shard_map/all_to_all | solution.py:168
  239.5 0.8 copy-start.4
Sparse Core Ops, SparseCore 0:
  115.3 22.9 reduce-scatter.1
Sparse Core Ops, SparseCore 1:
  118.8 67.4 all-gather.1

commit v7 on v6

--- a/solution.py
+++ b/solution.py
@@ -221,6 +221,7 @@
 
 CHUNK = 2 * HEAD_DIM
 CHUNKS = FEATURES // CHUNK
+AHEAD = 3
 
 
 CHUNK = 2 * HEAD_DIM
@@ -228,15 +229,27 @@
 
 
 def norm_back_body(
-    grad, weight, normed, inverse, gain, feat_query, grad_att, state, hats, norms, feats, products
+    grad, weight, normed, inverse, gain, feat_query, grad_att, state,
+    weights, hats, norms, feats, products, sems
 ):
     step = pl.program_id(0)
 
+    def arriving(c):
+        rows = pl.ds(pl.multiple_of(c * CHUNK, CHUNK), CHUNK)
+        return pltpu.make_async_copy(weight.at[rows], weights.at[c], sems.at[c])
+
     @pl.when(step == 0)
     def _():
+        for c in range(AHEAD):
+            arriving(c).start()
         products[...] = jnp.zeros_like(products)
 
-    hat = dot_nt(grad[...], weight[...]) * gain[...]
+    @pl.when(step + AHEAD < CHUNKS)
+    def _():
+        arriving(step + AHEAD).start()
+
+    arriving(step).wait()
+    hat = dot_nt(grad[...], weights[step]) * gain[...]
     product = hat * normed[...]
     products[...] += product[:, :HEAD_DIM] + product[:, HEAD_DIM:]
     hats[step] = hat
@@ -262,7 +275,7 @@
         (CHUNKS,),
         [
             whole,
-            spec((CHUNK, FEATURES), lambda i: (i, 0)),
+            pl.BlockSpec(memory_space=pltpu.HBM),
             part,
             spec((BLOCK, HEAD_DIM), lambda i: (0, 0)),
             spec((1, CHUNK), lambda i: (0, i)),
@@ -273,10 +286,12 @@
         5 << 30,
         18 * MIB,
         scratch=[
+            pltpu.VMEM((CHUNKS, CHUNK, FEATURES), BF16),
             pltpu.VMEM((CHUNKS, BLOCK, CHUNK), F32),
             pltpu.VMEM((CHUNKS, BLOCK, CHUNK), F32),
             pltpu.VMEM((CHUNKS, CHUNK, BLOCK), BF16),
             pltpu.VMEM((BLOCK, HEAD_DIM), F32),
+            pltpu.SemaphoreType.DMA((CHUNKS,)),
         ],
         limit=60,
     )(grad_result, weight, normed, inverse, gain, feat_query)

time: 259 us -> 260 us (level)
  no operation moved by 1% of the time
where the time goes in v7:
time: 260 us; the launch traced here: 256 us
  waiting for transfers between devices  99.7 us (38%)
  Pallas kernels  80.6 us (31%)
  starting transfers between devices  26.9 us (10%)
  blocking collectives  19.4 us (7%)
  between operations  15.6 us (6%)
  matrix products  9.05 us (3%)
  local copies, waits for them, and re-layouts  4.21 us (2%)
    all_gather x1, waiting for transfers between devices, layer(): full_weight = lax.all_gather(out_weight, SEQ_DP, axis=0, tiled=True)  36.1 us
    ppermute x4, waiting for transfers between devices, hop(): return lax.ppermute(sent, axis, CYCLES[which])  32 us
    pallas_call x4, Pallas kernels, parted(): call(run, (count,), [kinds[a.ndim] for a in args] + [ANY] * len(olds), [p...  25.4 us
    reduce_scatter x1, waiting for transfers between devices, gradient_rows(): total = lax.psum_scatter(total, 'seq_0', scatter_dimension=0, tiled=True)  22.6 us
    all_to_all x1, blocking collectives, scanned(): pieces = lax.all_to_all(pieces, SEQ, 0, 0, tiled=True)  19.4 us
    pallas_call x8, Pallas kernels, placed_call(): pl.pallas_call(body, grid_spec=pltpu.PrefetchScalarGridSpec(num_scalar_pr...  17.7 us
    pallas_call x1, Pallas kernels, norm_back(): call(norm_back_body, (CHUNKS,), [whole, pl.BlockSpec(memory_space=pltpu.H...  14.1 us
    all_to_all x2, starting transfers between devices, scanned(): sums = lax.all_to_all(sums, SEQ, 0, 0, tiled=True)  9.51 us
  transfers between devices with their start and end apart: 14, of which 10 were waited for; matrix products, arithmetic and copies ran while one was open for 4% of the time, Pallas kernels for 15%

profile of v7, /device:TPU:2, one launch (start us, length us, event | category | flops | bytes accessed | tf_op | source)
XLA Modules:
  0.0 256.2 jit_solution(11437651332565482044)
XLA Ops:
  8.0 4.7 %shard_map.101 = (bf16[512,2048]{1,0:T(8,128)(2,1)}, bf16[16,128,128]{2,1,0:T(8,128)(2,1)}) custom-call(bf16[512,2048]{1,0:T(8,128)(2,1)} %bitcast.30, bf16[512,2048]{1,0:T(8,128)(2,1)} %bitcast.24), custom_call_target="tpu_custom_call" | custom-call | flops 536870912 | bytes 7340032 | tf_op jit(solution)/shard_map/pallas_call | solution.py:101
  12.7 19.4 %all_to_all.20.a = bf16[32,64,128]{2,1,0:T(8,128)(2,1)S(1)} all-to-all(bf16[32,64,128]{2,1,0:T(8,128)(2,1)} %bitcast.45), channel_id=1, replica_groups=mesh['seq_0'=4,'seq_1'=4,'seq_2'=2,'dp'=4] {'seq_0','seq_1','seq_2'}, dimensions={0} | all-to-all | bytes 1048576 | tf_op jit(solution)/shard_map/all_to_all | solution.py:166
  32.1 0.9 shard_map.103
  33.0 4.1 %all-to-all-start.1 = ((bf16[32,64,128]{2,1,0:T(8,128)(2,1)}), bf16[32,64,128]{2,1,0:T(8,128)(2,1)S(1)}, u32[]{:S(2)}, u32[]{:S(2)}) async-start(bf16[32,64,128]{2,1,0:T(8,128)(2,1)} %shard_map.103), calls=%async_computation.1 | async-start | bytes 1048576 | tf_op jit(solution)/shard_map/all_to_all | solution.py:168
  37.3 9.2 %shard_map.102 = (bf16[512,2048]{1,0:T(8,128)(2,1)}, f32[512,2048]{1,0:T(8,128)}, bf16[16,3,256,256]{3,2,1,0:T(8,128)(2,1)}) custom-call(bf16[512,2048]{1,0:T(8,128)(2,1)} %bitcast.33, bf16[512,2048]{1,0:T(8,128)(2,1)} %get-tuple-element.42.feat_key.refs_2_.refs_1_, bf16[512,2048]{1,0:T(8,128)(2,1)} %bitcast.25), custom_call_target="tpu_custom_call" | custom-call | flops 4294967296 | bytes 18874368 | tf_op jit(solution)/shard_map/pallas_call | solution.py:127
  46.6 1.7 all-to-all-done.1
  48.3 0.8 copy-done.3
  49.1 7.6 %shard_map.104 = (bf16[512,2048]{1,0:T(8,128)(2,1)}, bf16[2,1024,512]{2,1,0:T(8,128)(2,1)}, f32[512,2048]{1,0:T(8,128)}, f32[512,128]{1,0:T(8,128)}) custom-call(f32[512,2048]{1,0:T(8,128)} %get-tuple-element.43.inside, bf16[512,2048]{1,0:T(8,128)(2,1)} %get-tuple-element.44.feat_query.refs_1_, bf16[16,128,128]{2,1,0:T(8,128)(2,1)} %bitcast.36, ...), custom_call_target="tpu_custom_call" | custom-call | flops 536870912 | bytes 15728640 | tf_op jit(solution)/shard_map/pallas_call | solution.py:205
  56.7 1.6 copy-done.2
  58.3 4.4 %shard_map.112 = (bf16[1024,1024]{1,0:T(8,128)(2,1)S(1)}, bf16[1024,1024]{1,0:T(8,128)(2,1)S(1)}) custom-call(s32[5]{0:T(128)S(1)} %stack.31.place.refs_0_, bf16[2,1024,512]{2,1,0:T(8,128)(2,1)S(1)} %copy-done.2, bf16[512,2048]{1,0:T(8,128)(2,1)S(1)} %bitcast.22), custom_call_target="tpu_custom_call" | custom-call | flops 2147483648 | bytes 7340032 | tf_op jit(solution)/shard_map/pallas_call | solution.py:430
  62.7 0.9 collective-permute-start
  63.5 0.1 collective-permute-start.3
  63.6 4.4 %shard_map.111 = (bf16[1024,1024]{1,0:T(8,128)(2,1)S(1)}, bf16[1024,1024]{1,0:T(8,128)(2,1)S(1)}) custom-call(s32[5]{0:T(128)S(1)} %stack.31.place.refs_0_, bf16[2,1024,512]{2,1,0:T(8,128)(2,1)S(1)} %copy-done.2, bf16[512,2048]{1,0:T(8,128)(2,1)S(1)} %bitcast.23), custom_call_target="tpu_custom_call" | custom-call | flops 2147483648 | bytes 7340032 | tf_op jit(solution)/shard_map/pallas_call | solution.py:430
  68.0 2.0 shard_map.113
  70.0 0.6 collective-permute-start.1
  70.7 2.0 shard_map.115
  72.7 2.2 collective-permute-start.4
  74.9 20.7 %collective-permute-done.1.refs_2_ = bf16[512,1024]{1,0:T(8,128)(2,1)S(1)} collective-permute-done((bf16[512,1024]{1,0:T(8,128)(2,1)S(1)}, bf16[512,1024]{1,0:T(8,128)(2,1)S(1)}, u32[]{:S(2)}, u32[]{:S(2)}) %collective-permute-start.1) | collective-permute-done | bytes 1048608 | tf_op jit(solution)/shard_map/ppermute | solution.py:380
  95.6 1.3 shard_map.114
  96.9 1.6 collective-permute-start.2
  98.5 1.3 shard_map.116
  99.9 2.2 collective-permute-start.5
  102.1 8.3 %collective-permute-done.2.got0 = bf16[256,1024]{1,0:T(8,128)(2,1)S(1)} collective-permute-done((bf16[256,1024]{1,0:T(8,128)(2,1)S(1)}, bf16[256,1024]{1,0:T(8,128)(2,1)S(1)}, u32[]{:S(2)}, u32[]{:S(2)}) %collective-permute-start.2) | collective-permute-done | bytes 524320 | tf_op jit(solution)/shard_map/ppermute | solution.py:380
  110.4 3.0 %collective-permute-done.5.got1 = bf16[256,1024]{1,0:T(8,128)(2,1)S(1)} collective-permute-done((bf16[256,1024]{1,0:T(8,128)(2,1)S(1)}, bf16[256,1024]{1,0:T(8,128)(2,1)S(1)}, u32[]{:S(2)}, u32[]{:S(2)}) %collective-permute-start.5) | collective-permute-done | bytes 524320 | tf_op jit(solution)/shard_map/ppermute | solution.py:380
  113.4 1.7 shard_map.117
  115.3 0.5 all-gather.2.cloned.1.call-update
  115.8 22.6 %reduce-scatter.2.cloned.1.call-done.rows = bf16[64,2048]{1,0:T(8,128)(2,1)} async-done(((bf16[256,2048]{1,0:T(8,128)(2,1)}), bf16[64,2048]{1,0:T(8,128)(2,1)}) %reduce-scatter.2.cloned.1.call-update) | async-done | bytes 262160 | tf_op jit(solution)/shard_map/reduce_scatter | solution.py:517
  138.4 0.9 copy-done
  139.3 0.6 shard_map.118
  139.9 3.1 %collective-permute-start.8 = (bf16[16,2048]{1,0:T(8,128)(2,1)S(1)}, bf16[16,2048]{1,0:T(8,128)(2,1)S(1)}, u32[]{:S(2)}, u32[]{:S(2)}) collective-permute-start(bf16[16,2048]{1,0:T(8,128)(2,1)S(1)} %get-tuple-element.78), channel_id=1, source_target_pairs={{0,24},{8,0},{16,8},{24,16},{1,25},{9,1},{17,9},{25,17},{2,26},{10... | collective-permute-start | bytes 196616 | tf_op jit(solution)/shard_map/ppermute | solution.py:532
  143.0 0.6 collective-permute-start.7
  143.6 1.0 collective-permute-start.6
  144.6 0.3 collective-permute-done.8
  144.9 3.9 %collective-permute-done.7 = bf16[16,2048]{1,0:T(8,128)(2,1)S(1)} collective-permute-done((bf16[16,2048]{1,0:T(8,128)(2,1)S(1)}, bf16[16,2048]{1,0:T(8,128)(2,1)S(1)}, u32[]{:S(2)}, u32[]{:S(2)}) %collective-permute-start.7) | collective-permute-done | bytes 65568 | tf_op jit(solution)/shard_map/ppermute | solution.py:532
  148.8 0.7 collective-permute-done.6
  149.4 0.7 convert_add_fusion
  150.1 36.1 %all-gather.2.cloned.1.call-done.weight = bf16[2048,2048]{1,0:T(8,128)(2,1)} async-done(((bf16[16,2048]{1,0:T(8,128)(2,1)}), bf16[2048,2048]{1,0:T(8,128)(2,1)}) %all-gather.2.cloned.1.call-update) | async-done | bytes 8388624 | tf_op jit(solution)/shard_map/all_gather | solution.py:540
  186.3 14.1 %shard_map.105 = (bf16[512,2048]{1,0:T(8,128)(2,1)}, bf16[16,128,128]{2,1,0:T(8,128)(2,1)}) custom-call(bf16[512,2048]{1,0:T(8,128)(2,1)} %bitcast.21, bf16[2048,2048]{1,0:T(8,128)(2,1)} %all-gather.2.cloned.1.call-done.weight, f32[512,2048]{1,0:T(8,128)} %get-tuple-element.47.normed, f32[512,128]{1,0:T(8,128)} %get-tuple-element.48.inverse, ...), custom_call_target="tpu_custom_call" | custom-call | flops 5368709120 | bytes 18874368 | tf_op jit(solution)/shard_map/pallas_call | solution.py:273
  200.4 5.0 %all-to-all-start.2 = ((bf16[32,64,128]{2,1,0:T(8,128)(2,1)}), bf16[32,64,128]{2,1,0:T(8,128)(2,1)S(1)}, u32[]{:S(2)}, u32[]{:S(2)}) async-start(bf16[32,64,128]{2,1,0:T(8,128)(2,1)} %bitcast.44), calls=%async_computation.2 | async-start | bytes 1048576 | tf_op jit(solution)/shard_map/all_to_all | solution.py:166
  205.4 9.0 %fusion = bf16[1,512,2048]{2,1,0:T(8,128)(2,1)} fusion(bf16[512,2048]{1,0:T(8,128)(2,1)S(1)} %copy-done.5, bf16[2048,2048]{1,0:T(8,128)(2,1)} %all-gather.2.cloned.1.call-done.weight), kind=kOutput, calls=%fused_computation.1 | convolution fusion | flops 4296015872 | bytes 12582912 | tf_op jit(solution)/shard_map/dot_general | solution.py:32
  214.4 1.8 all-to-all-done.2.a
  216.2 0.9 shard_map.108
  217.1 5.4 %all-to-all-start.3 = ((bf16[32,64,128]{2,1,0:T(8,128)(2,1)}), bf16[32,64,128]{2,1,0:T(8,128)(2,1)S(1)}, u32[]{:S(2)}, u32[]{:S(2)}) async-start(bf16[32,64,128]{2,1,0:T(8,128)(2,1)} %shard_map.108), calls=%async_computation.3 | async-start | bytes 1048576 | tf_op jit(solution)/shard_map/all_to_all | solution.py:168
  222.5 11.2 %shard_map.106 = (bf16[512,2048]{1,0:T(8,128)(2,1)}, bf16[512,2048]{1,0:T(8,128)(2,1)}, bf16[512,2048]{1,0:T(8,128)(2,1)}) custom-call(bf16[512,2048]{1,0:T(8,128)(2,1)} %bitcast.34, bf16[512,2048]{1,0:T(8,128)(2,1)} %get-tuple-element.44.feat_query.refs_1_, bf16[512,2048]{1,0:T(8,128)(2,1)} %get-tuple-element.42.feat_key.refs_2_.refs_1_, ...), custom_call_target="tpu_custom_call" | custom-call | flops 3221225472 | bytes 5242880 | tf_op jit(solution)/shard_map/pallas_call | solution.py:336
  233.8 5.9 %shard_map.107 = (bf16[512,2048]{1,0:T(8,128)(2,1)}, bf16[512,2048]{1,0:T(8,128)(2,1)}, bf16[512,2048]{1,0:T(8,128)(2,1)}) custom-call(bf16[512,2048]{1,0:T(8,128)(2,1)} %bitcast.35, bf16[512,2048]{1,0:T(8,128)(2,1)} %get-tuple-element.44.feat_query.refs_1_, ...), custom_call_target="tpu_custom_call", output_to_operand_aliasing={{0}: (7, {}), {1}: (8, {}), {2}: (9, {})} | custom-call | flops 3221225472 | bytes 5242880 | tf_op jit(solution)/shard_map/pallas_call | solution.py:336
  239.7 0.8 copy-done.4
  240.4 4.1 %shard_map.109 = (bf16[512,2048]{1,0:T(8,128)(2,1)}, bf16[512,2048]{1,0:T(8,128)(2,1)}) custom-call(bf16[512,2048]{1,0:T(8,128)(2,1)} %bitcast.31, bf16[512,2048]{1,0:T(8,128)(2,1)} %get-tuple-element.42.feat_key.refs_2_.refs_1_, bf16[512,2048]{1,0:T(8,128)(2,1)} %bitcast.28, bf16[512,2048]{1,0:T(8,128)(2,1)} %get-tuple-element.55.refs_3_, ...), custom_call_target="tpu_custom_call" | custom-call | flops 536870912 | bytes 9437184 | tf_op jit(solution)/shard_map/pallas_call | solution.py:336
  244.6 4.2 %shard_map.110 = (bf16[512,2048]{1,0:T(8,128)(2,1)}, bf16[512,2048]{1,0:T(8,128)(2,1)}) custom-call(bf16[512,2048]{1,0:T(8,128)(2,1)} %bitcast.32, bf16[512,2048]{1,0:T(8,128)(2,1)} %get-tuple-element.42.feat_key.refs_2_.refs_1_, bf16[512,2048]{1,0:T(8,128)(2,1)} %bitcast.29, ...), custom_call_target="tpu_custom_call", output_to_operand_aliasing={{0}: (6, {}), {1}: (7, {})} | custom-call | flops 536870912 | bytes 9437184 | tf_op jit(solution)/shard_map/pallas_call | solution.py:336
  (16 shorter events, 0.2 us)
Async XLA Ops:
  33.0 15.2 %all-to-all-start.1 = ((bf16[32,64,128]{2,1,0:T(8,128)(2,1)}), bf16[32,64,128]{2,1,0:T(8,128)(2,1)S(1)}, u32[]{:S(2)}, u32[]{:S(2)}) async-start(bf16[32,64,128]{2,1,0:T(8,128)(2,1)} %shard_map.103), calls=%async_computation.1 | async-start | bytes 1048576 | tf_op jit(solution)/shard_map/all_to_all | solution.py:168
  37.2 101.2 %reduce-scatter.2.cloned.1.call-start = ((), (), s32[]{:S(2)}) async-start(), calls=%async_computation.6 | async-start | bytes 1310720 | tf_op jit(solution)/shard_map/reduce_scatter | solution.py:517
  48.3 0.8 copy-start.3
  49.1 7.6 %copy-start.1 = (bf16[1,512,2048]{2,1,0:T(8,128)(2,1)S(1)}, bf16[1,512,2048]{2,1,0:T(8,128)(2,1)}, u32[]{:S(2)}) copy-start(bf16[1,512,2048]{2,1,0:T(8,128)(2,1)} %param.9) | copy-start | bytes 6291460
  56.7 1.6 copy-start.2
  62.7 5.3 %collective-permute-start = (bf16[1024,1024]{1,0:T(8,128)(2,1)S(1)}, bf16[1024,1024]{1,0:T(8,128)(2,1)S(1)}, u32[]{:S(2)}, u32[]{:S(2)}) collective-permute-start(bf16[1024,1024]{1,0:T(8,128)(2,1)S(1)} %get-tuple-element.64), channel_id=1, source_target_pairs={{0,4},{4,0},{1,5},{5,1},{2,6},{6,2},{3,7},{7,3},{8,12},{12,8},{9,1... | collective-permute-start | bytes 6291464 | tf_op jit(solution)/shard_map/ppermute | solution.py:476
  63.5 7.1 %collective-permute-start.3 = (bf16[1024,1024]{1,0:T(8,128)(2,1)S(1)}, bf16[1024,1024]{1,0:T(8,128)(2,1)S(1)}, u32[]{:S(2)}, u32[]{:S(2)}) collective-permute-start(bf16[1024,1024]{1,0:T(8,128)(2,1)S(1)} %get-tuple-element.70), channel_id=1, source_target_pairs={{0,4},{4,0},{1,5},{5,1},{2,6},{6,2},{3,7},{7,3},{8,12},{12,8},{9,1... | collective-permute-start | bytes 6291464 | tf_op jit(solution)/shard_map/ppermute | solution.py:476
  70.0 25.6 %collective-permute-start.1 = (bf16[512,1024]{1,0:T(8,128)(2,1)S(1)}, bf16[512,1024]{1,0:T(8,128)(2,1)S(1)}, u32[]{:S(2)}, u32[]{:S(2)}) collective-permute-start(bf16[512,1024]{1,0:T(8,128)(2,1)S(1)} %get-tuple-element.66), channel_id=1, source_target_pairs={{0,1},{1,0},{2,3},{3,2},{4,5},{5,4},{6,7},{7,6},{8,9},{9,8},{10,11... | collective-permute-start | bytes 3145736 | tf_op jit(solution)/shard_map/ppermute | solution.py:380
  72.7 25.8 %collective-permute-start.4 = (bf16[512,1024]{1,0:T(8,128)(2,1)S(1)}, bf16[512,1024]{1,0:T(8,128)(2,1)S(1)}, u32[]{:S(2)}, u32[]{:S(2)}) collective-permute-start(bf16[512,1024]{1,0:T(8,128)(2,1)S(1)} %get-tuple-element.72), channel_id=1, source_target_pairs={{0,3},{3,0},{1,2},{2,1},{4,7},{7,4},{5,6},{6,5},{8,11},{11,8},{9,1... | collective-permute-start | bytes 3145736 | tf_op jit(solution)/shard_map/ppermute | solution.py:380
  96.9 13.5 %collective-permute-start.2 = (bf16[256,1024]{1,0:T(8,128)(2,1)S(1)}, bf16[256,1024]{1,0:T(8,128)(2,1)S(1)}, u32[]{:S(2)}, u32[]{:S(2)}) collective-permute-start(bf16[256,1024]{1,0:T(8,128)(2,1)S(1)} %get-tuple-element.68), channel_id=1, source_target_pairs={{0,3},{3,0},{1,2},{2,1},{4,7},{7,4},{5,6},{6,5},{8,11},{11,8},{9,1... | collective-permute-start | bytes 1572872 | tf_op jit(solution)/shard_map/ppermute | solution.py:380
  99.9 13.6 %collective-permute-start.5 = (bf16[256,1024]{1,0:T(8,128)(2,1)S(1)}, bf16[256,1024]{1,0:T(8,128)(2,1)S(1)}, u32[]{:S(2)}, u32[]{:S(2)}) collective-permute-start(bf16[256,1024]{1,0:T(8,128)(2,1)S(1)} %get-tuple-element.74), channel_id=1, source_target_pairs={{0,1},{1,0},{2,3},{3,2},{4,5},{5,4},{6,7},{7,6},{8,9},{9,8},{10,11... | collective-permute-start | bytes 1572872 | tf_op jit(solution)/shard_map/ppermute | solution.py:380
  115.2 71.1 %all-gather.2.cloned.1.call-start = ((), (), s32[]{:S(2)}) async-start(), calls=%async_computation.5 | async-start | bytes 8454144 | tf_op jit(solution)/shard_map/all_gather | solution.py:540
  138.4 1.0 copy-start
  139.9 5.0 %collective-permute-start.8 = (bf16[16,2048]{1,0:T(8,128)(2,1)S(1)}, bf16[16,2048]{1,0:T(8,128)(2,1)S(1)}, u32[]{:S(2)}, u32[]{:S(2)}) collective-permute-start(bf16[16,2048]{1,0:T(8,128)(2,1)S(1)} %get-tuple-element.78), channel_id=1, source_target_pairs={{0,24},{8,0},{16,8},{24,16},{1,25},{9,1},{17,9},{25,17},{2,26},{10... | collective-permute-start | bytes 196616 | tf_op jit(solution)/shard_map/ppermute | solution.py:532
  143.0 5.8 %collective-permute-start.7 = (bf16[16,2048]{1,0:T(8,128)(2,1)S(1)}, bf16[16,2048]{1,0:T(8,128)(2,1)S(1)}, u32[]{:S(2)}, u32[]{:S(2)}) collective-permute-start(bf16[16,2048]{1,0:T(8,128)(2,1)S(1)} %get-tuple-element.77), channel_id=1, source_target_pairs={{0,16},{8,24},{16,0},{24,8},{1,17},{9,25},{17,1},{25,9},{2,18},{10... | collective-permute-start | bytes 196616 | tf_op jit(solution)/shard_map/ppermute | solution.py:532
  143.6 5.9 %collective-permute-start.6 = (bf16[16,2048]{1,0:T(8,128)(2,1)S(1)}, bf16[16,2048]{1,0:T(8,128)(2,1)S(1)}, u32[]{:S(2)}, u32[]{:S(2)}) collective-permute-start(bf16[16,2048]{1,0:T(8,128)(2,1)S(1)} %get-tuple-element.76), channel_id=1, source_target_pairs={{0,8},{8,16},{16,24},{24,0},{1,9},{9,17},{17,25},{25,1},{2,10},{10... | collective-permute-start | bytes 196616 | tf_op jit(solution)/shard_map/ppermute | solution.py:532
  186.3 19.1 %copy-start.5 = (bf16[512,2048]{1,0:T(8,128)(2,1)S(1)}, bf16[512,2048]{1,0:T(8,128)(2,1)}, u32[]{:S(2)}) copy-start(bf16[512,2048]{1,0:T(8,128)(2,1)} %get-tuple-element.46) | copy-start | bytes 6291460
  200.4 15.9 %all-to-all-start.2 = ((bf16[32,64,128]{2,1,0:T(8,128)(2,1)}), bf16[32,64,128]{2,1,0:T(8,128)(2,1)S(1)}, u32[]{:S(2)}, u32[]{:S(2)}) async-start(bf16[32,64,128]{2,1,0:T(8,128)(2,1)} %bitcast.44), calls=%async_computation.2 | async-start | bytes 1048576 | tf_op jit(solution)/shard_map/all_to_all | solution.py:166
  217.1 22.5 %all-to-all-start.3 = ((bf16[32,64,128]{2,1,0:T(8,128)(2,1)}), bf16[32,64,128]{2,1,0:T(8,128)(2,1)S(1)}, u32[]{:S(2)}, u32[]{:S(2)}) async-start(bf16[32,64,128]{2,1,0:T(8,128)(2,1)} %shard_map.108), calls=%async_computation.3 | async-start | bytes 1048576 | tf_op jit(solution)/shard_map/all_to_all | solution.py:168
  239.7 0.8 copy-start.4
Sparse Core Ops, SparseCore 0:
  115.3 22.9 reduce-scatter.1
Sparse Core Ops, SparseCore 1:
  118.8 67.4 all-gather.1
